TPU v7x, 128 devices: a whole 4x4x4 slice. The times are simulated.
128 devices in a mesh: rep: 1, dp: 128 (over x, y, z, core).
Axes of the slice: x: 4, y: 4, z: 4, core: 2. Of those that a mesh axis runs over, the one named last changes fastest.
Arguments:
- x: bfloat16 [128, 1024, 1536], P(('rep', 'dp'))
- dy: bfloat16 [128, 1024, 1536], P(('rep', 'dp'))
- w_gate: bfloat16 [2, 1536, 3584], replicated
- w_up: bfloat16 [2, 1536, 3584], replicated
- w_down: bfloat16 [2, 3584, 1536], replicated
- m_w_gate: float32 [2, 1536, 3584], P(None, 'dp')
- m_w_up: float32 [2, 1536, 3584], P(None, 'dp')
- m_w_down: float32 [2, 3584, 1536], P(None, 'dp')
- v_w_gate: float32 [2, 1536, 3584], P(None, 'dp')
- v_w_up: float32 [2, 1536, 3584], P(None, 'dp')
- v_w_down: float32 [2, 3584, 1536], P(None, 'dp')
Outputs:
- output 1: bfloat16 [2, 1536, 3584], P('rep')
- output 2: bfloat16 [2, 1536, 3584], P('rep')
- output 3: bfloat16 [2, 3584, 1536], P('rep')
- output 4: float32 [2, 1536, 3584], P('rep', 'dp')
- output 5: float32 [2, 1536, 3584], P('rep', 'dp')
- output 6: float32 [2, 3584, 1536], P('rep', 'dp')
- output 7: float32 [2, 1536, 3584], P('rep', 'dp')
- output 8: float32 [2, 1536, 3584], P('rep', 'dp')
- output 9: float32 [2, 3584, 1536], P('rep', 'dp')
All inputs are finite; a program needn't handle non-finite values.
Results may differ from a plain program's by a relative error of at most 0.022.
Values are sent between devices in bfloat16 or wider.
A program may use at most 1.5 GiB of HBM per device.

v0:
```python
import jax
import jax.numpy as jnp
from jax import lax

NAMES = ("w_gate", "w_up", "w_down")


def matmul(a, w):
    return jnp.dot(a, w, preferred_element_type=jnp.float32).astype(jnp.bfloat16)


def normed(h):
    wide = h.astype(jnp.float32)
    scale = lax.rsqrt(jnp.mean(wide**2, -1, keepdims=True) + 1e-6)
    return (wide * scale).astype(jnp.bfloat16)


def layer(h, w):
    a = normed(h)
    gate = jnp.dot(a, w["w_gate"], preferred_element_type=jnp.float32)
    up = jnp.dot(a, w["w_up"], preferred_element_type=jnp.float32)
    return h + matmul((jax.nn.silu(gate) * up).astype(jnp.bfloat16), w["w_down"])


def adamw(w, m, v, g):
    m = 0.9 * m + 0.1 * g
    v = 0.95 * v + 0.05 * g * g
    step = m * lax.rsqrt(v + 1e-8) + 0.1 * w
    return (w - 0.02 * step).astype(jnp.bfloat16), m, v


def stack(weights, h):
    for number in range(weights["w_gate"].shape[0]):
        h = layer(h, {name: w[number] for name, w in weights.items()})
    return h


def solution(mesh):
    groups = mesh.shape["rep"]

    def step(x, dy, *arrays):
        weights, m, v = (arrays[i : i + 3] for i in (0, 3, 6))
        x, dy = (t.reshape(groups, -1, *t.shape[1:]) for t in (x, dy))

        def of_a_group(x, dy):
            _, back = jax.vjp(lambda w: stack(w, x), dict(zip(NAMES, weights, strict=True)))
            by_weights = back(dy)[0]
            gradients = [by_weights[name].astype(jnp.float32) for name in NAMES]
            new = [adamw(w.astype(jnp.float32), m, v, g) for w, m, v, g in zip(weights, m, v, gradients, strict=True)]
            return tuple(one[which] for which in range(3) for one in new)

        return tuple(t.reshape(-1, *t.shape[2:]) for t in jax.vmap(of_a_group)(x, dy))

    return step
```

profile of v0, /device:TPU:1, one launch (start us, length us, event | category | flops | bytes accessed | tf_op | source)
XLA Modules:
  0.0 2921.8 jit_solution(16329933671208655407)
XLA Ops:
  9.8 15.5 fusion.42
  25.4 21.5 fusion.40
  46.8 7.6 fusion.64
  54.5 16.9 fusion.77
  71.5 15.5 fusion.30
  87.0 21.5 fusion.34
  108.5 17.2 fusion.58
  125.6 10.1 fusion.12
  138.6 15.1 fusion.85
  153.8 22.3 fusion.79
  180.0 16.4 fusion.61
  196.4 16.0 fusion.168
  212.4 26.7 fusion.16
  239.1 413.6 %fusion.160 = (f32[3584,16]{0,1:T(8,128)}, f32[1536,32]{0,1:T(8,128)S(1)}) fusion(f32[3584,1536]{0,1:T(8,128)} %fusion.16, f32[1536,3584]{0,1:T(8,128)} %fusion.168), kind=kCustom, calls=%all-reduce-scatter.6 | all-reduce-scatter fusion | flops 13631490 | bytes 44466176
  654.7 19.5 fusion.156
  674.2 23.2 fusion.66
  697.4 415.0 %fusion.161 = (f32[3584,16]{0,1:T(8,128)S(1)}, f32[32,1536]{1,0:T(8,128)}) fusion(f32[3584,1536]{0,1:T(8,128)} %fusion.156, f32[3584,1536]{1,0:T(8,128)} %fusion.66), kind=kCustom, calls=%all-reduce-scatter.7 | all-reduce-scatter fusion | flops 13631490 | bytes 44466176
  1126.1 8.8 collective-permute-start.150
  1138.8 20.3 collective-permute-start.148
  1200.5 27.6 concatenate.5
  1243.6 27.9 concatenate.4
  1289.9 8.2 collective-permute-start.58
  1339.6 7.7 collective-permute-start.42
  1388.5 6.9 collective-permute-start.26
  1404.2 7.1 collective-permute-start.21
  1416.4 5.4 collective-permute-start.19
  1421.8 6.2 collective-permute-start.18
  1433.3 6.5 collective-permute-start.16
  1454.3 6.6 collective-permute-start.10
  1462.8 8.6 collective-permute-start.8
  1496.6 81.1 %concatenate.1 = bf16[3584,524]{0,1:T(8,128)(2,1)} concatenate(bf16[3584,12]{0,1:T(8,128)(2,1)} %copy-done.14, bf16[3584,16]{0,1:T(8,128)(2,1)} %collective-permute-done.62, bf16[3584,16]{0,1:T(8,128)(2,1)} %collective-permute-done.61, bf16[3584,16]{0,1:T(8,128)(2,1)} %collective-permute-done.60, bf16[3584,16]{0,1:T(8,128)(2,1)} %collective-permute-done.59, ...), dimensions={1} | concatenate | bytes 7626752
  1577.8 79.8 %concatenate = bf16[3584,524]{0,1:T(8,128)(2,1)} concatenate(bf16[3584,12]{0,1:T(8,128)(2,1)S(1)} %collective-permute-done.31, bf16[3584,16]{0,1:T(8,128)(2,1)} %collective-permute-done.30, bf16[3584,16]{0,1:T(8,128)(2,1)} %collective-permute-done.29, bf16[3584,16]{0,1:T(8,128)(2,1)} %collective-permute-done.28, bf16[3584,16]{0,1:T(8,128)(2,1)} %collective-permute-done.27, ...), dimensions={1} | concatenate | bytes 7626752
  1662.9 21.2 fusion.8
  1684.1 373.3 %fusion.3 = f32[3584,16]{0,1:T(8,128)S(1)} fusion(f32[3584,1536]{0,1:T(8,128)} %fusion.8), kind=kCustom, calls=%all-reduce-scatter.3 | all-reduce-scatter fusion | flops 7340033 | bytes 22249472
  2064.0 21.5 fusion.49
  2085.4 362.4 %fusion.2 = f32[3584,16]{0,1:T(8,128)S(1)} fusion(f32[3584,1536]{0,1:T(8,128)} %fusion.49), kind=kCustom, calls=%all-reduce-scatter.2 | all-reduce-scatter fusion | flops 7340033 | bytes 22249472
  2457.3 10.7 collective-permute-start.118
  2501.1 12.4 collective-permute-start.106
  2533.1 7.2 collective-permute-start.97
  2542.5 7.1 collective-permute-start.94
  2549.5 6.1 collective-permute-start.93
  2602.8 21.6 collective-permute-start.74
  2647.4 80.0 %concatenate.3 = bf16[3584,524]{0,1:T(8,128)(2,1)} concatenate(bf16[3584,12]{0,1:T(8,128)(2,1)} %collective-permute-done.127, bf16[3584,16]{0,1:T(8,128)(2,1)S(1)} %collective-permute-done.126, bf16[3584,16]{0,1:T(8,128)(2,1)} %collective-permute-done.125, bf16[3584,16]{0,1:T(8,128)(2,1)S(1)} %collective-permute-done.124, bf16[3584,16]{0,1:T(8,128)(2,1)S(1)} %collective-permute-done.123, ...), dimensions={1} | concatenate | bytes 7626752
  2727.5 79.8 %concatenate.2 = bf16[3584,524]{0,1:T(8,128)(2,1)} concatenate(bf16[3584,12]{0,1:T(8,128)(2,1)S(1)} %collective-permute-done.95, bf16[3584,16]{0,1:T(8,128)(2,1)} %collective-permute-done.94, bf16[3584,16]{0,1:T(8,128)(2,1)} %collective-permute-done.93, bf16[3584,16]{0,1:T(8,128)(2,1)} %collective-permute-done.92, bf16[3584,16]{0,1:T(8,128)(2,1)} %collective-permute-done.91, ...), dimensions={1} | concatenate | bytes 7626752
  2817.6 21.9 copy.23
  2839.4 20.9 copy.21
  2860.3 33.9 %all-gather.12.cloned.1.call-done = bf16[1,2,1536,3584]{3,1,0,2:T(2,128)(2,1)} async-done(((bf16[1,2,12,3584]{3,1,0,2:T(2,128)(2,1)}), bf16[1,2,1536,3584]{3,1,0,2:T(2,128)(2,1)}) %all-gather.12.cloned.1.call-update) | async-done | bytes 22020112 | tf_op jit(solution)/reshape | solution.py:52
  2894.2 20.9 copy.22
  (416 shorter events, 403.7 us)
Async XLA Ops:
  7.2 2810.4 %all-gather.14.cloned.1.call-start = ((), (), s32[]{:S(2)}) async-start(), calls=%async_computation.2 | async-start | bytes 22192128 | tf_op jit(solution)/reshape | solution.py:52
  652.7 466.8 %collective-permute-start.159 = (bf16[1536,28]{0,1:T(8,128)(2,1)S(1)}, bf16[1536,28]{0,1:T(8,128)(2,1)}, u32[]{:S(2)}, u32[]{:S(2)}) collective-permute-start(bf16[1536,28]{0,1:T(8,128)(2,1)S(1)} %slice.29), channel_id=1, source_target_pairs={{0,16},{1,17},{2,18},{3,19},{4,20},{5,21},{6,22},{7,23},{8,24},{9,... | collective-permute-start | bytes 258056
  1123.5 35.6 %collective-permute-start.152 = (bf16[1536,32]{0,1:T(8,128)(2,1)S(1)}, bf16[1536,32]{0,1:T(8,128)(2,1)S(1)}, u32[]{:S(2)}, u32[]{:S(2)}) collective-permute-start(bf16[1536,32]{0,1:T(8,128)(2,1)S(1)} %convert.354), channel_id=1, source_target_pairs={{0,9},{1,10},{2,11},{3,12},{4,13},{5,14},{6,15},{7,16},{8,17},{9,1... | collective-permute-start | bytes 294920
  1124.8 35.6 %collective-permute-start.151 = (bf16[1536,32]{0,1:T(8,128)(2,1)S(1)}, bf16[1536,32]{0,1:T(8,128)(2,1)S(1)}, u32[]{:S(2)}, u32[]{:S(2)}) collective-permute-start(bf16[1536,32]{0,1:T(8,128)(2,1)S(1)} %convert.354), channel_id=1, source_target_pairs={{0,8},{1,9},{2,10},{3,11},{4,12},{5,13},{6,14},{7,15},{8,16},{9,17... | collective-permute-start | bytes 294920
  1126.1 39.5 %collective-permute-start.150 = (bf16[1536,32]{0,1:T(8,128)(2,1)S(1)}, bf16[1536,32]{0,1:T(8,128)(2,1)S(1)}, u32[]{:S(2)}, u32[]{:S(2)}) collective-permute-start(bf16[1536,32]{0,1:T(8,128)(2,1)S(1)} %convert.354), channel_id=1, source_target_pairs={{0,7},{1,8},{2,9},{3,10},{4,11},{5,12},{6,13},{7,14},{8,15},{9,16}... | collective-permute-start | bytes 294920
  1134.9 32.6 %collective-permute-start.149 = (bf16[1536,32]{0,1:T(8,128)(2,1)S(1)}, bf16[1536,32]{0,1:T(8,128)(2,1)S(1)}, u32[]{:S(2)}, u32[]{:S(2)}) collective-permute-start(bf16[1536,32]{0,1:T(8,128)(2,1)S(1)} %convert.354), channel_id=1, source_target_pairs={{0,6},{1,7},{2,8},{3,9},{4,10},{5,11},{6,12},{7,13},{8,14},{9,15},... | collective-permute-start | bytes 294920
  1138.8 33.9 %collective-permute-start.148 = (bf16[1536,32]{0,1:T(8,128)(2,1)S(1)}, bf16[1536,32]{0,1:T(8,128)(2,1)S(1)}, u32[]{:S(2)}, u32[]{:S(2)}) collective-permute-start(bf16[1536,32]{0,1:T(8,128)(2,1)S(1)} %convert.354), channel_id=1, source_target_pairs={{0,5},{1,6},{2,7},{3,8},{4,9},{5,10},{6,11},{7,12},{8,13},{9,14},{... | collective-permute-start | bytes 294920
  1188.4 39.7 %collective-permute-start.137 = (bf16[32,1536]{1,0:T(8,128)(2,1)}, bf16[32,1536]{1,0:T(8,128)(2,1)}, u32[]{:S(2)}, u32[]{:S(2)}) collective-permute-start(bf16[32,1536]{1,0:T(8,128)(2,1)} %convert.353), channel_id=1, source_target_pairs={{0,10},{1,11},{2,12},{3,13},{4,14},{5,15},{6,16},{7,17},{8,18},{9,... | collective-permute-start | bytes 294920
  1190.3 39.9 %collective-permute-start.136 = (bf16[32,1536]{1,0:T(8,128)(2,1)}, bf16[32,1536]{1,0:T(8,128)(2,1)}, u32[]{:S(2)}, u32[]{:S(2)}) collective-permute-start(bf16[32,1536]{1,0:T(8,128)(2,1)} %convert.353), channel_id=1, source_target_pairs={{0,9},{1,10},{2,11},{3,12},{4,13},{5,14},{6,15},{7,16},{8,17},{9,1... | collective-permute-start | bytes 294920
  1192.2 41.1 %collective-permute-start.135 = (bf16[32,1536]{1,0:T(8,128)(2,1)}, bf16[32,1536]{1,0:T(8,128)(2,1)}, u32[]{:S(2)}, u32[]{:S(2)}) collective-permute-start(bf16[32,1536]{1,0:T(8,128)(2,1)} %convert.353), channel_id=1, source_target_pairs={{0,8},{1,9},{2,10},{3,11},{4,12},{5,13},{6,14},{7,15},{8,16},{9,17... | collective-permute-start | bytes 294920
  1194.3 42.8 %collective-permute-start.134 = (bf16[32,1536]{1,0:T(8,128)(2,1)}, bf16[32,1536]{1,0:T(8,128)(2,1)}, u32[]{:S(2)}, u32[]{:S(2)}) collective-permute-start(bf16[32,1536]{1,0:T(8,128)(2,1)} %convert.353), channel_id=1, source_target_pairs={{0,7},{1,8},{2,9},{3,10},{4,11},{5,12},{6,13},{7,14},{8,15},{9,16}... | collective-permute-start | bytes 294920
  1196.2 43.1 %collective-permute-start.133 = (bf16[32,1536]{1,0:T(8,128)(2,1)}, bf16[32,1536]{1,0:T(8,128)(2,1)}, u32[]{:S(2)}, u32[]{:S(2)}) collective-permute-start(bf16[32,1536]{1,0:T(8,128)(2,1)} %convert.353), channel_id=1, source_target_pairs={{0,6},{1,7},{2,8},{3,9},{4,10},{5,11},{6,12},{7,13},{8,14},{9,15},... | collective-permute-start | bytes 294920
  1275.7 1563.8 %all-gather.10.cloned.1.call-start = ((), (), s32[]{:S(2)}) async-start(), calls=%async_computation | async-start | bytes 22192128 | tf_op jit(solution)/reshape | solution.py:52
  1399.3 22.5 collective-permute-start.23
  1401.2 26.8 collective-permute-start.22
  1404.2 29.1 collective-permute-start.21
  1411.3 28.5 collective-permute-start.20
  1416.4 26.3 collective-permute-start.19
  1421.8 25.2 collective-permute-start.18
  1451.2 22.8 collective-permute-start.11
  1454.3 23.1 collective-permute-start.10
  1462.8 22.9 collective-permute-start.8
  1482.0 95.7 %collective-permute-start.4 = (bf16[3584,16]{0,1:T(8,128)(2,1)}, bf16[3584,16]{0,1:T(8,128)(2,1)}, u32[]{:S(2)}, u32[]{:S(2)}) collective-permute-start(bf16[3584,16]{0,1:T(8,128)(2,1)} %convert.351), channel_id=1, source_target_pairs={{0,5},{1,6},{2,7},{3,8},{4,9},{5,10},{6,11},{7,12},{8,13},{9,14},{... | collective-permute-start | bytes 344072
  1485.7 92.1 %collective-permute-start.3 = (bf16[3584,16]{0,1:T(8,128)(2,1)}, bf16[3584,16]{0,1:T(8,128)(2,1)}, u32[]{:S(2)}, u32[]{:S(2)}) collective-permute-start(bf16[3584,16]{0,1:T(8,128)(2,1)} %convert.351), channel_id=1, source_target_pairs={{0,4},{1,5},{2,6},{3,7},{4,8},{5,9},{6,10},{7,11},{8,12},{9,13},{1... | collective-permute-start | bytes 344072
  1487.7 90.1 %collective-permute-start.2 = (bf16[3584,16]{0,1:T(8,128)(2,1)}, bf16[3584,16]{0,1:T(8,128)(2,1)}, u32[]{:S(2)}, u32[]{:S(2)}) collective-permute-start(bf16[3584,16]{0,1:T(8,128)(2,1)} %convert.351), channel_id=1, source_target_pairs={{0,3},{1,4},{2,5},{3,6},{4,7},{5,8},{6,9},{7,10},{8,11},{9,12},{10... | collective-permute-start | bytes 344072
  1492.2 85.5 %collective-permute-start.1 = (bf16[3584,16]{0,1:T(8,128)(2,1)}, bf16[3584,16]{0,1:T(8,128)(2,1)}, u32[]{:S(2)}, u32[]{:S(2)}) collective-permute-start(bf16[3584,16]{0,1:T(8,128)(2,1)} %convert.351), channel_id=1, source_target_pairs={{0,2},{1,3},{2,4},{3,5},{4,6},{5,7},{6,8},{7,9},{8,10},{9,11},{10,... | collective-permute-start | bytes 344072
  1494.2 83.6 %collective-permute-start = (bf16[3584,16]{0,1:T(8,128)(2,1)}, bf16[3584,16]{0,1:T(8,128)(2,1)}, u32[]{:S(2)}, u32[]{:S(2)}) collective-permute-start(bf16[3584,16]{0,1:T(8,128)(2,1)} %convert.351), channel_id=1, source_target_pairs={{0,1},{1,2},{2,3},{3,4},{4,5},{5,6},{6,7},{7,8},{8,9},{9,10},{10,1... | collective-permute-start | bytes 344072
  1662.9 1231.3 %all-gather.12.cloned.1.call-start = ((), (), s32[]{:S(2)}) async-start(), calls=%async_computation.1 | async-start | bytes 22192128 | tf_op jit(solution)/reshape | solution.py:52
  2058.1 395.2 %collective-permute-start.126 = (bf16[3584,16]{0,1:T(8,128)(2,1)}, bf16[3584,16]{0,1:T(8,128)(2,1)S(1)}, u32[]{:S(2)}, u32[]{:S(2)}) collective-permute-start(bf16[3584,16]{0,1:T(8,128)(2,1)} %convert.350), channel_id=1, source_target_pairs={{0,31},{1,32},{2,33},{3,34},{4,35},{5,36},{6,37},{7,38},{8,39},{9,... | collective-permute-start | bytes 344072
  2059.4 395.2 %collective-permute-start.125 = (bf16[3584,16]{0,1:T(8,128)(2,1)}, bf16[3584,16]{0,1:T(8,128)(2,1)}, u32[]{:S(2)}, u32[]{:S(2)}) collective-permute-start(bf16[3584,16]{0,1:T(8,128)(2,1)} %convert.350), channel_id=1, source_target_pairs={{0,30},{1,31},{2,32},{3,33},{4,34},{5,35},{6,36},{7,37},{8,38},{9,... | collective-permute-start | bytes 344072
  2062.1 388.7 %collective-permute-start.127 = (bf16[3584,12]{0,1:T(8,128)(2,1)}, bf16[3584,12]{0,1:T(8,128)(2,1)}, u32[]{:S(2)}, u32[]{:S(2)}) collective-permute-start(bf16[3584,12]{0,1:T(8,128)(2,1)} %slice.27), channel_id=1, source_target_pairs={{0,32},{1,33},{2,34},{3,35},{4,36},{5,37},{6,38},{7,39},{8,40},{9,... | collective-permute-start | bytes 258056
  2456.0 22.7 collective-permute-start.119
  2457.3 23.3 collective-permute-start.118
  2490.6 22.9 collective-permute-start.110
  2492.5 22.9 collective-permute-start.109
  2526.7 22.8 collective-permute-start.99
  2529.2 26.4 collective-permute-start.98
  2533.1 24.8 collective-permute-start.97
  2592.1 32.3 %collective-permute-start.78 = (bf16[3584,16]{0,1:T(8,128)(2,1)}, bf16[3584,16]{0,1:T(8,128)(2,1)}, u32[]{:S(2)}, u32[]{:S(2)}) collective-permute-start(bf16[3584,16]{0,1:T(8,128)(2,1)} %convert.349), channel_id=1, source_target_pairs={{0,15},{1,16},{2,17},{3,18},{4,19},{5,20},{6,21},{7,22},{8,23},{9,... | collective-permute-start | bytes 344072
  2594.0 32.2 %collective-permute-start.77 = (bf16[3584,16]{0,1:T(8,128)(2,1)}, bf16[3584,16]{0,1:T(8,128)(2,1)}, u32[]{:S(2)}, u32[]{:S(2)}) collective-permute-start(bf16[3584,16]{0,1:T(8,128)(2,1)} %convert.349), channel_id=1, source_target_pairs={{0,14},{1,15},{2,16},{3,17},{4,18},{5,19},{6,20},{7,21},{8,22},{9,... | collective-permute-start | bytes 344072
  2596.0 32.3 %collective-permute-start.76 = (bf16[3584,16]{0,1:T(8,128)(2,1)}, bf16[3584,16]{0,1:T(8,128)(2,1)}, u32[]{:S(2)}, u32[]{:S(2)}) collective-permute-start(bf16[3584,16]{0,1:T(8,128)(2,1)} %convert.349), channel_id=1, source_target_pairs={{0,13},{1,14},{2,15},{3,16},{4,17},{5,18},{6,19},{7,20},{8,21},{9,... | collective-permute-start | bytes 344072
  2600.8 29.5 %collective-permute-start.75 = (bf16[3584,16]{0,1:T(8,128)(2,1)}, bf16[3584,16]{0,1:T(8,128)(2,1)}, u32[]{:S(2)}, u32[]{:S(2)}) collective-permute-start(bf16[3584,16]{0,1:T(8,128)(2,1)} %convert.349), channel_id=1, source_target_pairs={{0,12},{1,13},{2,14},{3,15},{4,16},{5,17},{6,18},{7,19},{8,20},{9,... | collective-permute-start | bytes 344072
  2602.8 29.5 %collective-permute-start.74 = (bf16[3584,16]{0,1:T(8,128)(2,1)}, bf16[3584,16]{0,1:T(8,128)(2,1)}, u32[]{:S(2)}, u32[]{:S(2)}) collective-permute-start(bf16[3584,16]{0,1:T(8,128)(2,1)} %convert.349), channel_id=1, source_target_pairs={{0,11},{1,12},{2,13},{3,14},{4,15},{5,16},{6,17},{7,18},{8,19},{9,... | collective-permute-start | bytes 344072
  2634.4 93.1 %collective-permute-start.68 = (bf16[3584,16]{0,1:T(8,128)(2,1)}, bf16[3584,16]{0,1:T(8,128)(2,1)}, u32[]{:S(2)}, u32[]{:S(2)}) collective-permute-start(bf16[3584,16]{0,1:T(8,128)(2,1)} %convert.349), channel_id=1, source_target_pairs={{0,5},{1,6},{2,7},{3,8},{4,9},{5,10},{6,11},{7,12},{8,13},{9,14},{... | collective-permute-start | bytes 344072
  2637.1 90.4 %collective-permute-start.67 = (bf16[3584,16]{0,1:T(8,128)(2,1)}, bf16[3584,16]{0,1:T(8,128)(2,1)}, u32[]{:S(2)}, u32[]{:S(2)}) collective-permute-start(bf16[3584,16]{0,1:T(8,128)(2,1)} %convert.349), channel_id=1, source_target_pairs={{0,4},{1,5},{2,6},{3,7},{4,8},{5,9},{6,10},{7,11},{8,12},{9,13},{1... | collective-permute-start | bytes 344072
  2639.6 87.9 %collective-permute-start.66 = (bf16[3584,16]{0,1:T(8,128)(2,1)}, bf16[3584,16]{0,1:T(8,128)(2,1)}, u32[]{:S(2)}, u32[]{:S(2)}) collective-permute-start(bf16[3584,16]{0,1:T(8,128)(2,1)} %convert.349), channel_id=1, source_target_pairs={{0,3},{1,4},{2,5},{3,6},{4,7},{5,8},{6,9},{7,10},{8,11},{9,12},{10... | collective-permute-start | bytes 344072
  2643.3 84.1 %collective-permute-start.65 = (bf16[3584,16]{0,1:T(8,128)(2,1)}, bf16[3584,16]{0,1:T(8,128)(2,1)}, u32[]{:S(2)}, u32[]{:S(2)}) collective-permute-start(bf16[3584,16]{0,1:T(8,128)(2,1)} %convert.349), channel_id=1, source_target_pairs={{0,2},{1,3},{2,4},{3,5},{4,6},{5,7},{6,8},{7,9},{8,10},{9,11},{10,... | collective-permute-start | bytes 344072
  2645.5 82.0 %collective-permute-start.64 = (bf16[3584,16]{0,1:T(8,128)(2,1)}, bf16[3584,16]{0,1:T(8,128)(2,1)}, u32[]{:S(2)}, u32[]{:S(2)}) collective-permute-start(bf16[3584,16]{0,1:T(8,128)(2,1)} %convert.349), channel_id=1, source_target_pairs={{0,1},{1,2},{2,3},{3,4},{4,5},{5,6},{6,7},{7,8},{8,9},{9,10},{10,1... | collective-permute-start | bytes 344072
  (149 other events, 4089.3 us)
Sparse Core Ops, SparseCore 0:
  1275.8 128.8 all-gather.13
  1663.0 104.3 all-gather.9
  2811.7 82.4 all-gather.11
where the time goes:
time: 2950 us; the launch traced here: 2920 us
  blocking collectives  1560 us (53%)
  starting transfers between devices  515 us (17%)
  local copies, waits for them, and re-layouts  460 us (16%)
  matrix products  290 us (10%)
  waiting for transfers between devices  40.7 us (1%)
  other arithmetic  35.9 us (1%)
    unnamed x4, blocking collectives  1560 us
    unnamed x160, starting transfers between devices  515 us
    unnamed x89, local copies, waits for them, and re-layouts  452 us
    dot_general x5, matrix products, layer(): up = jnp.dot(a, w['w_up'], preferred_element_type=jnp.float32)  108 us
    dot_general x5, matrix products, layer(): gate = jnp.dot(a, w['w_gate'], preferred_element_type=jnp.float32)  92.3 us
    dot_general x5, matrix products, matmul(): jnp.dot(a, w, preferred_element_type=jnp.float32).astype(jnp.bfloat16)  89.7 us
  transfers between devices with their start and end apart: 163, of which 5 were waited for; matrix products, arithmetic and copies ran while one was open for 57% of the time, Pallas kernels for 0%

commit v1 on v0

v1 whole, which is shorter than its diff:
```python
import functools

import jax
import jax.numpy as jnp
import numpy as np
from jax import lax
from jax.experimental import pallas as pl
from jax.experimental.pallas import tpu as pltpu
from jax.sharding import Mesh
from jax.sharding import PartitionSpec as P

MESH = pl.DeviceIdType.MESH
RING = ("x", "y", "z")
ALL = ("x", "y", "z", "core")
N = 4
F32, BF16 = jnp.float32, jnp.bfloat16
LANES = 256


ORDERS = ((0, 1, 2), (1, 2, 0), (2, 0, 1))


def add_blocks(lead, out, *terms):
    def one(i, _):
        at = (i,) if len(lead) == 1 else (i // N, i % N)
        total = terms[0].at[at][...].astype(F32) if lead else None
        for t in terms[1:]:
            total = total + t.at[at][...].astype(F32)
        out.at[at][...] = total.astype(out.dtype)
        return 0

    if lead:
        lax.fori_loop(0, int(np.prod(lead)), one, 0)
    else:
        total = terms[0][...].astype(F32)
        for t in terms[1:]:
            total = total + t[...].astype(F32)
        out[...] = total.astype(out.dtype)


def scatter_kernel(*refs):
    grads, outs, scratch = refs[:3], refs[3:6], refs[6:]
    per = 8
    me = [lax.axis_index(a) for a in RING]
    right = [lax.rem(i + 1, N) for i in me]
    left = [lax.rem(i + N - 1, N) for i in me]
    across = [lax.rem(i + 2, N) for i in me]

    barrier = pltpu.get_barrier_semaphore()
    for axis in range(3):
        for to in (right[axis], left[axis]):
            pl.semaphore_signal(barrier, inc=1, device_id={RING[axis]: to}, device_id_type=MESH)

    colours = []
    for m in range(3):
        own, rx1, rx2, relay2, sum2, rx3, relay3, sum3 = scratch[m * per : (m + 1) * per]
        colours.append((own, (rx1, rx2, rx3), (None, relay2, relay3), (None, sum2, sum3)))
    local_sem, send_sem, recv_sem = scratch[3 * per :]

    def source(m, phase, index, half):
        own, _, _, sums = colours[m]
        a, b, _ = ORDERS[m]
        if phase == 0:
            width = grads[m].shape[-1] // 2
            at = [slice(None)] * 3
            at[a] = index
            return grads[m].at[(*at, slice(None), pl.ds(half * width, width))]
        if phase == 1:
            first = [axis for axis in range(3) if axis != a][0] == b
            return own.at[2 + half, index] if first else own.at[2 + half, :, index]
        return sums[1].at[half, index]

    loads = []
    for m in range(3):
        a = ORDERS[m][0]
        for k, (index, half) in enumerate(((right[a], 1), (left[a], 0), (me[a], 0), (me[a], 1))):
            copy = pltpu.make_async_copy(source(m, 0, index, half), colours[m][0].at[k], local_sem.at[m, k])
            copy.start()
            loads.append(copy)

    pl.semaphore_wait(barrier, 6)

    pending = []
    for phase in range(3):
        lead = ((N, N), (N,), ())[phase]

        def send(m, k, src, to):
            axis = ORDERS[m][phase]
            copy = pltpu.make_async_remote_copy(
                src_ref=src,
                dst_ref=colours[m][1][phase].at[k],
                send_sem=send_sem.at[m, phase, k],
                recv_sem=recv_sem.at[m, phase, k],
                device_id={RING[axis]: to},
                device_id_type=MESH,
            )
            copy.start()
            pending.append(copy)
            return copy

        flights = []
        for m in range(3):
            axis = ORDERS[m][phase]
            flights.append(
                [
                    send(m, 0, source(m, phase, across[axis], 1), right[axis]),
                    send(m, 1, source(m, phase, across[axis], 0), left[axis]),
                ]
            )
        for m in range(3):
            axis = ORDERS[m][phase]
            flights[m] += [
                send(m, 2, source(m, phase, right[axis], 0), right[axis]),
                send(m, 3, source(m, phase, left[axis], 1), left[axis]),
            ]
        if phase == 0:
            for copy in loads:
                copy.wait()
        for k in range(2):
            for m in range(3):
                axis = ORDERS[m][phase]
                own, rx, relays, _ = colours[m]
                flights[m][k].wait_recv()
                to = (right, left)[k][axis]
                if phase == 0:
                    passed = own.at[k]
                    add_blocks(lead, passed, passed, rx[phase].at[k])
                else:
                    passed = relays[phase].at[k]
                    add_blocks(lead, passed, source(m, phase, to, 1 - k), rx[phase].at[k])
                flights[m].append(send(m, 4 + k, passed, to))
        for half in range(2):
            for m in range(3):
                axis = ORDERS[m][phase]
                own, rx, _, sums = colours[m]
                direct, relayed = (2, 5) if half == 0 else (3, 4)
                flights[m][direct].wait_recv()
                flights[m][relayed].wait_recv()
                mine = own.at[2 + half] if phase == 0 else source(m, phase, me[axis], half)
                target = mine if phase == 0 else sums[phase].at[half]
                add_blocks(lead, target, mine, rx[phase].at[direct], rx[phase].at[relayed])
    for copy in pending:
        copy.wait_send()
    for m in range(3):
        width = outs[m].shape[-1] // 2
        for half in range(2):
            outs[m][:, half * width : (half + 1) * width] = colours[m][3][2][half].astype(outs[m].dtype)


def sum_over_chips(grads):
    scratch = []
    for g in grads:
        rows, half = g.shape[-2], g.shape[-1] // 2
        for lead in ((4, N, N), (6, N, N), (6, N), (2, N), (2, N), (6,), (2,), (2,)):
            scratch.append(pltpu.VMEM((*lead, rows, half), BF16))
    scratch += [
        pltpu.SemaphoreType.DMA((3, 4)),
        pltpu.SemaphoreType.DMA((3, 3, 6)),
        pltpu.SemaphoreType.DMA((3, 3, 6)),
    ]
    return pl.pallas_call(
        scatter_kernel,
        name="sum_over_chips",
        out_shape=[jax.ShapeDtypeStruct(g.shape[-2:], BF16) for g in grads],
        in_specs=[pl.BlockSpec(memory_space=pl.ANY)] * 3,
        out_specs=[pl.BlockSpec(memory_space=pltpu.VMEM)] * 3,
        scratch_shapes=scratch,
        compiler_params=pltpu.CompilerParams(collective_id=0, has_side_effects=True, vmem_limit_bytes=40 * 2**20),
        cost_estimate=pl.CostEstimate(flops=100_000_000, bytes_accessed=60_000_000, transcendentals=0),
    )(*grads)


def grad_kernel(core, a, a_other, d, d_other, out):
    dims = (((0,), (0,)), ((), ()))
    total = lax.dot_general(a[...], d[...], dims, preferred_element_type=F32)
    total = total + lax.dot_general(a_other[...], d_other[...], dims, preferred_element_type=F32)
    out[...] = total.astype(out.dtype)


def pair_gradient(core, a, a_other, d, d_other, bm, bn):
    tokens, m = a.shape
    n = d.shape[1] // 2
    left = pl.BlockSpec((tokens, bm), lambda i, j, core: (0, i))
    side = pl.BlockSpec((tokens, bn), lambda i, j, core: (0, core[0] * (n // bn) + j))
    return pl.pallas_call(
        grad_kernel,
        name="pair_gradient",
        out_shape=jax.ShapeDtypeStruct((m, n), BF16),
        grid_spec=pltpu.PrefetchScalarGridSpec(
            num_scalar_prefetch=1,
            grid=(m // bm, n // bn),
            in_specs=[left, left, side, side],
            out_specs=pl.BlockSpec((bm, bn), lambda i, j, core: (i, j)),
        ),
        cost_estimate=pl.CostEstimate(flops=4 * tokens * m * n, bytes_accessed=4 * tokens * (m + n) + 2 * m * n, transcendentals=0),
    )(core, a, a_other, d, d_other)


def place_kernel(width, *refs):
    blocks, out = refs[0], refs[-1]
    rows = out.shape[1]
    parts = width // 2 // LANES
    for core in range(2):
        for part in range(parts):
            at = (core * parts + part) * LANES
            out[0, :, at : at + LANES] = blocks[core, part * rows : (part + 1) * rows, :]


def place(gathered, which, layer, shape, so_far):
    _, total, width = shape
    rows = total // 64
    size = gathered.shape[1] // 3
    in_specs = [pl.BlockSpec((2, size, LANES), lambda p: (p, which, 0))]
    args = [gathered]
    if so_far is not None:
        in_specs.append(pl.BlockSpec(memory_space=pl.ANY))
        args.append(so_far)
    return pl.pallas_call(
        functools.partial(place_kernel, width),
        name="place",
        out_shape=jax.ShapeDtypeStruct(shape, BF16),
        grid=(64,),
        in_specs=in_specs,
        out_specs=pl.BlockSpec((1, rows, width), lambda p: (layer, p, 0)),
        input_output_aliases={} if so_far is None else {1: 0},
        cost_estimate=pl.CostEstimate(flops=10_000_000, bytes_accessed=4 * total * width, transcendentals=0),
    )(*args)


def swap(t):
    return lax.ppermute(t, "core", [(0, 1), (1, 0)])


def dot(a, b, over=(1, 0)):
    return lax.dot_general(a, b, (((over[0],), (over[1],)), ((), ())), preferred_element_type=F32)


def scale_of(h):
    wide = h.astype(F32)
    return lax.rsqrt(jnp.mean(wide**2, -1, keepdims=True) + 1e-6)


def adamw(w, m, v, g):
    m = 0.9 * m + 0.1 * g
    v = 0.95 * v + 0.05 * g * g
    step = m * lax.rsqrt(v + 1e-8) + 0.1 * w
    return (w - 0.02 * step).astype(BF16), m, v


def local_step(x, dy, wg, wu, wd, *moments):
    ms, vs = moments[:3], moments[3:]
    weights = (wg, wu, wd)
    core = lax.axis_index("core")
    chip = (lax.axis_index("x") * N + lax.axis_index("y")) * N + lax.axis_index("z")
    which = core.astype(jnp.int32)[None]
    layers = wg.shape[0]

    h, back = x[0], dy[0]
    kept = []
    for n in range(layers):
        a = (h.astype(F32) * scale_of(h)).astype(BF16)
        gate, up = dot(a, wg[n]), dot(a, wu[n])
        act = (jax.nn.silu(gate) * up).astype(BF16)
        kept.append((h, a, swap(a), gate, up, act, swap(act)))
        if n < layers - 1:
            h = h + dot(act, wd[n]).astype(BF16)

    new = [[None] * layers for _ in range(9)]
    placed = [None] * 3
    gathered = [None] * layers
    for n in reversed(range(layers)):
        h, a, a_other, gate, up, act, act_other = kept[n]
        back_other = swap(back)
        d_act = dot(back, wd[n], (1, 1)).astype(BF16).astype(F32)
        s = jax.nn.sigmoid(gate)
        d_up = (d_act * (gate * s)).astype(BF16)
        d_gate = (d_act * up * (s * (1 + gate * (1 - s)))).astype(BF16)
        d_up_other, d_gate_other = swap(d_up), swap(d_gate)
        by_down = pair_gradient(which, act, act_other, back, back_other, 512, 768)
        if n > 0:
            d_a = (dot(d_gate, wg[n], (1, 1)) + dot(d_up, wu[n], (1, 1))).astype(BF16).astype(F32)
            wide, scale = h.astype(F32), scale_of(h)
            inner = jnp.mean(d_a * wide, -1, keepdims=True)
            back = back + (scale * d_a - wide * (scale * scale * scale * inner)).astype(BF16)
        by_gate = pair_gradient(which, a, a_other, d_gate, d_gate_other, 512, 896)
        by_up = pair_gradient(which, a, a_other, d_up, d_up_other, 512, 896)
        sums = sum_over_chips([g.reshape(N, N, N, -1, g.shape[1]) for g in (by_gate, by_up, by_down)])

        blocks = []
        for k, total in enumerate(sums):
            other = swap(total)
            rows, half = total.shape[0] // 2, total.shape[1]
            halves = jnp.where(core == 0, jnp.stack([total, other]), jnp.stack([other, total]))
            mine = lax.dynamic_slice_in_dim(halves, core * rows, rows, 1)
            g = jnp.concatenate([mine[0], mine[1]], 1).astype(F32)
            at = (chip * 2 + core) * rows
            w = lax.dynamic_slice(weights[k], (n, at, 0), (1, rows, 2 * half))[0].astype(F32)
            w, m, v = adamw(w, ms[k][n], vs[k][n], g)
            new[3 + k][n], new[6 + k][n] = m, v
            keep = jnp.where(core == 0, w[:, :half], w[:, half:])
            give = jnp.where(core == 0, w[:, half:], w[:, :half])
            take = swap(give)
            both = jnp.where(core == 0, jnp.concatenate([keep, take], 0), jnp.concatenate([take, keep], 0))
            blocks += [both[:, i : i + LANES] for i in range(0, half, LANES)]
        gathered[n] = lax.all_gather(jnp.concatenate(blocks, 0), ALL, axis=0, tiled=False)

    for n in reversed(range(layers)):
        for k in range(3):
            placed[k] = place(gathered[n], k, n, weights[k].shape, placed[k])
    return (*placed, *(jnp.stack(new[i]) for i in range(3, 9)))


def solution(mesh):
    torus = Mesh(np.asarray(mesh.devices).reshape(N, N, N, 2), ALL)
    moments = P(None, ALL, None)
    return jax.shard_map(
        local_step,
        mesh=torus,
        in_specs=(P(ALL), P(ALL), P(), P(), P(), *([moments] * 6)),
        out_specs=(P(), P(), P(), *([moments] * 6)),
        check_vma=False,
    )
```

time: 2950 us -> 854 us (0.29)
  blocking collectives: 1560 us -> 0 us
  starting transfers between devices: 515 us -> 14 us
  Pallas kernels: 0 us -> 468 us
  local copies, waits for them, and re-layouts: 460 us -> 20.8 us
  matrix products: 290 us -> 181 us
  waiting for transfers between devices: 40.7 us -> 126 us
    unnamed x4 -> x0, blocking collectives: 1560 us -> none
    unnamed x160 -> x0, starting transfers between devices: 515 us -> none
    pallas_call x0 -> x14, Pallas kernels: none -> 468 us  [the longest x6 213 us: place(): pl.pallas_call(functools.partial(place_kernel, width), name='place', out_...]
    unnamed x89 -> x80, local copies, waits for them, and re-layouts: 452 us -> 19.1 us
    dot_general x15 -> x9, matrix products: 290 us -> 181 us  [dot(): lax.dot_general(a, b, (((over[0],), (over[1],)), ((), ())), preferred_ele...]
    all_gather x0 -> x2, waiting for transfers between devices: none -> 95.1 us  [local_step(): lax.all_gather(jnp.concatenate(blocks, 0), ALL, axis=0, tiled=False)]
    reshape x3 -> x0, waiting for transfers between devices: 33.9 us -> none  [step(): t.reshape(-1, *t.shape[2:])]
    ppermute x0 -> x22, waiting for transfers between devices: none -> 31 us  [swap(): return lax.ppermute(t, 'core', [(0, 1), (1, 0)])]
  transfers between devices with their start and end apart: 163 -> 24, of which waited for: 5 -> 9; matrix products, arithmetic and copies ran while one was open for 57% -> 1% of each run, Pallas kernels for 0% -> 43%
where the time goes in v1:
time: 854 us; the launch traced here: 839 us
  Pallas kernels  468 us (55%)
  matrix products  181 us (21%)
  waiting for transfers between devices  126 us (15%)
  local copies, waits for them, and re-layouts  20.8 us (2%)
  between operations  15.2 us (2%)
  starting transfers between devices  14 us (2%)
  other arithmetic  13.9 us (2%)
    pallas_call x6, Pallas kernels, place(): pl.pallas_call(functools.partial(place_kernel, width), name='place', out_...  213 us
    dot_general x9, matrix products, dot(): lax.dot_general(a, b, (((over[0],), (over[1],)), ((), ())), preferred_ele...  181 us
    pallas_call x2, Pallas kernels, sum_over_chips(): pl.pallas_call(scatter_kernel, name='sum_over_chips', out_shape=[jax.Shap...  145 us
    pallas_call x6, Pallas kernels, pair_gradient(): pl.pallas_call(grad_kernel, name='pair_gradient', out_shape=jax.ShapeDtyp...  110 us
    all_gather x2, waiting for transfers between devices, local_step(): lax.all_gather(jnp.concatenate(blocks, 0), ALL, axis=0, tiled=False)  95.1 us
    ppermute x22, waiting for transfers between devices, swap(): return lax.ppermute(t, 'core', [(0, 1), (1, 0)])  31 us
    unnamed x80, local copies, waits for them, and re-layouts  19.1 us
  transfers between devices with their start and end apart: 24, of which 9 were waited for; matrix products, arithmetic and copies ran while one was open for 1% of the time, Pallas kernels for 43%

profile of v1, /device:TPU:1, one launch (start us, length us, event | category | flops | bytes accessed | tf_op | source)
XLA Modules:
  0.0 839.4 jit_solution(3682249827747451483)
XLA Ops:
  7.2 2.6 fusion.41
  9.8 17.3 %fusion.38 = bf16[1024,3584]{1,0:T(8,128)(2,1)} fusion(bf16[2,3584,1536]{2,1,0:T(8,128)(2,1)} %param.15, bf16[1,1024,1536]{2,1,0:T(8,128)(2,1)} %param.12), kind=kOutput, calls=%fused_computation.51 | convolution fusion | flops 11277959168 | bytes 21495808 | tf_op jit(solution)/shard_map/dot_general | solution.py:235
  27.2 17.5 %fusion.24 = f32[1024,3584]{1,0:T(8,128)} fusion(bf16[2,1536,3584]{2,1,0:T(8,128)(2,1)} %param.13, bf16[1,1024,1536]{2,1,0:T(8,128)(2,1)S(1)} %copy-done.4, f32[1024]{0:T(1024)S(1)} %add_rsqrt_fusion.1), kind=kOutput, calls=%fused_computation.32 | convolution fusion | flops 11279007744 | bytes 28839936 | tf_op jit(solution)/shard_map/dot_general | solution.py:235
  44.7 22.7 %multiply_convert_fusion.1 = (bf16[1024,3584]{1,0:T(8,128)(2,1)}, f32[1024,3584]{1,0:T(8,128)}) fusion(f32[1024,3584]{1,0:T(8,128)} %fusion.24, bf16[2,1536,3584]{2,1,0:T(8,128)(2,1)} %param.14, bf16[1,1024,1536]{2,1,0:T(8,128)(2,1)S(1)} %copy-done.4, f32[1024]{0:T(1024)S(1)} %add_rsqrt_fusion.1), kind=kOutput, calls=%fused_computation.13 | convolution fusion | flops 11301027840 | bytes 50860032 | tf_op jit(solution)/shard_map/dot_general | solution.py:235
  67.4 16.8 %fusion.45 = (f32[1024]{0:T(1024)S(1)}, bf16[1024,1536]{1,0:T(8,128)(2,1)S(1)}) fusion(bf16[1024,3584]{1,0:T(8,128)(2,1)} %get-tuple-element.101.a, bf16[2,3584,1536]{2,1,0:T(8,128)(2,1)} %param.15, bf16[1,1024,1536]{2,1,0:T(8,128)(2,1)S(1)} %copy-done.4), kind=kOutput, calls=%fused_computation.56 | convolution fusion | flops 11282152448 | bytes 24645632 | tf_op jit(solution)/shard_map/dot_general | solution.py:235
  84.2 2.2 fusion.46.a
  86.4 18.3 %fusion.10 = f32[1024,3584]{1,0:T(8,128)} fusion(bf16[1024,1536]{1,0:T(8,128)(2,1)} %fusion.46.a, bf16[2,1536,3584]{2,1,0:T(8,128)(2,1)} %param.13), kind=kOutput, calls=%fused_computation.18 | convolution fusion | flops 11274289152 | bytes 28835840 | tf_op jit(solution)/shard_map/dot_general | solution.py:235
  104.7 25.9 %multiply_convert_fusion = (bf16[1024,3584]{1,0:T(8,128)(2,1)}, bf16[1024,3584]{1,0:T(8,128)(2,1)S(1)}, bf16[1024,3584]{1,0:T(8,128)(2,1)}) fusion(f32[1024,3584]{1,0:T(8,128)} %fusion.10, bf16[1024,3584]{1,0:T(8,128)(2,1)} %fusion.38, bf16[1024,1536]{1,0:T(8,128)(2,1)} %fusion.46.a, bf16[2,1536,3584]{2,1,0:T(8,128)(2,1)} %param.14), kind=kOutput, calls=%fused_computation.10 | convolution fusion | flops 11333009408 | bytes 58195968 | tf_op jit(solution)/shard_map/dot_general | solution.py:235
  130.6 18.0 %fusion.8 = f32[1024,1536]{1,0:T(8,128)} fusion(bf16[1024,3584]{1,0:T(8,128)(2,1)S(1)} %get-tuple-element.31.d, bf16[2,1536,3584]{2,1,0:T(8,128)(2,1)} %param.13), kind=kOutput, calls=%fused_computation.16 | convolution fusion | flops 11274289152 | bytes 24641536 | tf_op jit(solution)/shard_map/dot_general | solution.py:235
  148.7 17.3 %fusion.47 = (f32[1024]{0:T(1024)S(1)}, bf16[1024,1536]{1,0:T(8,128)(2,1)S(1)}) fusion(bf16[1024,1536]{1,0:T(8,128)(2,1)S(1)} %get-tuple-element.104, f32[1024,1536]{1,0:T(8,128)} %fusion.8, bf16[1024,3584]{1,0:T(8,128)(2,1)} %get-tuple-element.32.d, bf16[2,1536,3584]{2,1,0:T(8,128)(2,1)} %param.14), kind=kOutput, calls=%fused_computation.58 | convolution fusion | flops 11283725312 | bytes 30937088 | tf_op jit(solution)/shard_map/dot_general | solution.py:235
  166.0 3.4 fusion.57.d
  169.5 27.1 %fusion.5 = (bf16[1024,3584]{1,0:T(8,128)(2,1)}, bf16[1024,3584]{1,0:T(8,128)(2,1)}) fusion(f32[1024,3584]{1,0:T(8,128)} %fusion.24, f32[1024,3584]{1,0:T(8,128)} %get-tuple-element.102, bf16[1024,1536]{1,0:T(8,128)(2,1)S(1)} %fusion.57.d, bf16[2,3584,1536]{2,1,0:T(8,128)(2,1)} %param.15), kind=kOutput, calls=%fused_computation.9 | convolution fusion | flops 11329339392 | bytes 58195968 | tf_op jit(solution)/shard_map/dot_general | solution.py:235
  196.6 1.4 collective-permute-start.2
  199.7 24.6 %collective-permute-done.a_other = bf16[1024,1536]{1,0:T(8,128)(2,1)S(1)} collective-permute-done((bf16[1024,1536]{1,0:T(8,128)(2,1)S(1)}, bf16[1024,1536]{1,0:T(8,128)(2,1)S(1)}, u32[]{:S(2)}, u32[]{:S(2)}) %collective-permute-start) | collective-permute-done | bytes 3145760 | tf_op jit(solution)/shard_map/ppermute | solution.py:231
  224.7 4.1 collective-permute-done.4.d_other
  229.2 1.3 copy-done.19
  232.2 19.2 %pair_gradient.7 = bf16[1536,1792]{1,0:T(8,128)(2,1)} custom-call(s32[1]{0:T(128)} %bitcast.2.core, bf16[1024,1536]{1,0:T(8,128)(2,1)} %copy-done.7, bf16[1024,1536]{1,0:T(8,128)(2,1)} %copy-done.20, bf16[1024,3584]{1,0:T(8,128)(2,1)} %get-tuple-element.39.d, bf16[1024,3584]{1,0:T(8,128)(2,1)} %collective-permute-done.2.d_other), custom_call_target="tpu_custom_call" | custom-call | flops 11274289152 | bytes 19136512 | tf_op jit(solution)/shard_map/pair_gradient/pallas_call | solution.py:185
  251.4 19.2 %pair_gradient.6 = bf16[1536,1792]{1,0:T(8,128)(2,1)} custom-call(s32[1]{0:T(128)} %bitcast.2.core, bf16[1024,1536]{1,0:T(8,128)(2,1)} %copy-done.7, bf16[1024,1536]{1,0:T(8,128)(2,1)} %copy-done.20, bf16[1024,3584]{1,0:T(8,128)(2,1)} %get-tuple-element.40.d, bf16[1024,3584]{1,0:T(8,128)(2,1)} %collective-permute-done.1.d_other), custom_call_target="tpu_custom_call" | custom-call | flops 11274289152 | bytes 19136512 | tf_op jit(solution)/shard_map/pair_gradient/pallas_call | solution.py:185
  271.1 16.6 %pair_gradient.8 = bf16[3584,768]{1,0:T(8,128)(2,1)} custom-call(s32[1]{0:T(128)} %bitcast.2.core, bf16[1024,3584]{1,0:T(8,128)(2,1)} %get-tuple-element.101.a, bf16[1024,3584]{1,0:T(8,128)(2,1)} %collective-permute-done.3.a_other, bf16[1024,1536]{1,0:T(8,128)(2,1)} %copy-done.6, bf16[1024,1536]{1,0:T(8,128)(2,1)} %copy-done.19), custom_call_target="tpu_custom_call" | custom-call | flops 11274289152 | bytes 23330816 | tf_op jit(solution)/shard_map/pair_gradient/pallas_call | solution.py:185
  287.6 2.6 copy-done.1
  290.2 2.6 copy-done.2
  292.7 74.9 %sum_over_chips.2 = (bf16[24,1792]{1,0:T(8,128)(2,1)S(1)}, bf16[24,1792]{1,0:T(8,128)(2,1)S(1)}, bf16[56,768]{1,0:T(8,128)(2,1)S(1)}) custom-call(bf16[4,4,4,24,1792]{4,3,2,1,0:T(8,128)(2,1)S(1)} %bitcast.169, bf16[4,4,4,24,1792]{4,3,2,1,0:T(8,128)(2,1)S(1)} %bitcast.168, bf16[4,4,4,56,768]{4,3,2,1,0:T(8,128)(2,1)} %bitcast.183), custom_call_target="tpu_custom_call" | custom-call | flops 100000000 | bytes 60000000 | tf_op jit(solution)/shard_map/sum_over_chips/pallas_call | solution.py:161
  367.6 3.6 collective-permute-start.7
  371.2 19.2 %pair_gradient.9 = bf16[1536,1792]{1,0:T(8,128)(2,1)} custom-call(s32[1]{0:T(128)} %bitcast.2.core, bf16[1024,1536]{1,0:T(8,128)(2,1)} %fusion.46.a, bf16[1024,1536]{1,0:T(8,128)(2,1)} %collective-permute-done.11.a_other, bf16[1024,3584]{1,0:T(8,128)(2,1)} %copy-done.18, bf16[1024,3584]{1,0:T(8,128)(2,1)} %collective-permute-done.12.d_other), custom_call_target="tpu_custom_call" | custom-call | flops 11274289152 | bytes 19136512 | tf_op jit(solution)/shard_map/pair_gradient/pallas_call | solution.py:185
  390.5 19.2 %pair_gradient.10 = bf16[1536,1792]{1,0:T(8,128)(2,1)} custom-call(s32[1]{0:T(128)} %bitcast.2.core, bf16[1024,1536]{1,0:T(8,128)(2,1)} %fusion.46.a, bf16[1024,1536]{1,0:T(8,128)(2,1)} %collective-permute-done.11.a_other, bf16[1024,3584]{1,0:T(8,128)(2,1)} %get-tuple-element.32.d, bf16[1024,3584]{1,0:T(8,128)(2,1)} %collective-permute-done.13.d_other), custom_call_target="tpu_custom_call" | custom-call | flops 11274289152 | bytes 19136512 | tf_op jit(solution)/shard_map/pair_gradient/pallas_call | solution.py:185
  409.7 16.4 %pair_gradient.11 = bf16[3584,768]{1,0:T(8,128)(2,1)} custom-call(s32[1]{0:T(128)} %bitcast.2.core, bf16[1024,3584]{1,0:T(8,128)(2,1)} %get-tuple-element.30.a, bf16[1024,3584]{1,0:T(8,128)(2,1)} %collective-permute-done.14.a_other, bf16[1024,1536]{1,0:T(8,128)(2,1)} %bitcast.4.d, bf16[1024,1536]{1,0:T(8,128)(2,1)} %collective-permute-done.15.d_other), custom_call_target="tpu_custom_call" | custom-call | flops 11274289152 | bytes 23330816 | tf_op jit(solution)/shard_map/pair_gradient/pallas_call | solution.py:185
  426.2 2.6 copy-done
  428.7 2.6 copy-done.3
  431.3 70.2 %sum_over_chips.3 = (bf16[24,1792]{1,0:T(8,128)(2,1)S(1)}, bf16[24,1792]{1,0:T(8,128)(2,1)S(1)}, bf16[56,768]{1,0:T(8,128)(2,1)S(1)}) custom-call(bf16[4,4,4,24,1792]{4,3,2,1,0:T(8,128)(2,1)S(1)} %bitcast.167, bf16[4,4,4,24,1792]{4,3,2,1,0:T(8,128)(2,1)S(1)} %bitcast.170, bf16[4,4,4,56,768]{4,3,2,1,0:T(8,128)(2,1)} %bitcast.184), custom_call_target="tpu_custom_call" | custom-call | flops 100000000 | bytes 60000000 | tf_op jit(solution)/shard_map/sum_over_chips/pallas_call | solution.py:161
  501.5 2.6 collective-permute-start.18
  507.2 1.2 fusion.119
  508.9 1.3 fusion.82
  510.5 1.3 fusion.83
  512.4 0.8 collective-permute-done.19
  517.2 1.0 copy.40
  518.3 1.0 copy.37
  519.5 1.0 copy.39
  520.5 1.0 copy.36
  521.7 1.0 copy.38
  522.8 1.0 copy.35
  523.8 94.2 %all-gather.7.cloned.1.call-done = bf16[64512,256]{1,0:T(8,128)(2,1)} async-done(((bf16[504,256]{1,0:T(8,128)(2,1)}), bf16[64512,256]{1,0:T(8,128)(2,1)}) %all-gather.7.cloned.1.call-update) | async-done | bytes 33030160 | tf_op jit(solution)/shard_map/all_gather | solution.py:305
  617.9 35.5 %place.10.refs_1_ = bf16[2,3584,1536]{2,1,0:T(8,128)(2,1)} custom-call(bf16[128,504,256]{2,1,0:T(8,128)(2,1)} %bitcast.180), custom_call_target="tpu_custom_call" | custom-call | flops 10000000 | bytes 22020096 | tf_op jit(solution)/shard_map/place/pallas_call | solution.py:218
  653.5 35.5 %place.8.refs_1_ = bf16[2,1536,3584]{2,1,0:T(8,128)(2,1)} custom-call(bf16[128,504,256]{2,1,0:T(8,128)(2,1)} %bitcast.181), custom_call_target="tpu_custom_call" | custom-call | flops 10000000 | bytes 22020096 | tf_op jit(solution)/shard_map/place/pallas_call | solution.py:218
  689.0 35.5 %place.6.refs_1_ = bf16[2,1536,3584]{2,1,0:T(8,128)(2,1)} custom-call(bf16[128,504,256]{2,1,0:T(8,128)(2,1)} %bitcast.182), custom_call_target="tpu_custom_call" | custom-call | flops 10000000 | bytes 22020096 | tf_op jit(solution)/shard_map/place/pallas_call | solution.py:218
  724.5 1.0 all-gather.5.cloned.1.call-done
  725.5 35.5 %place.11 = bf16[2,3584,1536]{2,1,0:T(8,128)(2,1)} custom-call(bf16[128,504,256]{2,1,0:T(8,128)(2,1)} %bitcast.177, bf16[2,3584,1536]{2,1,0:T(8,128)(2,1)} %place.10.refs_1_), custom_call_target="tpu_custom_call", output_to_operand_aliasing={{}: (1, {})} | custom-call | flops 10000000 | bytes 22020096 | tf_op jit(solution)/shard_map/place/pallas_call | solution.py:218
  761.0 35.5 %place.7 = bf16[2,1536,3584]{2,1,0:T(8,128)(2,1)} custom-call(bf16[128,504,256]{2,1,0:T(8,128)(2,1)} %bitcast.178, bf16[2,1536,3584]{2,1,0:T(8,128)(2,1)} %place.6.refs_1_), custom_call_target="tpu_custom_call", output_to_operand_aliasing={{}: (1, {})} | custom-call | flops 10000000 | bytes 22020096 | tf_op jit(solution)/shard_map/place/pallas_call | solution.py:218
  796.6 35.5 %place.9 = bf16[2,1536,3584]{2,1,0:T(8,128)(2,1)} custom-call(bf16[128,504,256]{2,1,0:T(8,128)(2,1)} %bitcast.179, bf16[2,1536,3584]{2,1,0:T(8,128)(2,1)} %place.8.refs_1_), custom_call_target="tpu_custom_call", output_to_operand_aliasing={{}: (1, {})} | custom-call | flops 10000000 | bytes 22020096 | tf_op jit(solution)/shard_map/place/pallas_call | solution.py:218
  (153 shorter events, 13.2 us)
Async XLA Ops:
  7.2 610.8 %all-gather.7.cloned.1.call-start = ((), (), s32[]{:S(2)}) async-start(), calls=%async_computation.1 | async-start | bytes 33288192 | tf_op jit(solution)/shard_map/all_gather | solution.py:305
  9.8 34.9 %copy-start.16 = (f32[1024]{0:T(1024)}, f32[1024]{0:T(1024)S(1)}, u32[]{:S(2)}) copy-start(f32[1024]{0:T(1024)S(1)} %add_rsqrt_fusion.1) | copy-start | bytes 12292
  9.8 17.4 %copy-start.4 = (bf16[1,1024,1536]{2,1,0:T(8,128)(2,1)S(1)}, bf16[1,1024,1536]{2,1,0:T(8,128)(2,1)}, u32[]{:S(2)}) copy-start(bf16[1,1024,1536]{2,1,0:T(8,128)(2,1)} %param.11) | copy-start | bytes 9437188
  130.6 18.1 %copy-start.18 = (bf16[1024,3584]{1,0:T(8,128)(2,1)}, bf16[1024,3584]{1,0:T(8,128)(2,1)S(1)}, u32[]{:S(2)}) copy-start(bf16[1024,3584]{1,0:T(8,128)(2,1)S(1)} %get-tuple-element.31.d) | copy-start | bytes 22020100
  169.4 29.8 %copy-start.6 = (bf16[1024,1536]{1,0:T(8,128)(2,1)}, bf16[1024,1536]{1,0:T(8,128)(2,1)S(1)}, u32[]{:S(2)}) copy-start(bf16[1024,1536]{1,0:T(8,128)(2,1)S(1)} %fusion.57.d) | copy-start | bytes 9437188
  169.4 28.7 %copy-start.5 = (bf16[1,1024,1536]{2,1,0:T(8,128)(2,1)S(1)}, bf16[1,1024,1536]{2,1,0:T(8,128)(2,1)}, u32[]{:S(2)}) copy-start(bf16[1,1024,1536]{2,1,0:T(8,128)(2,1)} %param.11) | copy-start | bytes 9437188
  169.5 28.7 %copy-start.17 = (f32[1024]{0:T(1024)S(1)}, f32[1024]{0:T(1024)}, u32[]{:S(2)}) copy-start(f32[1024]{0:T(1024)} %copy-done.16) | copy-start | bytes 12292
  169.5 61.4 %copy-start.8 = (f32[2,12,3584]{2,0,1:T(2,128)S(1)}, f32[2,12,3584]{2,0,1:T(2,128)}, u32[]{:S(2)}) copy-start(f32[2,12,3584]{2,0,1:T(2,128)} %param.16) | copy-start | bytes 1032196
  169.5 61.4 %copy-start.9 = (f32[2,12,3584]{2,0,1:T(2,128)S(1)}, f32[2,12,3584]{2,0,1:T(2,128)}, u32[]{:S(2)}) copy-start(f32[2,12,3584]{2,0,1:T(2,128)} %param.19) | copy-start | bytes 1032196
  196.6 34.8 %copy-start.10 = (f32[2,12,3584]{2,0,1:T(2,128)S(1)}, f32[2,12,3584]{2,0,1:T(2,128)}, u32[]{:S(2)}) copy-start(f32[2,12,3584]{2,0,1:T(2,128)} %param.17) | copy-start | bytes 1032196
  196.6 34.8 %copy-start.11 = (f32[2,12,3584]{2,0,1:T(2,128)S(1)}, f32[2,12,3584]{2,0,1:T(2,128)}, u32[]{:S(2)}) copy-start(f32[2,12,3584]{2,0,1:T(2,128)} %param.20) | copy-start | bytes 1032196
  196.6 33.9 %collective-permute-start.2 = (bf16[1024,3584]{1,0:T(8,128)(2,1)}, bf16[1024,3584]{1,0:T(8,128)(2,1)}, u32[]{:S(2)}, u32[]{:S(2)}) collective-permute-start(bf16[1024,3584]{1,0:T(8,128)(2,1)} %get-tuple-element.39.d), channel_id=1, source_target_pairs={{0,1},{1,0},{2,3},{3,2},{4,5},{5,4},{6,7},{7,6},{8,9},{9,8},{10,11... | collective-permute-start | bytes 22020104 | tf_op jit(solution)/shard_map/ppermute | solution.py:231
  198.0 33.9 %collective-permute-start.1 = (bf16[1024,3584]{1,0:T(8,128)(2,1)}, bf16[1024,3584]{1,0:T(8,128)(2,1)}, u32[]{:S(2)}, u32[]{:S(2)}) collective-permute-start(bf16[1024,3584]{1,0:T(8,128)(2,1)} %get-tuple-element.40.d), channel_id=1, source_target_pairs={{0,1},{1,0},{2,3},{3,2},{4,5},{5,4},{6,7},{7,6},{8,9},{9,8},{10,11... | collective-permute-start | bytes 22020104 | tf_op jit(solution)/shard_map/ppermute | solution.py:231
  198.7 30.1 %copy-start.7 = (bf16[1024,1536]{1,0:T(8,128)(2,1)}, bf16[1024,1536]{1,0:T(8,128)(2,1)S(1)}, u32[]{:S(2)}) copy-start(bf16[1024,1536]{1,0:T(8,128)(2,1)S(1)} %fusion.42.a) | copy-start | bytes 9437188
  198.7 25.6 %collective-permute-start = (bf16[1024,1536]{1,0:T(8,128)(2,1)S(1)}, bf16[1024,1536]{1,0:T(8,128)(2,1)S(1)}, u32[]{:S(2)}, u32[]{:S(2)}) collective-permute-start(bf16[1024,1536]{1,0:T(8,128)(2,1)S(1)} %fusion.42.a), channel_id=1, source_target_pairs={{0,1},{1,0},{2,3},{3,2},{4,5},{5,4},{6,7},{7,6},{8,9},{9,8},{10,11... | collective-permute-start | bytes 9437192 | tf_op jit(solution)/shard_map/ppermute | solution.py:231
  199.2 29.6 %collective-permute-start.4 = (bf16[1024,1536]{1,0:T(8,128)(2,1)S(1)}, bf16[1024,1536]{1,0:T(8,128)(2,1)S(1)}, u32[]{:S(2)}, u32[]{:S(2)}) collective-permute-start(bf16[1024,1536]{1,0:T(8,128)(2,1)S(1)} %fusion.57.d), channel_id=1, source_target_pairs={{0,1},{1,0},{2,3},{3,2},{4,5},{5,4},{6,7},{7,6},{8,9},{9,8},{10,11... | collective-permute-start | bytes 9437192 | tf_op jit(solution)/shard_map/ppermute | solution.py:231
  199.3 71.4 %collective-permute-start.3 = (bf16[1024,3584]{1,0:T(8,128)(2,1)}, bf16[1024,3584]{1,0:T(8,128)(2,1)}, u32[]{:S(2)}, u32[]{:S(2)}) collective-permute-start(bf16[1024,3584]{1,0:T(8,128)(2,1)} %get-tuple-element.101.a), channel_id=1, source_target_pairs={{0,1},{1,0},{2,3},{3,2},{4,5},{5,4},{6,7},{7,6},{8,9},{9,8},{10,11... | collective-permute-start | bytes 22020104 | tf_op jit(solution)/shard_map/ppermute | solution.py:231
  224.3 6.2 copy-start.20
  224.3 146.9 %collective-permute-start.12 = (bf16[1024,3584]{1,0:T(8,128)(2,1)}, bf16[1024,3584]{1,0:T(8,128)(2,1)}, u32[]{:S(2)}, u32[]{:S(2)}) collective-permute-start(bf16[1024,3584]{1,0:T(8,128)(2,1)} %copy-done.18), channel_id=1, source_target_pairs={{0,1},{1,0},{2,3},{3,2},{4,5},{5,4},{6,7},{7,6},{8,9},{9,8},{10,11... | collective-permute-start | bytes 22020104 | tf_op jit(solution)/shard_map/ppermute | solution.py:231
  228.8 1.7 copy-start.19
  228.8 161.7 %collective-permute-start.13 = (bf16[1024,3584]{1,0:T(8,128)(2,1)}, bf16[1024,3584]{1,0:T(8,128)(2,1)}, u32[]{:S(2)}, u32[]{:S(2)}) collective-permute-start(bf16[1024,3584]{1,0:T(8,128)(2,1)} %get-tuple-element.32.d), channel_id=1, source_target_pairs={{0,1},{1,0},{2,3},{3,2},{4,5},{5,4},{6,7},{7,6},{8,9},{9,8},{10,11... | collective-permute-start | bytes 22020104 | tf_op jit(solution)/shard_map/ppermute | solution.py:231
  230.5 179.2 %collective-permute-start.14 = (bf16[1024,3584]{1,0:T(8,128)(2,1)}, bf16[1024,3584]{1,0:T(8,128)(2,1)}, u32[]{:S(2)}, u32[]{:S(2)}) collective-permute-start(bf16[1024,3584]{1,0:T(8,128)(2,1)} %get-tuple-element.30.a), channel_id=1, source_target_pairs={{0,1},{1,0},{2,3},{3,2},{4,5},{5,4},{6,7},{7,6},{8,9},{9,8},{10,11... | collective-permute-start | bytes 22020104 | tf_op jit(solution)/shard_map/ppermute | solution.py:231
  232.0 135.6 %collective-permute-start.11 = (bf16[1024,1536]{1,0:T(8,128)(2,1)}, bf16[1024,1536]{1,0:T(8,128)(2,1)}, u32[]{:S(2)}, u32[]{:S(2)}) collective-permute-start(bf16[1024,1536]{1,0:T(8,128)(2,1)} %fusion.46.a), channel_id=1, source_target_pairs={{0,1},{1,0},{2,3},{3,2},{4,5},{5,4},{6,7},{7,6},{8,9},{9,8},{10,11... | collective-permute-start | bytes 9437192 | tf_op jit(solution)/shard_map/ppermute | solution.py:231
  270.7 139.1 %collective-permute-start.15 = (bf16[1024,1536]{1,0:T(8,128)(2,1)}, bf16[1024,1536]{1,0:T(8,128)(2,1)}, u32[]{:S(2)}, u32[]{:S(2)}) collective-permute-start(bf16[1024,1536]{1,0:T(8,128)(2,1)} %bitcast.4.d), channel_id=1, source_target_pairs={{0,1},{1,0},{2,3},{3,2},{4,5},{5,4},{6,7},{7,6},{8,9},{9,8},{10,11... | collective-permute-start | bytes 9437192 | tf_op jit(solution)/shard_map/ppermute | solution.py:231
  287.6 2.6 copy-start.1
  290.2 2.6 copy-start.2
  367.6 137.7 %collective-permute-start.7 = (bf16[24,1792]{1,0:T(8,128)(2,1)S(1)}, bf16[24,1792]{1,0:T(8,128)(2,1)S(1)}, u32[]{:S(2)}, u32[]{:S(2)}) collective-permute-start(bf16[24,1792]{1,0:T(8,128)(2,1)S(1)} %get-tuple-element.16), channel_id=1, source_target_pairs={{0,1},{1,0},{2,3},{3,2},{4,5},{5,4},{6,7},{7,6},{8,9},{9,8},{10,11... | collective-permute-start | bytes 258056 | tf_op jit(solution)/shard_map/ppermute | solution.py:231
  426.1 2.6 copy-start
  428.7 2.6 copy-start.3
  431.3 72.8 %copy-start.12 = (f32[2,28,1536]{2,0,1:T(2,128)S(1)}, f32[2,28,1536]{2,0,1:T(2,128)}, u32[]{:S(2)}) copy-start(f32[2,28,1536]{2,0,1:T(2,128)} %param.21) | copy-start | bytes 1032196
  431.3 72.8 %copy-start.13 = (f32[2,28,1536]{2,0,1:T(2,128)S(1)}, f32[2,28,1536]{2,0,1:T(2,128)}, u32[]{:S(2)}) copy-start(f32[2,28,1536]{2,0,1:T(2,128)} %param.18) | copy-start | bytes 1032196
  501.5 4.5 collective-permute-start.18
  504.6 2.4 collective-permute-start.5
  504.7 1.4 collective-permute-start.9
  505.2 1.8 collective-permute-start.16
  505.3 1.6 collective-permute-start.20
  508.4 4.8 collective-permute-start.21
  510.2 2.0 collective-permute-start.17
  511.8 1.3 collective-permute-start.19
  513.3 0.7 copy-start.14
  514.1 211.4 %all-gather.5.cloned.1.call-start = ((), (), s32[]{:S(2)}) async-start(), calls=%async_computation | async-start | bytes 33288192 | tf_op jit(solution)/shard_map/all_gather | solution.py:305
  514.1 1.9 collective-permute-start.10
  514.6 1.3 collective-permute-start.6
  514.8 1.3 collective-permute-start.8
  516.3 0.7 copy-start.15
Sparse Core Ops, SparseCore 0:
  514.2 103.7 all-gather.6
  621.0 104.4 all-gather.4

commit v2 on v1

--- a/solution.py
+++ b/solution.py
@@ -166,73 +166,170 @@
         out_specs=[pl.BlockSpec(memory_space=pltpu.VMEM)] * 3,
         scratch_shapes=scratch,
         compiler_params=pltpu.CompilerParams(collective_id=0, has_side_effects=True, vmem_limit_bytes=40 * 2**20),
-        cost_estimate=pl.CostEstimate(flops=100_000_000, bytes_accessed=60_000_000, transcendentals=0),
+        cost_estimate=pl.CostEstimate(flops=40_000_000_000, bytes_accessed=60_000_000, transcendentals=0),
     )(*grads)
 
 
 def grad_kernel(core, a, a_other, d, d_other, out):
-    dims = (((0,), (0,)), ((), ()))
-    total = lax.dot_general(a[...], d[...], dims, preferred_element_type=F32)
-    total = total + lax.dot_general(a_other[...], d_other[...], dims, preferred_element_type=F32)
-    out[...] = total.astype(out.dtype)
-
-
-def pair_gradient(core, a, a_other, d, d_other, bm, bn):
+    left, side = jnp.concatenate([a[...], a_other[...]], 0), jnp.concatenate([d[...], d_other[...]], 0)
+    out[...] = lax.dot_general(left, side, (((0,), (0,)), ((), ())), preferred_element_type=F32).astype(out.dtype)
+
+
+def pair_gradient(core, a, a_other, d, d_other, bm):
     tokens, m = a.shape
     n = d.shape[1] // 2
-    left = pl.BlockSpec((tokens, bm), lambda i, j, core: (0, i))
-    side = pl.BlockSpec((tokens, bn), lambda i, j, core: (0, core[0] * (n // bn) + j))
+    left = pl.BlockSpec((tokens, bm), lambda i, core: (0, i))
+    side = pl.BlockSpec((tokens, n), lambda i, core: (0, core[0]))
     return pl.pallas_call(
         grad_kernel,
         name="pair_gradient",
         out_shape=jax.ShapeDtypeStruct((m, n), BF16),
         grid_spec=pltpu.PrefetchScalarGridSpec(
             num_scalar_prefetch=1,
-            grid=(m // bm, n // bn),
+            grid=(m // bm,),
             in_specs=[left, left, side, side],
-            out_specs=pl.BlockSpec((bm, bn), lambda i, j, core: (i, j)),
+            out_specs=pl.BlockSpec((bm, n), lambda i, core: (i, 0)),
         ),
+        compiler_params=pltpu.CompilerParams(vmem_limit_bytes=48 * 2**20),
         cost_estimate=pl.CostEstimate(flops=4 * tokens * m * n, bytes_accessed=4 * tokens * (m + n) + 2 * m * n, transcendentals=0),
     )(core, a, a_other, d, d_other)
 
 
-def place_kernel(width, *refs):
+def dot(a, b, over=(1, 0)):
+    return lax.dot_general(a, b, (((over[0],), (over[1],)), ((), ())), preferred_element_type=F32)
+
+
+def local_call(body, name, flops, moved, **kw):
+    return pl.pallas_call(
+        body,
+        name=name,
+        compiler_params=pltpu.CompilerParams(vmem_limit_bytes=60 * 2**20),
+        cost_estimate=pl.CostEstimate(flops=flops, bytes_accessed=moved, transcendentals=0),
+        **kw,
+    )
+
+
+def gated_kernel(a, w_gate, w_up, gate, up, act):
+    g, u = dot(a[...], w_gate[...]), dot(a[...], w_up[...])
+    gate[...] = g
+    up[...] = u
+    act[...] = (g * jax.nn.sigmoid(g) * u).astype(act.dtype)
+
+
+def gated(a, w_gate, w_up, layer, bn=512):
+    tokens, d = a.shape
+    ff = w_gate.shape[2]
+    weight = pl.BlockSpec((None, d, bn), lambda j: (layer, 0, j))
+    out = pl.BlockSpec((tokens, bn), lambda j: (0, j))
+    return local_call(
+        gated_kernel,
+        "gated",
+        4 * tokens * d * ff,
+        4 * d * ff + 10 * tokens * ff,
+        out_shape=[jax.ShapeDtypeStruct((tokens, ff), t) for t in (F32, F32, BF16)],
+        grid=(ff // bn,),
+        in_specs=[pl.BlockSpec((tokens, d), lambda j: (0, 0)), weight, weight],
+        out_specs=[out] * 3,
+    )(a, w_gate, w_up)
+
+
+def gated_back_kernel(back, w_down, gate, up, d_gate, d_up):
+    d_act = dot(back[...], w_down[...], (1, 1)).astype(BF16).astype(F32)
+    g, u = gate[...], up[...]
+    s = jax.nn.sigmoid(g)
+    d_up[...] = (d_act * (g * s)).astype(d_up.dtype)
+    d_gate[...] = (d_act * u * (s * (1 + g * (1 - s)))).astype(d_gate.dtype)
+
+
+def gated_back(back, w_down, gate, up, layer, bn=512):
+    tokens, d = back.shape
+    ff = gate.shape[1]
+    wide = pl.BlockSpec((tokens, bn), lambda j: (0, j))
+    return local_call(
+        gated_back_kernel,
+        "gated_back",
+        2 * tokens * d * ff,
+        2 * d * ff + 12 * tokens * ff,
+        out_shape=[jax.ShapeDtypeStruct((tokens, ff), BF16)] * 2,
+        grid=(ff // bn,),
+        in_specs=[pl.BlockSpec((tokens, d), lambda j: (0, 0)), pl.BlockSpec((None, bn, d), lambda j: (layer, j, 0)), wide, wide],
+        out_specs=[wide] * 2,
+    )(back, w_down, gate, up)
+
+
+def normed_back_kernel(d_gate, d_up, w_gate, w_up, h, back, out):
+    d_a = dot(d_gate[...], w_gate[...], (1, 1)) + dot(d_up[...], w_up[...], (1, 1))
+    d_a, wide = d_a.astype(BF16).astype(F32), h[...].astype(F32)
+    scale = lax.rsqrt(jnp.mean(wide**2, -1, keepdims=True) + 1e-6)
+    inner = jnp.mean(d_a * wide, -1, keepdims=True)
+    out[...] = back[...] + (scale * d_a - wide * (scale * scale * scale * inner)).astype(BF16)
+
+
+def normed_back(d_gate, d_up, w_gate, w_up, h, back, layer, bt=256):
+    tokens, d = h.shape
+    ff = d_gate.shape[1]
+    wide = pl.BlockSpec((bt, ff), lambda i: (i, 0))
+    weight = pl.BlockSpec((None, d, ff), lambda i: (layer, 0, 0), pipeline_mode=pl.Buffered(1))
+    narrow = pl.BlockSpec((bt, d), lambda i: (i, 0))
+    return local_call(
+        normed_back_kernel,
+        "normed_back",
+        4 * tokens * d * ff,
+        4 * d * ff + 4 * tokens * ff,
+        out_shape=jax.ShapeDtypeStruct((tokens, d), BF16),
+        grid=(tokens // bt,),
+        in_specs=[wide, wide, weight, weight, narrow, narrow],
+        out_specs=narrow,
+    )(d_gate, d_up, w_gate, w_up, h, back)
+
+
+def place_kernel(rows, *refs):
     blocks, out = refs[0], refs[-1]
-    rows = out.shape[1]
-    parts = width // 2 // LANES
-    for core in range(2):
-        for part in range(parts):
-            at = (core * parts + part) * LANES
-            out[0, :, at : at + LANES] = blocks[core, part * rows : (part + 1) * rows, :]
-
-
-def place(gathered, which, layer, shape, so_far):
+    parts = out.shape[2] // 2 // LANES
+
+    def one(chip, _):
+        for core in range(2):
+            for part in range(parts):
+                at = (core * parts + part) * LANES
+                out[0, pl.ds(chip * rows, rows), at : at + LANES] = blocks[chip * 2 + core, part * rows : (part + 1) * rows, :]
+        return 0
+
+    lax.fori_loop(0, out.shape[1] // rows, one, 0)
+
+
+def place(gathered, which, layer, shape, so_far, steps=8):
     _, total, width = shape
     rows = total // 64
+    chips = 64 // steps
     size = gathered.shape[1] // 3
-    in_specs = [pl.BlockSpec((2, size, LANES), lambda p: (p, which, 0))]
+    in_specs = [pl.BlockSpec((2 * chips, size, LANES), lambda p: (p, which, 0))]
     args = [gathered]
     if so_far is not None:
         in_specs.append(pl.BlockSpec(memory_space=pl.ANY))
         args.append(so_far)
-    return pl.pallas_call(
-        functools.partial(place_kernel, width),
-        name="place",
+    return local_call(
+        functools.partial(place_kernel, rows),
+        "place",
+        100_000_000,
+        4 * total * width,
         out_shape=jax.ShapeDtypeStruct(shape, BF16),
-        grid=(64,),
+        grid=(steps,),
         in_specs=in_specs,
-        out_specs=pl.BlockSpec((1, rows, width), lambda p: (layer, p, 0)),
+        out_specs=pl.BlockSpec((1, rows * chips, width), lambda p: (layer, p, 0)),
         input_output_aliases={} if so_far is None else {1: 0},
-        cost_estimate=pl.CostEstimate(flops=10_000_000, bytes_accessed=4 * total * width, transcendentals=0),
     )(*args)
+
+
+def tied(*ts):
+    return lax.optimization_barrier(ts)
+
+
+def gather(blocks):
+    return lax.all_gather(blocks, ALL, axis=0, tiled=False)
 
 
 def swap(t):
     return lax.ppermute(t, "core", [(0, 1), (1, 0)])
-
-
-def dot(a, b, over=(1, 0)):
-    return lax.dot_general(a, b, (((over[0],), (over[1],)), ((), ())), preferred_element_type=F32)
 
 
 def scale_of(h):
@@ -257,34 +354,40 @@
 
     h, back = x[0], dy[0]
     kept = []
+    last = layers - 1
+    back_other = swap(back)
     for n in range(layers):
         a = (h.astype(F32) * scale_of(h)).astype(BF16)
-        gate, up = dot(a, wg[n]), dot(a, wu[n])
-        act = (jax.nn.silu(gate) * up).astype(BF16)
-        kept.append((h, a, swap(a), gate, up, act, swap(act)))
-        if n < layers - 1:
+        a_other = swap(a)
+        gate, up, act = gated(a, wg, wu, n)
+        if n > 0:
+            act, back_other, kept[n - 1][2], kept[n - 1][6] = tied(act, back_other, kept[n - 1][2], kept[n - 1][6])
+        kept.append([h, a, a_other, gate, up, act, swap(act)])
+        if n < last:
             h = h + dot(act, wd[n]).astype(BF16)
 
     new = [[None] * layers for _ in range(9)]
     placed = [None] * 3
     gathered = [None] * layers
+    pending = None
     for n in reversed(range(layers)):
         h, a, a_other, gate, up, act, act_other = kept[n]
-        back_other = swap(back)
-        d_act = dot(back, wd[n], (1, 1)).astype(BF16).astype(F32)
-        s = jax.nn.sigmoid(gate)
-        d_up = (d_act * (gate * s)).astype(BF16)
-        d_gate = (d_act * up * (s * (1 + gate * (1 - s)))).astype(BF16)
+        if n < last:
+            back_other = swap(back)
+        d_gate, d_up = gated_back(back, wd, gate, up, n)
         d_up_other, d_gate_other = swap(d_up), swap(d_gate)
-        by_down = pair_gradient(which, act, act_other, back, back_other, 512, 768)
+        if pending is not None:
+            d_gate, d_up, pending = tied(d_gate, d_up, pending)
+            gathered[n + 1] = gather(pending)
         if n > 0:
-            d_a = (dot(d_gate, wg[n], (1, 1)) + dot(d_up, wu[n], (1, 1))).astype(BF16).astype(F32)
-            wide, scale = h.astype(F32), scale_of(h)
-            inner = jnp.mean(d_a * wide, -1, keepdims=True)
-            back = back + (scale * d_a - wide * (scale * scale * scale * inner)).astype(BF16)
-        by_gate = pair_gradient(which, a, a_other, d_gate, d_gate_other, 512, 896)
-        by_up = pair_gradient(which, a, a_other, d_up, d_up_other, 512, 896)
+            below = normed_back(d_gate, d_up, wg, wu, h, back, n)
+            d_gate, d_up, below = tied(d_gate, d_up, below)
+        by_down = pair_gradient(which, act, act_other, back, back_other, 896)
+        by_gate = pair_gradient(which, a, a_other, d_gate, d_gate_other, 512)
+        by_up = pair_gradient(which, a, a_other, d_up, d_up_other, 512)
         sums = sum_over_chips([g.reshape(N, N, N, -1, g.shape[1]) for g in (by_gate, by_up, by_down)])
+        if n > 0:
+            back, *sums = tied(below, *sums)
 
         blocks = []
         for k, total in enumerate(sums):
@@ -302,7 +405,10 @@
             take = swap(give)
             both = jnp.where(core == 0, jnp.concatenate([keep, take], 0), jnp.concatenate([take, keep], 0))
             blocks += [both[:, i : i + LANES] for i in range(0, half, LANES)]
-        gathered[n] = lax.all_gather(jnp.concatenate(blocks, 0), ALL, axis=0, tiled=False)
+        pending = jnp.concatenate(blocks, 0)
+        if n == 0:
+            pending, *gathered[1:] = tied(pending, *gathered[1:])
+            gathered[0] = gather(pending)
 
     for n in reversed(range(layers)):
         for k in range(3):

time: 854 us -> 667 us (0.78)
  matrix products: 181 us -> 16.8 us
  waiting for transfers between devices: 126 us -> 91.5 us
  local copies, waits for them, and re-layouts: 20.8 us -> 35.3 us
    dot_general x9 -> x1, matrix products: 181 us -> 16.8 us  [dot(): lax.dot_general(a, b, (((over[0],), (over[1],)), ((), ())), preferred_ele...]
    all_gather x2, waiting for transfers between devices: 95.1 us -> 63.4 us  [gather(): return lax.all_gather(blocks, ALL, axis=0, tiled=False)]
    pallas_call x2, Pallas kernels: 145 us -> 157 us  [sum_over_chips(): pl.pallas_call(scatter_kernel, name='sum_over_chips', out_shape=[jax.Shap...]
    slice x3 -> x6, local copies, waits for them, and re-layouts: 1.59 us -> 11.4 us  [local_step(): w, m, v = adamw(w, ms[k][n], vs[k][n], g)]
    pallas_call x6, Pallas kernels: 110 us -> 101 us  [pair_gradient(): pl.pallas_call(grad_kernel, name='pair_gradient', out_shape=jax.ShapeDtyp...]
    pallas_call x6 -> x11, Pallas kernels: 213 us -> 209 us  [the longest x6 63.4 us: place(): local_call(functools.partial(place_kernel, rows), 'place', 100000000, 4 *...]
    unnamed x80 -> x102, local copies, waits for them, and re-layouts: 19.1 us -> 20 us
  transfers between devices with their start and end apart: 24 -> 24, of which waited for: 9 -> 6; matrix products, arithmetic and copies ran while one was open for 1% -> 7% of each run, Pallas kernels for 43% -> 52%
where the time goes in v2:
time: 667 us; the launch traced here: 657 us
  Pallas kernels  467 us (70%)
  waiting for transfers between devices  91.5 us (14%)
  local copies, waits for them, and re-layouts  35.3 us (5%)
  matrix products  16.8 us (3%)
  other arithmetic  15.8 us (2%)
  between operations  15.2 us (2%)
  starting transfers between devices  15.1 us (2%)
    pallas_call x2, Pallas kernels, sum_over_chips(): pl.pallas_call(scatter_kernel, name='sum_over_chips', out_shape=[jax.Shap...  157 us
    pallas_call x6, Pallas kernels, pair_gradient(): pl.pallas_call(grad_kernel, name='pair_gradient', out_shape=jax.ShapeDtyp...  101 us
    pallas_call x6, Pallas kernels, place(): local_call(functools.partial(place_kernel, rows), 'place', 100000000, 4 *...  63.4 us
    all_gather x2, waiting for transfers between devices, gather(): return lax.all_gather(blocks, ALL, axis=0, tiled=False)  63.4 us
    pallas_call x2, Pallas kernels, gated(): local_call(gated_kernel, 'gated', 4 * tokens * d * ff, 4 * d * ff + 10 *...  59.1 us
    pallas_call x2, Pallas kernels, gated_back(): local_call(gated_back_kernel, 'gated_back', 2 * tokens * d * ff, 2 * d *...  51.7 us
    pallas_call x1, Pallas kernels, normed_back(): local_call(normed_back_kernel, 'normed_back', 4 * tokens * d * ff, 4 * d...  34.8 us
    ppermute x22, waiting for transfers between devices, swap(): return lax.ppermute(t, 'core', [(0, 1), (1, 0)])  28.1 us
  transfers between devices with their start and end apart: 24, of which 6 were waited for; matrix products, arithmetic and copies ran while one was open for 7% of the time, Pallas kernels for 52%

profile of v2, /device:TPU:1, one launch (start us, length us, event | category | flops | bytes accessed | tf_op | source)
XLA Modules:
  0.0 656.8 jit_solution(950659894761038233)
XLA Ops:
  7.2 2.6 fusion.3
  9.8 2.5 fusion.4.a
  12.3 1.4 collective-permute-start.1
  13.9 29.6 %gated.2 = (f32[1024,3584]{1,0:T(8,128)}, f32[1024,3584]{1,0:T(8,128)}, bf16[1024,3584]{1,0:T(8,128)(2,1)}) custom-call(bf16[1024,1536]{1,0:T(8,128)(2,1)} %copy-done, bf16[2,1536,3584]{2,1,0:T(8,128)(2,1)} %w_gate.5, bf16[2,1536,3584]{2,1,0:T(8,128)(2,1)} %w_up.5), custom_call_target="tpu_custom_call" | custom-call | flops 22548578304 | bytes 58720256 | tf_op jit(solution)/shard_map/gated/pallas_call | solution.py:224
  43.5 1.3 collective-permute-start.2
  44.8 16.8 %fusion.5 = (f32[1024]{0:T(1024)S(1)}, bf16[1024,1536]{1,0:T(8,128)(2,1)S(1)}) fusion(bf16[1024,3584]{1,0:T(8,128)(2,1)} %get-tuple-element.41.a, bf16[2,3584,1536]{2,1,0:T(8,128)(2,1)} %w_down.3, bf16[1,1024,1536]{2,1,0:T(8,128)(2,1)} %param.11), kind=kOutput, calls=%fused_computation.9 | convolution fusion | flops 11282152448 | bytes 24645632 | tf_op jit(solution)/shard_map/dot_general | solution.py:199
  61.6 1.6 copy-done.7
  63.2 2.2 fusion.6.a
  65.4 29.5 %gated.3 = (f32[1024,3584]{1,0:T(8,128)}, f32[1024,3584]{1,0:T(8,128)}, bf16[1024,3584]{1,0:T(8,128)(2,1)}) custom-call(bf16[1024,1536]{1,0:T(8,128)(2,1)} %fusion.6.a, bf16[2,1536,3584]{2,1,0:T(8,128)(2,1)} %w_gate.5, bf16[2,1536,3584]{2,1,0:T(8,128)(2,1)} %w_up.5), custom_call_target="tpu_custom_call" | custom-call | flops 22548578304 | bytes 58720256 | tf_op jit(solution)/shard_map/gated/pallas_call | solution.py:224
  95.0 25.9 %gated_back.2 = (bf16[1024,3584]{1,0:T(8,128)(2,1)}, bf16[1024,3584]{1,0:T(8,128)(2,1)}) custom-call(bf16[1024,1536]{1,0:T(8,128)(2,1)} %bitcast.5.back.d, bf16[2,3584,1536]{2,1,0:T(8,128)(2,1)} %w_down.3, f32[1024,3584]{1,0:T(8,128)} %get-tuple-element.44.gate, f32[1024,3584]{1,0:T(8,128)} %get-tuple-element.45.up), custom_call_target="tpu_custom_call" | custom-call | flops 11274289152 | bytes 55050240 | tf_op jit(solution)/shard_map/gated_back/pallas_call | solution.py:248
  122.5 34.8 %normed_back.1.back.d = bf16[1024,1536]{1,0:T(8,128)(2,1)} custom-call(bf16[1024,3584]{1,0:T(8,128)(2,1)} %get-tuple-element.49.d_gate.d, bf16[1024,3584]{1,0:T(8,128)(2,1)} %get-tuple-element.50.d_up.d, bf16[2,1536,3584]{2,1,0:T(8,128)(2,1)} %w_gate.5, bf16[2,1536,3584]{2,1,0:T(8,128)(2,1)} %w_up.5, bf16[1024,1536]{1,0:T(8,128)(2,1)} %copy-done.7, ...), custom_call_target="tpu_custom_call" | custom-call | flops 22548578304 | bytes 36700160 | tf_op jit(solution)/shard_map/normed_back/pallas_call | solution.py:274
  157.3 1.0 fusion.100
  158.3 2.0 fusion.103
  160.4 2.1 fusion.99
  162.5 2.0 fusion.101
  164.5 2.1 fusion.104
  166.6 2.1 fusion.102
  168.7 17.0 %pair_gradient.6 = bf16[1536,1792]{1,0:T(8,128)(2,1)} custom-call(s32[1]{0:T(128)} %bitcast.2.core, bf16[1024,1536]{1,0:T(8,128)(2,1)S(1)} %copy-done.2, bf16[1024,1536]{1,0:T(8,128)(2,1)} %collective-permute-done.3.a_other, bf16[1024,3584]{1,0:T(8,128)(2,1)} %get-tuple-element.49.d_gate.d, bf16[1024,3584]{1,0:T(8,128)(2,1)} %collective-permute-done.4.d_other), custom_call_target="tpu_custom_call" | custom-call | flops 11274289152 | bytes 19136512 | tf_op jit(solution)/shard_map/pair_gradient/pallas_call | solution.py:183
  185.7 17.1 %pair_gradient.7 = bf16[1536,1792]{1,0:T(8,128)(2,1)} custom-call(s32[1]{0:T(128)} %bitcast.2.core, bf16[1024,1536]{1,0:T(8,128)(2,1)S(1)} %copy-done.2, bf16[1024,1536]{1,0:T(8,128)(2,1)} %collective-permute-done.3.a_other, bf16[1024,3584]{1,0:T(8,128)(2,1)} %get-tuple-element.50.d_up.d, bf16[1024,3584]{1,0:T(8,128)(2,1)} %collective-permute-done.5.d_other), custom_call_target="tpu_custom_call" | custom-call | flops 11274289152 | bytes 19136512 | tf_op jit(solution)/shard_map/pair_gradient/pallas_call | solution.py:183
  202.8 16.7 %pair_gradient.8 = bf16[3584,768]{1,0:T(8,128)(2,1)} custom-call(s32[1]{0:T(128)} %bitcast.2.core, bf16[1024,3584]{1,0:T(8,128)(2,1)} %get-tuple-element.51.a, bf16[1024,3584]{1,0:T(8,128)(2,1)} %collective-permute-done.6.a_other, bf16[1024,1536]{1,0:T(8,128)(2,1)} %bitcast.5.back.d, bf16[1024,1536]{1,0:T(8,128)(2,1)} %collective-permute-done.d_other), custom_call_target="tpu_custom_call" | custom-call | flops 11274289152 | bytes 23330816 | tf_op jit(solution)/shard_map/pair_gradient/pallas_call | solution.py:183
  219.6 2.6 copy-done.4
  222.1 74.5 %sum_over_chips.2 = (bf16[24,1792]{1,0:T(8,128)(2,1)S(1)}, bf16[24,1792]{1,0:T(8,128)(2,1)S(1)}, bf16[56,768]{1,0:T(8,128)(2,1)S(1)}) custom-call(bf16[4,4,4,24,1792]{4,3,2,1,0:T(8,128)(2,1)S(1)} %bitcast.126, bf16[4,4,4,24,1792]{4,3,2,1,0:T(8,128)(2,1)S(1)} %bitcast.127, bf16[4,4,4,56,768]{4,3,2,1,0:T(8,128)(2,1)} %bitcast.143), custom_call_target="tpu_custom_call" | custom-call | flops 40000000000 | bytes 60000000 | tf_op jit(solution)/shard_map/sum_over_chips/pallas_call | solution.py:161
  296.6 3.9 collective-permute-start.7
  301.1 25.9 %gated_back.3 = (bf16[1024,3584]{1,0:T(8,128)(2,1)}, bf16[1024,3584]{1,0:T(8,128)(2,1)}) custom-call(bf16[1024,1536]{1,0:T(8,128)(2,1)} %normed_back.1.back.d, bf16[2,3584,1536]{2,1,0:T(8,128)(2,1)} %w_down.3, f32[1024,3584]{1,0:T(8,128)} %get-tuple-element.57.gate, f32[1024,3584]{1,0:T(8,128)} %get-tuple-element.58.up), custom_call_target="tpu_custom_call" | custom-call | flops 11274289152 | bytes 55050240 | tf_op jit(solution)/shard_map/gated_back/pallas_call | solution.py:248
  327.6 1.0 fusion.71
  330.3 1.1 fusion.33
  331.9 1.1 fusion.34
  333.3 1.0 collective-permute-done.10
  336.1 25.9 %collective-permute-done.15.d_other = bf16[1024,1536]{1,0:T(8,128)(2,1)} collective-permute-done((bf16[1024,1536]{1,0:T(8,128)(2,1)}, bf16[1024,1536]{1,0:T(8,128)(2,1)}, u32[]{:S(2)}, u32[]{:S(2)}) %collective-permute-start.15) | collective-permute-done | bytes 3145760 | tf_op jit(solution)/shard_map/ppermute | solution.py:332
  362.0 1.9 copy-done.3
  363.9 16.2 %pair_gradient.11 = bf16[3584,768]{1,0:T(8,128)(2,1)} custom-call(s32[1]{0:T(128)} %bitcast.2.core, bf16[1024,3584]{1,0:T(8,128)(2,1)} %get-tuple-element.41.a, bf16[1024,3584]{1,0:T(8,128)(2,1)} %collective-permute-done.2.a_other, bf16[1024,1536]{1,0:T(8,128)(2,1)S(1)} %copy-done.3, bf16[1024,1536]{1,0:T(8,128)(2,1)} %collective-permute-done.15.d_other), custom_call_target="tpu_custom_call" | custom-call | flops 11274289152 | bytes 23330816 | tf_op jit(solution)/shard_map/pair_gradient/pallas_call | solution.py:183
  380.1 16.9 %pair_gradient.9 = bf16[1536,1792]{1,0:T(8,128)(2,1)} custom-call(s32[1]{0:T(128)} %bitcast.2.core, bf16[1024,1536]{1,0:T(8,128)(2,1)S(1)} %copy-done.1, bf16[1024,1536]{1,0:T(8,128)(2,1)} %collective-permute-done.1.a_other, bf16[1024,3584]{1,0:T(8,128)(2,1)} %get-tuple-element.64.d, bf16[1024,3584]{1,0:T(8,128)(2,1)} %collective-permute-done.13.d_other), custom_call_target="tpu_custom_call" | custom-call | flops 11274289152 | bytes 19136512 | tf_op jit(solution)/shard_map/pair_gradient/pallas_call | solution.py:183
  397.0 3.7 copy-done.29
  400.8 17.4 %pair_gradient.10 = bf16[1536,1792]{1,0:T(8,128)(2,1)} custom-call(s32[1]{0:T(128)} %bitcast.2.core, bf16[1024,1536]{1,0:T(8,128)(2,1)S(1)} %copy-done.1, bf16[1024,1536]{1,0:T(8,128)(2,1)} %collective-permute-done.1.a_other, bf16[1024,3584]{1,0:T(8,128)(2,1)} %get-tuple-element.65.d, bf16[1024,3584]{1,0:T(8,128)(2,1)} %copy-done.29), custom_call_target="tpu_custom_call" | custom-call | flops 11274289152 | bytes 19136512 | tf_op jit(solution)/shard_map/pair_gradient/pallas_call | solution.py:183
  418.1 2.6 copy-done.6
  420.7 82.1 %sum_over_chips.3 = (bf16[24,1792]{1,0:T(8,128)(2,1)S(1)}, bf16[24,1792]{1,0:T(8,128)(2,1)S(1)}, bf16[56,768]{1,0:T(8,128)(2,1)S(1)}) custom-call(bf16[4,4,4,24,1792]{4,3,2,1,0:T(8,128)(2,1)S(1)} %bitcast.128, bf16[4,4,4,24,1792]{4,3,2,1,0:T(8,128)(2,1)S(1)} %bitcast.129, bf16[4,4,4,56,768]{4,3,2,1,0:T(8,128)(2,1)} %bitcast.142), custom_call_target="tpu_custom_call" | custom-call | flops 40000000000 | bytes 60000000 | tf_op jit(solution)/shard_map/sum_over_chips/pallas_call | solution.py:161
  502.9 2.7 collective-permute-start.20
  507.2 1.0 fusion.72
  510.1 1.3 fusion.35
  514.2 1.0 fusion.79
  516.3 1.0 fusion.51
  522.7 10.6 %place.10.refs_1_ = bf16[2,3584,1536]{2,1,0:T(8,128)(2,1)} custom-call(bf16[128,504,256]{2,1,0:T(8,128)(2,1)} %bitcast.133), custom_call_target="tpu_custom_call" | custom-call | flops 100000000 | bytes 22020096 | tf_op jit(solution)/shard_map/place/pallas_call | solution.py:310
  533.2 10.6 %place.8.refs_1_ = bf16[2,1536,3584]{2,1,0:T(8,128)(2,1)} custom-call(bf16[128,504,256]{2,1,0:T(8,128)(2,1)} %bitcast.134), custom_call_target="tpu_custom_call" | custom-call | flops 100000000 | bytes 22020096 | tf_op jit(solution)/shard_map/place/pallas_call | solution.py:310
  543.8 10.6 %place.6.refs_1_ = bf16[2,1536,3584]{2,1,0:T(8,128)(2,1)} custom-call(bf16[128,504,256]{2,1,0:T(8,128)(2,1)} %bitcast.135), custom_call_target="tpu_custom_call" | custom-call | flops 100000000 | bytes 22020096 | tf_op jit(solution)/shard_map/place/pallas_call | solution.py:310
  554.4 63.3 %all-gather.7.cloned.1.call-done = bf16[64512,256]{1,0:T(8,128)(2,1)} async-done(((bf16[504,256]{1,0:T(8,128)(2,1)}), bf16[64512,256]{1,0:T(8,128)(2,1)}) %all-gather.7.cloned.1.call-update) | async-done | bytes 33030160 | tf_op jit(solution)/shard_map/all_gather | solution.py:328
  617.7 10.6 %place.11 = bf16[2,3584,1536]{2,1,0:T(8,128)(2,1)} custom-call(bf16[128,504,256]{2,1,0:T(8,128)(2,1)} %bitcast.130, bf16[2,3584,1536]{2,1,0:T(8,128)(2,1)} %place.10.refs_1_), custom_call_target="tpu_custom_call", output_to_operand_aliasing={{}: (1, {})} | custom-call | flops 100000000 | bytes 22020096 | tf_op jit(solution)/shard_map/place/pallas_call | solution.py:310
  628.3 10.6 %place.7 = bf16[2,1536,3584]{2,1,0:T(8,128)(2,1)} custom-call(bf16[128,504,256]{2,1,0:T(8,128)(2,1)} %bitcast.131, bf16[2,1536,3584]{2,1,0:T(8,128)(2,1)} %place.6.refs_1_), custom_call_target="tpu_custom_call", output_to_operand_aliasing={{}: (1, {})} | custom-call | flops 100000000 | bytes 22020096 | tf_op jit(solution)/shard_map/place/pallas_call | solution.py:310
  638.9 10.6 %place.9 = bf16[2,1536,3584]{2,1,0:T(8,128)(2,1)} custom-call(bf16[128,504,256]{2,1,0:T(8,128)(2,1)} %bitcast.132, bf16[2,1536,3584]{2,1,0:T(8,128)(2,1)} %place.8.refs_1_), custom_call_target="tpu_custom_call", output_to_operand_aliasing={{}: (1, {})} | custom-call | flops 100000000 | bytes 22020096 | tf_op jit(solution)/shard_map/place/pallas_call | solution.py:310
  (176 shorter events, 19.5 us)
Async XLA Ops:
  7.2 506.3 %all-gather.5.cloned.1.call-start = ((), (), s32[]{:S(2)}) async-start(), calls=%async_computation | async-start | bytes 33288192 | tf_op jit(solution)/shard_map/all_gather | solution.py:328
  12.3 109.1 %collective-permute-start.1 = (bf16[1024,1536]{1,0:T(8,128)(2,1)S(1)}, bf16[1024,1536]{1,0:T(8,128)(2,1)}, u32[]{:S(2)}, u32[]{:S(2)}) collective-permute-start(bf16[1024,1536]{1,0:T(8,128)(2,1)S(1)} %fusion.4.a), channel_id=1, source_target_pairs={{0,1},{1,0},{2,3},{3,2},{4,5},{5,4},{6,7},{7,6},{8,9},{9,8},{10,11... | collective-permute-start | bytes 9437192 | tf_op jit(solution)/shard_map/ppermute | solution.py:332
  13.7 107.8 %collective-permute-start = (bf16[1024,1536]{1,0:T(8,128)(2,1)}, bf16[1024,1536]{1,0:T(8,128)(2,1)}, u32[]{:S(2)}, u32[]{:S(2)}) collective-permute-start(bf16[1024,1536]{1,0:T(8,128)(2,1)} %bitcast.5.back.d), channel_id=1, source_target_pairs={{0,1},{1,0},{2,3},{3,2},{4,5},{5,4},{6,7},{7,6},{8,9},{9,8},{10,11... | collective-permute-start | bytes 9437192 | tf_op jit(solution)/shard_map/ppermute | solution.py:332
  43.5 78.0 %collective-permute-start.2 = (bf16[1024,3584]{1,0:T(8,128)(2,1)}, bf16[1024,3584]{1,0:T(8,128)(2,1)}, u32[]{:S(2)}, u32[]{:S(2)}) collective-permute-start(bf16[1024,3584]{1,0:T(8,128)(2,1)} %get-tuple-element.41.a), channel_id=1, source_target_pairs={{0,1},{1,0},{2,3},{3,2},{4,5},{5,4},{6,7},{7,6},{8,9},{9,8},{10,11... | collective-permute-start | bytes 22020104 | tf_op jit(solution)/shard_map/ppermute | solution.py:332
  120.9 47.8 %collective-permute-start.4 = (bf16[1024,3584]{1,0:T(8,128)(2,1)}, bf16[1024,3584]{1,0:T(8,128)(2,1)}, u32[]{:S(2)}, u32[]{:S(2)}) collective-permute-start(bf16[1024,3584]{1,0:T(8,128)(2,1)} %get-tuple-element.49.d_gate.d), channel_id=1, source_target_pairs={{0,1},{1,0},{2,3},{3,2},{4,5},{5,4},{6,7},{7,6},{8,9},{9,8},{10,11... | collective-permute-start | bytes 22020104 | tf_op jit(solution)/shard_map/ppermute | solution.py:332
  120.9 47.8 %collective-permute-start.3 = (bf16[1024,1536]{1,0:T(8,128)(2,1)}, bf16[1024,1536]{1,0:T(8,128)(2,1)}, u32[]{:S(2)}, u32[]{:S(2)}) collective-permute-start(bf16[1024,1536]{1,0:T(8,128)(2,1)} %fusion.6.a), channel_id=1, source_target_pairs={{0,1},{1,0},{2,3},{3,2},{4,5},{5,4},{6,7},{7,6},{8,9},{9,8},{10,11... | collective-permute-start | bytes 9437192 | tf_op jit(solution)/shard_map/ppermute | solution.py:332
  121.4 64.3 %collective-permute-start.5 = (bf16[1024,3584]{1,0:T(8,128)(2,1)}, bf16[1024,3584]{1,0:T(8,128)(2,1)}, u32[]{:S(2)}, u32[]{:S(2)}) collective-permute-start(bf16[1024,3584]{1,0:T(8,128)(2,1)} %get-tuple-element.50.d_up.d), channel_id=1, source_target_pairs={{0,1},{1,0},{2,3},{3,2},{4,5},{5,4},{6,7},{7,6},{8,9},{9,8},{10,11... | collective-permute-start | bytes 22020104 | tf_op jit(solution)/shard_map/ppermute | solution.py:332
  121.5 35.8 %copy-start.22 = (f32[2,28,1536]{2,0,1:T(2,128)S(1)}, f32[2,28,1536]{2,0,1:T(2,128)}, u32[]{:S(2)}) copy-start(f32[2,28,1536]{2,0,1:T(2,128)} %param.18) | copy-start | bytes 1032196
  121.5 47.2 %copy-start.2 = (bf16[1024,1536]{1,0:T(8,128)(2,1)S(1)}, bf16[1024,1536]{1,0:T(8,128)(2,1)}, u32[]{:S(2)}) copy-start(bf16[1024,1536]{1,0:T(8,128)(2,1)} %fusion.6.a) | copy-start | bytes 9437188
  121.5 81.3 %collective-permute-start.6 = (bf16[1024,3584]{1,0:T(8,128)(2,1)}, bf16[1024,3584]{1,0:T(8,128)(2,1)}, u32[]{:S(2)}, u32[]{:S(2)}) collective-permute-start(bf16[1024,3584]{1,0:T(8,128)(2,1)} %get-tuple-element.51.a), channel_id=1, source_target_pairs={{0,1},{1,0},{2,3},{3,2},{4,5},{5,4},{6,7},{7,6},{8,9},{9,8},{10,11... | collective-permute-start | bytes 22020104 | tf_op jit(solution)/shard_map/ppermute | solution.py:332
  164.5 167.4 %copy-start.12 = (f32[1,12,3584]{2,0,1:T(1,128)}, f32[1,12,3584]{2,0,1:T(1,128)S(1)}, u32[]{:S(2)}) copy-start(f32[1,12,3584]{2,0,1:T(1,128)S(1)} %get-tuple-element.87) | copy-start | bytes 516100
  185.7 33.9 %slice-start = ((s8[5505024]{0:T(1024)(128)(4,1)}), s8[4194304]{0:T(1024)(128)(4,1)S(1)}, s32[]{:S(2)}) async-start(s8[5505024]{0:T(1024)(128)(4,1)} %bitcast.124), calls=%async_computation.2 | async-start | bytes 8388608
  202.8 16.7 %slice-start.1 = ((s8[5505024]{0:T(1024)(128)(4,1)}), s8[1310720]{0:T(1024)(128)(4,1)S(1)}, s32[]{:S(2)}) async-start(s8[5505024]{0:T(1024)(128)(4,1)} %bitcast.124), calls=%async_computation.3 | async-start | bytes 2621440
  296.6 33.0 %collective-permute-start.7 = (bf16[24,1792]{1,0:T(8,128)(2,1)S(1)}, bf16[24,1792]{1,0:T(8,128)(2,1)S(1)}, u32[]{:S(2)}, u32[]{:S(2)}) collective-permute-start(bf16[24,1792]{1,0:T(8,128)(2,1)S(1)} %get-tuple-element.61), channel_id=1, source_target_pairs={{0,1},{1,0},{2,3},{3,2},{4,5},{5,4},{6,7},{7,6},{8,9},{9,8},{10,11... | collective-permute-start | bytes 258056 | tf_op jit(solution)/shard_map/ppermute | solution.py:332
  300.5 28.3 %collective-permute-start.9 = (bf16[24,1792]{1,0:T(8,128)(2,1)S(1)}, bf16[24,1792]{1,0:T(8,128)(2,1)S(1)}, u32[]{:S(2)}, u32[]{:S(2)}) collective-permute-start(bf16[24,1792]{1,0:T(8,128)(2,1)S(1)} %get-tuple-element.62), channel_id=1, source_target_pairs={{0,1},{1,0},{2,3},{3,2},{4,5},{5,4},{6,7},{7,6},{8,9},{9,8},{10,11... | collective-permute-start | bytes 258056 | tf_op jit(solution)/shard_map/ppermute | solution.py:332
  300.6 26.3 %collective-permute-start.11 = (bf16[56,768]{1,0:T(8,128)(2,1)S(1)}, bf16[56,768]{1,0:T(8,128)(2,1)S(1)}, u32[]{:S(2)}, u32[]{:S(2)}) collective-permute-start(bf16[56,768]{1,0:T(8,128)(2,1)S(1)} %get-tuple-element.63), channel_id=1, source_target_pairs={{0,1},{1,0},{2,3},{3,2},{4,5},{5,4},{6,7},{7,6},{8,9},{9,8},{10,11... | collective-permute-start | bytes 258056 | tf_op jit(solution)/shard_map/ppermute | solution.py:332
  301.1 26.6 %copy-start.17 = (f32[1,28,1536]{2,0,1:T(1,128)S(1)}, f32[1,28,1536]{2,0,1:T(1,128)}, u32[]{:S(2)}) copy-start(f32[1,28,1536]{2,0,1:T(1,128)} %get-tuple-element.85) | copy-start | bytes 516100
  301.1 26.6 %copy-start.20 = (f32[1,28,1536]{2,0,1:T(1,128)S(1)}, f32[1,28,1536]{2,0,1:T(1,128)}, u32[]{:S(2)}) copy-start(f32[1,28,1536]{2,0,1:T(1,128)} %get-tuple-element.83) | copy-start | bytes 516100
  301.1 30.8 %copy-start.14 = (f32[1,12,3584]{2,0,1:T(1,128)S(1)}, f32[1,12,3584]{2,0,1:T(1,128)}, u32[]{:S(2)}) copy-start(f32[1,12,3584]{2,0,1:T(1,128)} %get-tuple-element.89) | copy-start | bytes 516100
  328.7 5.7 collective-permute-start.12
  331.4 1.8 collective-permute-start.8
  333.0 1.3 collective-permute-start.10
  335.2 44.8 %copy-start.1 = (bf16[1024,1536]{1,0:T(8,128)(2,1)S(1)}, bf16[1024,1536]{1,0:T(8,128)(2,1)}, u32[]{:S(2)}) copy-start(bf16[1024,1536]{1,0:T(8,128)(2,1)} %copy-done) | copy-start | bytes 9437188
  335.3 282.5 %all-gather.7.cloned.1.call-start = ((), (), s32[]{:S(2)}) async-start(), calls=%async_computation.1 | async-start | bytes 33288192 | tf_op jit(solution)/shard_map/all_gather | solution.py:328
  335.3 44.8 %collective-permute-start.13 = (bf16[1024,3584]{1,0:T(8,128)(2,1)}, bf16[1024,3584]{1,0:T(8,128)(2,1)}, u32[]{:S(2)}, u32[]{:S(2)}) collective-permute-start(bf16[1024,3584]{1,0:T(8,128)(2,1)} %get-tuple-element.64.d), channel_id=1, source_target_pairs={{0,1},{1,0},{2,3},{3,2},{4,5},{5,4},{6,7},{7,6},{8,9},{9,8},{10,11... | collective-permute-start | bytes 22020104 | tf_op jit(solution)/shard_map/ppermute | solution.py:332
  335.5 61.5 %collective-permute-start.14 = (bf16[1024,3584]{1,0:T(8,128)(2,1)}, bf16[1024,3584]{1,0:T(8,128)(2,1)S(1)}, u32[]{:S(2)}, u32[]{:S(2)}) collective-permute-start(bf16[1024,3584]{1,0:T(8,128)(2,1)} %get-tuple-element.65.d), channel_id=1, source_target_pairs={{0,1},{1,0},{2,3},{3,2},{4,5},{5,4},{6,7},{7,6},{8,9},{9,8},{10,11... | collective-permute-start | bytes 22020104 | tf_op jit(solution)/shard_map/ppermute | solution.py:332
  335.9 26.1 %collective-permute-start.15 = (bf16[1024,1536]{1,0:T(8,128)(2,1)}, bf16[1024,1536]{1,0:T(8,128)(2,1)}, u32[]{:S(2)}, u32[]{:S(2)}) collective-permute-start(bf16[1024,1536]{1,0:T(8,128)(2,1)} %normed_back.1.back.d), channel_id=1, source_target_pairs={{0,1},{1,0},{2,3},{3,2},{4,5},{5,4},{6,7},{7,6},{8,9},{9,8},{10,11... | collective-permute-start | bytes 9437192 | tf_op jit(solution)/shard_map/ppermute | solution.py:332
  397.0 21.1 %copy-start.5 = (bf16[1536,1792]{1,0:T(8,128)(2,1)S(1)}, bf16[1536,1792]{1,0:T(8,128)(2,1)}, u32[]{:S(2)}) copy-start(bf16[1536,1792]{1,0:T(8,128)(2,1)} %pair_gradient.9) | copy-start | bytes 16515076
  420.7 86.5 %copy-start.16 = (f32[1,28,1536]{2,0,1:T(1,128)S(1)}, f32[1,28,1536]{2,0,1:T(1,128)}, u32[]{:S(2)}) copy-start(f32[1,28,1536]{2,0,1:T(1,128)} %get-tuple-element.84) | copy-start | bytes 516100
  420.7 86.5 %copy-start.19 = (f32[1,28,1536]{2,0,1:T(1,128)S(1)}, f32[1,28,1536]{2,0,1:T(1,128)}, u32[]{:S(2)}) copy-start(f32[1,28,1536]{2,0,1:T(1,128)} %get-tuple-element.82) | copy-start | bytes 516100
  420.7 89.4 %copy-start.8 = (f32[1,12,3584]{2,0,1:T(1,128)S(1)}, f32[1,12,3584]{2,0,1:T(1,128)}, u32[]{:S(2)}) copy-start(f32[1,12,3584]{2,0,1:T(1,128)} %get-tuple-element.91) | copy-start | bytes 516100
  420.7 89.4 %copy-start.9 = (f32[1,12,3584]{2,0,1:T(1,128)S(1)}, f32[1,12,3584]{2,0,1:T(1,128)}, u32[]{:S(2)}) copy-start(f32[1,12,3584]{2,0,1:T(1,128)} %get-tuple-element.93) | copy-start | bytes 516100
  420.7 89.4 %copy-start.10 = (f32[1,12,3584]{2,0,1:T(1,128)S(1)}, f32[1,12,3584]{2,0,1:T(1,128)}, u32[]{:S(2)}) copy-start(f32[1,12,3584]{2,0,1:T(1,128)} %get-tuple-element.86) | copy-start | bytes 516100
  420.7 89.4 %copy-start.11 = (f32[1,12,3584]{2,0,1:T(1,128)S(1)}, f32[1,12,3584]{2,0,1:T(1,128)}, u32[]{:S(2)}) copy-start(f32[1,12,3584]{2,0,1:T(1,128)} %get-tuple-element.88) | copy-start | bytes 516100
  420.7 93.5 %copy-start.18 = (f32[1,28,1536]{2,0,1:T(1,128)S(1)}, f32[1,28,1536]{2,0,1:T(1,128)}, u32[]{:S(2)}) copy-start(f32[1,28,1536]{2,0,1:T(1,128)} %get-tuple-element.85) | copy-start | bytes 516100
  420.7 93.5 %copy-start.21 = (f32[1,28,1536]{2,0,1:T(1,128)S(1)}, f32[1,28,1536]{2,0,1:T(1,128)}, u32[]{:S(2)}) copy-start(f32[1,28,1536]{2,0,1:T(1,128)} %get-tuple-element.83) | copy-start | bytes 516100
  502.8 13.5 %copy-start.13 = (f32[1,12,3584]{2,0,1:T(1,128)S(1)}, f32[1,12,3584]{2,0,1:T(1,128)}, u32[]{:S(2)}) copy-start(f32[1,12,3584]{2,0,1:T(1,128)} %copy-done.12) | copy-start | bytes 516100
  502.8 13.5 %copy-start.15 = (f32[1,12,3584]{2,0,1:T(1,128)S(1)}, f32[1,12,3584]{2,0,1:T(1,128)}, u32[]{:S(2)}) copy-start(f32[1,12,3584]{2,0,1:T(1,128)} %get-tuple-element.89) | copy-start | bytes 516100
  502.8 13.5 %copy-start.26 = (bf16[1,12,1792]{2,1,0:T(8,128)(2,1)S(1)}, bf16[1,12,1792]{2,1,0:T(8,128)(2,1)}, u32[]{:S(2)}) copy-start(bf16[1,12,1792]{2,1,0:T(8,128)(2,1)} %get-tuple-element.106) | copy-start | bytes 129028
  502.9 13.4 %copy-start.27 = (bf16[1,12,1792]{2,1,0:T(8,128)(2,1)S(1)}, bf16[1,12,1792]{2,1,0:T(8,128)(2,1)}, u32[]{:S(2)}) copy-start(bf16[1,12,1792]{2,1,0:T(8,128)(2,1)} %get-tuple-element.109) | copy-start | bytes 129028
  502.9 15.5 %copy-start.25 = (bf16[1,12,1792]{2,1,0:T(8,128)(2,1)S(1)}, bf16[1,12,1792]{2,1,0:T(8,128)(2,1)}, u32[]{:S(2)}) copy-start(bf16[1,12,1792]{2,1,0:T(8,128)(2,1)} %get-tuple-element.117) | copy-start | bytes 129028
  502.9 3.6 collective-permute-start.20
  505.6 3.1 collective-permute-start.16
  505.7 3.1 collective-permute-start.18
  508.3 4.9 collective-permute-start.21
  511.5 1.6 collective-permute-start.17
  512.0 1.3 collective-permute-start.19
  513.1 5.3 copy-start.28
  (8 other events, 15.4 us)
Sparse Core Ops, SparseCore 0:
  335.4 112.5 all-gather.4
  514.3 103.3 all-gather.6

commit v3 on v2

--- a/solution.py
+++ b/solution.py
@@ -38,8 +38,10 @@
         out[...] = total.astype(out.dtype)
 
 
-def scatter_kernel(*refs):
-    grads, outs, scratch = refs[:3], refs[3:6], refs[6:]
+def scatter_kernel(work, *refs):
+    ins, made = (work.inputs, work.outputs) if work else (0, 0)
+    grads, given, refs = refs[:3], refs[3 : 3 + ins], refs[3 + ins :]
+    outs, making, scratch = refs[:3], refs[3 : 3 + made], refs[3 + made :]
     per = 8
     me = [lax.axis_index(a) for a in RING]
     right = [lax.rem(i + 1, N) for i in me]
@@ -50,12 +52,14 @@
     for axis in range(3):
         for to in (right[axis], left[axis]):
             pl.semaphore_signal(barrier, inc=1, device_id={RING[axis]: to}, device_id_type=MESH)
+    if work:
+        pl.semaphore_signal(barrier, inc=1, device_id={"core": 1 - lax.axis_index("core")}, device_id_type=MESH)
 
     colours = []
     for m in range(3):
         own, rx1, rx2, relay2, sum2, rx3, relay3, sum3 = scratch[m * per : (m + 1) * per]
         colours.append((own, (rx1, rx2, rx3), (None, relay2, relay3), (None, sum2, sum3)))
-    local_sem, send_sem, recv_sem = scratch[3 * per :]
+    local_sem, send_sem, recv_sem, *work_sem = scratch[3 * per :]
 
     def source(m, phase, index, half):
         own, _, _, sums = colours[m]
@@ -78,7 +82,7 @@
             copy.start()
             loads.append(copy)
 
-    pl.semaphore_wait(barrier, 6)
+    pl.semaphore_wait(barrier, 7 if work else 6)
 
     pending = []
     for phase in range(3):
@@ -116,6 +120,8 @@
         if phase == 0:
             for copy in loads:
                 copy.wait()
+            if work:
+                work.first(given, making)
         for k in range(2):
             for m in range(3):
                 axis = ORDERS[m][phase]
@@ -129,6 +135,8 @@
                     passed = relays[phase].at[k]
                     add_blocks(lead, passed, source(m, phase, to, 1 - k), rx[phase].at[k])
                 flights[m].append(send(m, 4 + k, passed, to))
+        if phase == 0 and work:
+            handed = work.second(given, making, *work_sem)
         for half in range(2):
             for m in range(3):
                 axis = ORDERS[m][phase]
@@ -141,13 +149,16 @@
                 add_blocks(lead, target, mine, rx[phase].at[direct], rx[phase].at[relayed])
     for copy in pending:
         copy.wait_send()
+    if work:
+        for copy in handed:
+            copy.wait()
     for m in range(3):
         width = outs[m].shape[-1] // 2
         for half in range(2):
             outs[m][:, half * width : (half + 1) * width] = colours[m][3][2][half].astype(outs[m].dtype)
 
 
-def sum_over_chips(grads):
+def sum_over_chips(grads, work=None, given=()):
     scratch = []
     for g in grads:
         rows, half = g.shape[-2], g.shape[-1] // 2
@@ -158,16 +169,87 @@
         pltpu.SemaphoreType.DMA((3, 3, 6)),
         pltpu.SemaphoreType.DMA((3, 3, 6)),
     ]
+    anywhere = pl.BlockSpec(memory_space=pl.ANY)
+    out_shape = [jax.ShapeDtypeStruct(g.shape[-2:], BF16) for g in grads]
+    out_specs = [pl.BlockSpec(memory_space=pltpu.VMEM)] * 3
+    if work:
+        scratch += [pltpu.SemaphoreType.DMA((2,)), pltpu.SemaphoreType.DMA((2,))]
+        out_shape += work.shapes
+        out_specs += [anywhere] * work.outputs
     return pl.pallas_call(
-        scatter_kernel,
+        functools.partial(scatter_kernel, work),
         name="sum_over_chips",
-        out_shape=[jax.ShapeDtypeStruct(g.shape[-2:], BF16) for g in grads],
-        in_specs=[pl.BlockSpec(memory_space=pl.ANY)] * 3,
-        out_specs=[pl.BlockSpec(memory_space=pltpu.VMEM)] * 3,
+        out_shape=out_shape,
+        in_specs=[anywhere] * (3 + len(given)),
+        out_specs=out_specs,
         scratch_shapes=scratch,
-        compiler_params=pltpu.CompilerParams(collective_id=0, has_side_effects=True, vmem_limit_bytes=40 * 2**20),
+        compiler_params=pltpu.CompilerParams(collective_id=1 if work else 0, has_side_effects=True, vmem_limit_bytes=60 * 2**20),
         cost_estimate=pl.CostEstimate(flops=40_000_000_000, bytes_accessed=60_000_000, transcendentals=0),
-    )(*grads)
+    )(*grads, *given)
+
+
+class LayerBelow:
+    inputs, outputs = 7, 7
+
+    def __init__(self, tokens, d, ff):
+        self.tokens, self.d, self.ff = tokens, d, ff
+        half = jax.ShapeDtypeStruct((tokens, ff // 2), BF16)
+        self.shapes = [jax.ShapeDtypeStruct((ff, d // 2), BF16)] + [half] * 6
+
+    def first(self, given, making, bm=512):
+        act, act_other, back, back_other = given[:4]
+        tokens, half = self.tokens, self.d // 2
+        core = lax.axis_index("core")
+
+        def step(act, act_other, back, back_other, out):
+            dims = (((0,), (0,)), ((), ()))
+            total = lax.dot_general(act[...], back[...], dims, preferred_element_type=F32)
+            total = total + lax.dot_general(act_other[...], back_other[...], dims, preferred_element_type=F32)
+            out[...] = total.astype(out.dtype)
+
+        left = pl.BlockSpec((tokens, bm), lambda i: (0, i))
+        side = pl.BlockSpec((tokens, half), lambda i: (0, core))
+        pltpu.emit_pipeline(
+            step,
+            grid=(self.ff // bm,),
+            in_specs=[left, left, side, side],
+            out_specs=[pl.BlockSpec((bm, half), lambda i: (i, 0))],
+        )(act, act_other, back, back_other, making[0])
+
+    def second(self, given, making, send_sem, recv_sem, bn=256):
+        back, w_down, gate, up = given[2], given[4], given[5], given[6]
+        mine, theirs, others = making[1:3], making[3:5], making[5:7]
+        core = lax.axis_index("core")
+        blocks = self.ff // 2 // bn
+        copies = []
+        for half, outs in ((1 - core, theirs), (core, mine)):
+            first = half * blocks
+            wide = pl.BlockSpec((self.tokens, bn), lambda j, first=first: (0, first + j))
+            out = pl.BlockSpec((self.tokens, bn), lambda j: (0, j))
+            pltpu.emit_pipeline(
+                gated_back_kernel,
+                grid=(blocks,),
+                in_specs=[
+                    pl.BlockSpec((self.tokens, self.d), lambda j: (0, 0)),
+                    pl.BlockSpec((bn, self.d), lambda j, first=first: (first + j, 0)),
+                    wide,
+                    wide,
+                ],
+                out_specs=[out, out],
+            )(back, w_down.at[0], gate, up, *outs)
+            if outs is theirs:
+                for k in range(2):
+                    copy = pltpu.make_async_remote_copy(
+                        src_ref=theirs[k],
+                        dst_ref=others[k],
+                        send_sem=send_sem.at[k],
+                        recv_sem=recv_sem.at[k],
+                        device_id={"core": 1 - core},
+                        device_id_type=MESH,
+                    )
+                    copy.start()
+                    copies.append(copy)
+        return copies
 
 
 def grad_kernel(core, a, a_other, d, d_other, out):
@@ -175,11 +257,11 @@
     out[...] = lax.dot_general(left, side, (((0,), (0,)), ((), ())), preferred_element_type=F32).astype(out.dtype)
 
 
-def pair_gradient(core, a, a_other, d, d_other, bm):
+def pair_gradient(core, a, a_other, d, d_other, bm, halved=False):
     tokens, m = a.shape
-    n = d.shape[1] // 2
+    n = d.shape[1] if halved else d.shape[1] // 2
     left = pl.BlockSpec((tokens, bm), lambda i, core: (0, i))
-    side = pl.BlockSpec((tokens, n), lambda i, core: (0, core[0]))
+    side = pl.BlockSpec((tokens, n), lambda i, core: (0, 0 if halved else core[0]))
     return pl.pallas_call(
         grad_kernel,
         name="pair_gradient",
@@ -369,25 +451,31 @@
     new = [[None] * layers for _ in range(9)]
     placed = [None] * 3
     gathered = [None] * layers
-    pending = None
+    cut = lambda gs: [g.reshape(N, N, N, -1, g.shape[1]) for g in gs]
     for n in reversed(range(layers)):
         h, a, a_other, gate, up, act, act_other = kept[n]
-        if n < last:
-            back_other = swap(back)
-        d_gate, d_up = gated_back(back, wd, gate, up, n)
-        d_up_other, d_gate_other = swap(d_up), swap(d_gate)
-        if pending is not None:
-            d_gate, d_up, pending = tied(d_gate, d_up, pending)
-            gathered[n + 1] = gather(pending)
-        if n > 0:
+        if n == last:
+            d_gate, d_up = gated_back(back, wd, gate, up, n)
+            d_up_other, d_gate_other = swap(d_up), swap(d_gate)
             below = normed_back(d_gate, d_up, wg, wu, h, back, n)
             d_gate, d_up, below = tied(d_gate, d_up, below)
-        by_down = pair_gradient(which, act, act_other, back, back_other, 896)
-        by_gate = pair_gradient(which, a, a_other, d_gate, d_gate_other, 512)
-        by_up = pair_gradient(which, a, a_other, d_up, d_up_other, 512)
-        sums = sum_over_chips([g.reshape(N, N, N, -1, g.shape[1]) for g in (by_gate, by_up, by_down)])
-        if n > 0:
-            back, *sums = tied(below, *sums)
+            below_other = swap(below)
+            by_gate = pair_gradient(which, a, a_other, d_gate, d_gate_other, 512)
+            by_up = pair_gradient(which, a, a_other, d_up, d_up_other, 512)
+            by_down = pair_gradient(which, act, act_other, back, back_other, 896)
+            _, _, _, gate0, up0, act0, act0_other = kept[0]
+            work = LayerBelow(*back.shape, gate0.shape[1])
+            *sums, by_down0, d_gate, d_up, _, _, d_gate_other, d_up_other = sum_over_chips(
+                cut((by_gate, by_up, by_down)), work, (act0, act0_other, below, below_other, wd, gate0, up0)
+            )
+        else:
+            by_gate = pair_gradient(which, a, a_other, d_gate, d_gate_other, 512, True)
+            d_up, pending = tied(d_up, pending)
+            gathered[n + 1] = gather(pending)
+            by_up = pair_gradient(which, a, a_other, d_up, d_up_other, 512, True)
+            sums = sum_over_chips(cut((by_gate, by_up, by_down0)))
+            tied_all = tied(*sums, *ms, *vs)
+            sums, ms, vs = tied_all[:3], tied_all[3:6], tied_all[6:]
 
         blocks = []
         for k, total in enumerate(sums):

time: 667 us -> 655 us (0.982)
  waiting for transfers between devices: 91.5 us -> 63.7 us
  Pallas kernels: 467 us -> 475 us
  local copies, waits for them, and re-layouts: 35.3 us -> 43.3 us
  other arithmetic: 15.8 us -> 22.6 us
    pallas_call x2, Pallas kernels: 157 us -> 207 us  [sum_over_chips(): pl.pallas_call(functools.partial(scatter_kernel, work), name='sum_over_ch...]
    ppermute x22 -> x20, waiting for transfers between devices: 28.1 us -> 1.58 us  [swap(): return lax.ppermute(t, 'core', [(0, 1), (1, 0)])]
    pallas_call x2 -> x1, Pallas kernels: 51.7 us -> 25.9 us  [gated_back(): local_call(gated_back_kernel, 'gated_back', 2 * tokens * d * ff, 2 * d *...]
    pallas_call x6 -> x5, Pallas kernels: 101 us -> 84.1 us  [pair_gradient(): pl.pallas_call(grad_kernel, name='pair_gradient', out_shape=jax.ShapeDtyp...]
    unnamed x102 -> x72, local copies, waits for them, and re-layouts: 20 us -> 27.1 us
    ppermute x22 -> x20, starting transfers between devices: 15 us -> 12.8 us  [swap(): return lax.ppermute(t, 'core', [(0, 1), (1, 0)])]
  transfers between devices with their start and end apart: 24 -> 22, of which waited for: 6 -> 3; matrix products, arithmetic and copies ran while one was open for 7% -> 11% of each run, Pallas kernels for 52% -> 54%
where the time goes in v3:
time: 655 us; the launch traced here: 649 us
  Pallas kernels  475 us (73%)
  waiting for transfers between devices  63.7 us (10%)
  local copies, waits for them, and re-layouts  43.3 us (7%)
  other arithmetic  22.6 us (3%)
  matrix products  16.8 us (3%)
  between operations  14.8 us (2%)
  starting transfers between devices  12.8 us (2%)
    pallas_call x2, Pallas kernels, sum_over_chips(): pl.pallas_call(functools.partial(scatter_kernel, work), name='sum_over_ch...  207 us
    pallas_call x5, Pallas kernels, pair_gradient(): pl.pallas_call(grad_kernel, name='pair_gradient', out_shape=jax.ShapeDtyp...  84.1 us
    pallas_call x6, Pallas kernels, place(): local_call(functools.partial(place_kernel, rows), 'place', 100000000, 4 *...  63.4 us
    all_gather x2, waiting for transfers between devices, gather(): return lax.all_gather(blocks, ALL, axis=0, tiled=False)  62.1 us
    pallas_call x2, Pallas kernels, gated(): local_call(gated_kernel, 'gated', 4 * tokens * d * ff, 4 * d * ff + 10 *...  59.2 us
    pallas_call x1, Pallas kernels, normed_back(): local_call(normed_back_kernel, 'normed_back', 4 * tokens * d * ff, 4 * d...  34.8 us
    unnamed x72, local copies, waits for them, and re-layouts  27.1 us
    pallas_call x1, Pallas kernels, gated_back(): local_call(gated_back_kernel, 'gated_back', 2 * tokens * d * ff, 2 * d *...  25.9 us
  transfers between devices with their start and end apart: 22, of which 3 were waited for; matrix products, arithmetic and copies ran while one was open for 11% of the time, Pallas kernels for 54%

profile of v3, /device:TPU:1, one launch (start us, length us, event | category | flops | bytes accessed | tf_op | source)
XLA Modules:
  0.0 648.6 jit_solution(12163187371003189065)
XLA Ops:
  7.2 2.6 fusion.3
  9.8 2.5 fusion.4.a
  12.3 1.4 collective-permute-start.1
  14.0 29.5 %gated.2 = (f32[1024,3584]{1,0:T(8,128)}, f32[1024,3584]{1,0:T(8,128)}, bf16[1024,3584]{1,0:T(8,128)(2,1)}) custom-call(bf16[1024,1536]{1,0:T(8,128)(2,1)} %copy-done, bf16[2,1536,3584]{2,1,0:T(8,128)(2,1)} %w_gate.5, bf16[2,1536,3584]{2,1,0:T(8,128)(2,1)} %w_up.5), custom_call_target="tpu_custom_call" | custom-call | flops 22548578304 | bytes 58720256 | tf_op jit(solution)/shard_map/gated/pallas_call | solution.py:306
  43.5 1.4 collective-permute-start.2
  44.8 16.8 %fusion.5 = (f32[1024]{0:T(1024)S(1)}, bf16[1024,1536]{1,0:T(8,128)(2,1)S(1)}) fusion(bf16[1024,3584]{1,0:T(8,128)(2,1)} %get-tuple-element.48.refs_3_, bf16[2,3584,1536]{2,1,0:T(8,128)(2,1)} %refs_7_.1, bf16[1,1024,1536]{2,1,0:T(8,128)(2,1)} %param.11), kind=kOutput, calls=%fused_computation.9 | convolution fusion | flops 11282152448 | bytes 24645632 | tf_op jit(solution)/shard_map/dot_general | solution.py:281
  61.6 1.6 copy-done.3
  63.3 2.4 fusion.6.a
  65.7 29.6 %gated.3 = (f32[1024,3584]{1,0:T(8,128)}, f32[1024,3584]{1,0:T(8,128)}, bf16[1024,3584]{1,0:T(8,128)(2,1)}) custom-call(bf16[1024,1536]{1,0:T(8,128)(2,1)} %fusion.6.a, bf16[2,1536,3584]{2,1,0:T(8,128)(2,1)} %w_gate.5, bf16[2,1536,3584]{2,1,0:T(8,128)(2,1)} %w_up.5), custom_call_target="tpu_custom_call" | custom-call | flops 22548578304 | bytes 58720256 | tf_op jit(solution)/shard_map/gated/pallas_call | solution.py:306
  95.3 25.9 %gated_back.1 = (bf16[1024,3584]{1,0:T(8,128)(2,1)}, bf16[1024,3584]{1,0:T(8,128)(2,1)}) custom-call(bf16[1024,1536]{1,0:T(8,128)(2,1)} %bitcast.4.back.d, bf16[2,3584,1536]{2,1,0:T(8,128)(2,1)} %refs_7_.1, f32[1024,3584]{1,0:T(8,128)} %get-tuple-element.51.gate, f32[1024,3584]{1,0:T(8,128)} %get-tuple-element.52.up), custom_call_target="tpu_custom_call" | custom-call | flops 11274289152 | bytes 55050240 | tf_op jit(solution)/shard_map/gated_back/pallas_call | solution.py:330
  122.6 34.8 %normed_back.1.refs_5_ = bf16[1024,1536]{1,0:T(8,128)(2,1)} custom-call(bf16[1024,3584]{1,0:T(8,128)(2,1)} %get-tuple-element.55.d_gate.d, bf16[1024,3584]{1,0:T(8,128)(2,1)} %get-tuple-element.56.d_up.d, bf16[2,1536,3584]{2,1,0:T(8,128)(2,1)} %w_gate.5, bf16[2,1536,3584]{2,1,0:T(8,128)(2,1)} %w_up.5, bf16[1024,1536]{1,0:T(8,128)(2,1)} %copy-done.3, ...), custom_call_target="tpu_custom_call" | custom-call | flops 22548578304 | bytes 36700160 | tf_op jit(solution)/shard_map/normed_back/pallas_call | solution.py:356
  158.3 16.9 %pair_gradient.5 = bf16[1536,1792]{1,0:T(8,128)(2,1)} custom-call(s32[1]{0:T(128)} %bitcast.1.core, bf16[1024,1536]{1,0:T(8,128)(2,1)S(1)} %copy-done.2, bf16[1024,1536]{1,0:T(8,128)(2,1)} %collective-permute-done.3.a_other, bf16[1024,3584]{1,0:T(8,128)(2,1)} %get-tuple-element.55.d_gate.d, bf16[1024,3584]{1,0:T(8,128)(2,1)} %collective-permute-done.4.d_other), custom_call_target="tpu_custom_call" | custom-call | flops 11274289152 | bytes 19136512 | tf_op jit(solution)/shard_map/pair_gradient/pallas_call | solution.py:265
  175.3 16.9 %pair_gradient.6 = bf16[1536,1792]{1,0:T(8,128)(2,1)} custom-call(s32[1]{0:T(128)} %bitcast.1.core, bf16[1024,1536]{1,0:T(8,128)(2,1)S(1)} %copy-done.2, bf16[1024,1536]{1,0:T(8,128)(2,1)} %collective-permute-done.3.a_other, bf16[1024,3584]{1,0:T(8,128)(2,1)} %get-tuple-element.56.d_up.d, bf16[1024,3584]{1,0:T(8,128)(2,1)} %collective-permute-done.5.d_other), custom_call_target="tpu_custom_call" | custom-call | flops 11274289152 | bytes 19136512 | tf_op jit(solution)/shard_map/pair_gradient/pallas_call | solution.py:265
  192.2 16.4 %pair_gradient.7 = bf16[3584,768]{1,0:T(8,128)(2,1)} custom-call(s32[1]{0:T(128)} %bitcast.1.core, bf16[1024,3584]{1,0:T(8,128)(2,1)} %get-tuple-element.57.a, bf16[1024,3584]{1,0:T(8,128)(2,1)} %collective-permute-done.6.a_other, bf16[1024,1536]{1,0:T(8,128)(2,1)} %bitcast.4.back.d, bf16[1024,1536]{1,0:T(8,128)(2,1)} %collective-permute-done.d_other), custom_call_target="tpu_custom_call" | custom-call | flops 11274289152 | bytes 23330816 | tf_op jit(solution)/shard_map/pair_gradient/pallas_call | solution.py:265
  208.6 91.9 %sum_over_chips.2 = (bf16[24,1792]{1,0:T(8,128)(2,1)}, bf16[24,1792]{1,0:T(8,128)(2,1)}, bf16[56,768]{1,0:T(8,128)(2,1)}, bf16[3584,768]{1,0:T(8,128)(2,1)}, bf1...) custom-call(bf16[4,4,4,24,1792]{4,3,2,1,0:T(8,128)(2,1)} %bitcast.12, ...), custom_call_target="tpu_custom_call" | custom-call | flops 40000000000 | bytes 60000000 | tf_op jit(solution)/shard_map/sum_over_chips/pallas_call | solution.py:179
  300.5 2.7 collective-permute-start.12
  303.2 1.2 slice.226
  304.3 1.8 slice.239
  306.2 1.8 slice.252
  308.0 1.2 slice.229
  309.2 1.8 slice.242
  311.0 1.8 slice.255
  314.9 1.2 fusion.67
  316.4 1.0 fusion.84
  318.0 1.0 fusion.87
  319.7 1.5 fusion.33
  333.0 16.9 %pair_gradient.8 = bf16[1536,1792]{1,0:T(8,128)(2,1)} custom-call(s32[1]{0:T(128)} %bitcast.1.core, bf16[1024,1536]{1,0:T(8,128)(2,1)S(1)} %copy-done.1, bf16[1024,1536]{1,0:T(8,128)(2,1)} %collective-permute-done.1.a_other, bf16[1024,1792]{1,0:T(8,128)(2,1)} %get-tuple-element.63.d, bf16[1024,1792]{1,0:T(8,128)(2,1)} %get-tuple-element.64.d_other), custom_call_target="tpu_custom_call" | custom-call | flops 11274289152 | bytes 19136512 | tf_op jit(solution)/shard_map/pair_gradient/pallas_call | solution.py:265
  350.0 16.9 %pair_gradient.9 = bf16[1536,1792]{1,0:T(8,128)(2,1)} custom-call(s32[1]{0:T(128)} %bitcast.1.core, bf16[1024,1536]{1,0:T(8,128)(2,1)S(1)} %copy-done.1, bf16[1024,1536]{1,0:T(8,128)(2,1)} %collective-permute-done.1.a_other, bf16[1024,1792]{1,0:T(8,128)(2,1)} %get-tuple-element.69.d, bf16[1024,1792]{1,0:T(8,128)(2,1)} %get-tuple-element.70.d_other), custom_call_target="tpu_custom_call" | custom-call | flops 11274289152 | bytes 19136512 | tf_op jit(solution)/shard_map/pair_gradient/pallas_call | solution.py:265
  366.9 115.4 %sum_over_chips.3 = (bf16[24,1792]{1,0:T(8,128)(2,1)}, bf16[24,1792]{1,0:T(8,128)(2,1)}, bf16[56,768]{1,0:T(8,128)(2,1)}) custom-call(bf16[4,4,4,24,1792]{4,3,2,1,0:T(8,128)(2,1)} %bitcast.131, bf16[4,4,4,24,1792]{4,3,2,1,0:T(8,128)(2,1)} %bitcast.132, bf16[4,4,4,56,768]{4,3,2,1,0:T(8,128)(2,1)} %bitcast.127), custom_call_target="tpu_custom_call" | custom-call | flops 40000000000 | bytes 60000000 | tf_op jit(solution)/shard_map/sum_over_chips/pallas_call | solution.py:179
  482.4 2.9 collective-permute-start.18
  486.2 1.1 copy.32
  488.9 1.0 fusion.68
  491.8 1.1 fusion.35
  494.1 1.1 fusion.36
  505.8 1.0 fusion.76
  509.7 1.0 copy.40
  510.7 1.0 copy.37
  511.8 1.0 copy.38
  512.9 1.0 copy.35
  514.0 1.0 copy.39
  515.0 1.0 copy.36
  516.0 10.6 %place.10.refs_1_ = bf16[2,3584,1536]{2,1,0:T(8,128)(2,1)} custom-call(bf16[128,504,256]{2,1,0:T(8,128)(2,1)} %bitcast.113), custom_call_target="tpu_custom_call" | custom-call | flops 100000000 | bytes 22020096 | tf_op jit(solution)/shard_map/place/pallas_call | solution.py:392
  526.6 10.6 %place.8.refs_1_ = bf16[2,1536,3584]{2,1,0:T(8,128)(2,1)} custom-call(bf16[128,504,256]{2,1,0:T(8,128)(2,1)} %bitcast.114), custom_call_target="tpu_custom_call" | custom-call | flops 100000000 | bytes 22020096 | tf_op jit(solution)/shard_map/place/pallas_call | solution.py:392
  537.2 10.6 %place.6.refs_1_ = bf16[2,1536,3584]{2,1,0:T(8,128)(2,1)} custom-call(bf16[128,504,256]{2,1,0:T(8,128)(2,1)} %bitcast.115), custom_call_target="tpu_custom_call" | custom-call | flops 100000000 | bytes 22020096 | tf_op jit(solution)/shard_map/place/pallas_call | solution.py:392
  547.8 62.1 %all-gather.7.cloned.1.call-done = bf16[64512,256]{1,0:T(8,128)(2,1)} async-done(((bf16[504,256]{1,0:T(8,128)(2,1)}), bf16[64512,256]{1,0:T(8,128)(2,1)}) %all-gather.7.cloned.1.call-update) | async-done | bytes 33030160 | tf_op jit(solution)/shard_map/all_gather | solution.py:410
  609.8 10.6 %place.11 = bf16[2,3584,1536]{2,1,0:T(8,128)(2,1)} custom-call(bf16[128,504,256]{2,1,0:T(8,128)(2,1)} %bitcast.110, bf16[2,3584,1536]{2,1,0:T(8,128)(2,1)} %place.10.refs_1_), custom_call_target="tpu_custom_call", output_to_operand_aliasing={{}: (1, {})} | custom-call | flops 100000000 | bytes 22020096 | tf_op jit(solution)/shard_map/place/pallas_call | solution.py:392
  620.4 10.6 %place.7 = bf16[2,1536,3584]{2,1,0:T(8,128)(2,1)} custom-call(bf16[128,504,256]{2,1,0:T(8,128)(2,1)} %bitcast.111, bf16[2,1536,3584]{2,1,0:T(8,128)(2,1)} %place.6.refs_1_), custom_call_target="tpu_custom_call", output_to_operand_aliasing={{}: (1, {})} | custom-call | flops 100000000 | bytes 22020096 | tf_op jit(solution)/shard_map/place/pallas_call | solution.py:392
  631.0 10.6 %place.9 = bf16[2,1536,3584]{2,1,0:T(8,128)(2,1)} custom-call(bf16[128,504,256]{2,1,0:T(8,128)(2,1)} %bitcast.112, bf16[2,1536,3584]{2,1,0:T(8,128)(2,1)} %place.8.refs_1_), custom_call_target="tpu_custom_call", output_to_operand_aliasing={{}: (1, {})} | custom-call | flops 100000000 | bytes 22020096 | tf_op jit(solution)/shard_map/place/pallas_call | solution.py:392
  (148 shorter events, 37.4 us)
Async XLA Ops:
  7.2 498.6 %all-gather.5.cloned.1.call-start = ((), (), s32[]{:S(2)}) async-start(), calls=%async_computation | async-start | bytes 33288192 | tf_op jit(solution)/shard_map/all_gather | solution.py:410
  12.3 1.7 copy-start
  12.3 109.4 %collective-permute-start.1 = (bf16[1024,1536]{1,0:T(8,128)(2,1)S(1)}, bf16[1024,1536]{1,0:T(8,128)(2,1)}, u32[]{:S(2)}, u32[]{:S(2)}) collective-permute-start(bf16[1024,1536]{1,0:T(8,128)(2,1)S(1)} %fusion.4.a), channel_id=1, source_target_pairs={{0,1},{1,0},{2,3},{3,2},{4,5},{5,4},{6,7},{7,6},{8,9},{9,8},{10,11... | collective-permute-start | bytes 9437192 | tf_op jit(solution)/shard_map/ppermute | solution.py:414
  13.7 108.0 %collective-permute-start = (bf16[1024,1536]{1,0:T(8,128)(2,1)}, bf16[1024,1536]{1,0:T(8,128)(2,1)}, u32[]{:S(2)}, u32[]{:S(2)}) collective-permute-start(bf16[1024,1536]{1,0:T(8,128)(2,1)} %bitcast.4.back.d), channel_id=1, source_target_pairs={{0,1},{1,0},{2,3},{3,2},{4,5},{5,4},{6,7},{7,6},{8,9},{9,8},{10,11... | collective-permute-start | bytes 9437192 | tf_op jit(solution)/shard_map/ppermute | solution.py:414
  43.5 78.3 %collective-permute-start.2 = (bf16[1024,3584]{1,0:T(8,128)(2,1)}, bf16[1024,3584]{1,0:T(8,128)(2,1)}, u32[]{:S(2)}, u32[]{:S(2)}) collective-permute-start(bf16[1024,3584]{1,0:T(8,128)(2,1)} %get-tuple-element.48.refs_3_), channel_id=1, source_target_pairs={{0,1},{1,0},{2,3},{3,2},{4,5},{5,4},{6,7},{7,6},{8,9},{9,8},{10,11... | collective-permute-start | bytes 22020104 | tf_op jit(solution)/shard_map/ppermute | solution.py:414
  61.6 1.7 copy-start.3
  121.2 37.1 %collective-permute-start.4 = (bf16[1024,3584]{1,0:T(8,128)(2,1)}, bf16[1024,3584]{1,0:T(8,128)(2,1)}, u32[]{:S(2)}, u32[]{:S(2)}) collective-permute-start(bf16[1024,3584]{1,0:T(8,128)(2,1)} %get-tuple-element.55.d_gate.d), channel_id=1, source_target_pairs={{0,1},{1,0},{2,3},{3,2},{4,5},{5,4},{6,7},{7,6},{8,9},{9,8},{10,11... | collective-permute-start | bytes 22020104 | tf_op jit(solution)/shard_map/ppermute | solution.py:414
  121.2 54.0 %collective-permute-start.5 = (bf16[1024,3584]{1,0:T(8,128)(2,1)}, bf16[1024,3584]{1,0:T(8,128)(2,1)}, u32[]{:S(2)}, u32[]{:S(2)}) collective-permute-start(bf16[1024,3584]{1,0:T(8,128)(2,1)} %get-tuple-element.56.d_up.d), channel_id=1, source_target_pairs={{0,1},{1,0},{2,3},{3,2},{4,5},{5,4},{6,7},{7,6},{8,9},{9,8},{10,11... | collective-permute-start | bytes 22020104 | tf_op jit(solution)/shard_map/ppermute | solution.py:414
  121.7 36.6 %copy-start.2 = (bf16[1024,1536]{1,0:T(8,128)(2,1)S(1)}, bf16[1024,1536]{1,0:T(8,128)(2,1)}, u32[]{:S(2)}) copy-start(bf16[1024,1536]{1,0:T(8,128)(2,1)} %fusion.6.a) | copy-start | bytes 9437188
  121.8 70.4 %collective-permute-start.6 = (bf16[1024,3584]{1,0:T(8,128)(2,1)}, bf16[1024,3584]{1,0:T(8,128)(2,1)}, u32[]{:S(2)}, u32[]{:S(2)}) collective-permute-start(bf16[1024,3584]{1,0:T(8,128)(2,1)} %get-tuple-element.57.a), channel_id=1, source_target_pairs={{0,1},{1,0},{2,3},{3,2},{4,5},{5,4},{6,7},{7,6},{8,9},{9,8},{10,11... | collective-permute-start | bytes 22020104 | tf_op jit(solution)/shard_map/ppermute | solution.py:414
  121.9 36.4 %collective-permute-start.3 = (bf16[1024,1536]{1,0:T(8,128)(2,1)}, bf16[1024,1536]{1,0:T(8,128)(2,1)}, u32[]{:S(2)}, u32[]{:S(2)}) collective-permute-start(bf16[1024,1536]{1,0:T(8,128)(2,1)} %fusion.6.a), channel_id=1, source_target_pairs={{0,1},{1,0},{2,3},{3,2},{4,5},{5,4},{6,7},{7,6},{8,9},{9,8},{10,11... | collective-permute-start | bytes 9437192 | tf_op jit(solution)/shard_map/ppermute | solution.py:414
  157.4 51.2 %collective-permute-start.7 = (bf16[1024,1536]{1,0:T(8,128)(2,1)}, bf16[1024,1536]{1,0:T(8,128)(2,1)}, u32[]{:S(2)}, u32[]{:S(2)}) collective-permute-start(bf16[1024,1536]{1,0:T(8,128)(2,1)} %normed_back.1.refs_5_), channel_id=1, source_target_pairs={{0,1},{1,0},{2,3},{3,2},{4,5},{5,4},{6,7},{7,6},{8,9},{9,8},{10,11... | collective-permute-start | bytes 9437192 | tf_op jit(solution)/shard_map/ppermute | solution.py:414
  300.5 32.5 %copy-start.1 = (bf16[1024,1536]{1,0:T(8,128)(2,1)S(1)}, bf16[1024,1536]{1,0:T(8,128)(2,1)}, u32[]{:S(2)}) copy-start(bf16[1024,1536]{1,0:T(8,128)(2,1)} %copy-done) | copy-start | bytes 9437188
  300.5 12.8 %collective-permute-start.12 = (bf16[56,768]{1,0:T(8,128)(2,1)}, bf16[56,768]{1,0:T(8,128)(2,1)}, u32[]{:S(2)}, u32[]{:S(2)}) collective-permute-start(bf16[56,768]{1,0:T(8,128)(2,1)} %get-tuple-element.68), channel_id=1, source_target_pairs={{0,1},{1,0},{2,3},{3,2},{4,5},{5,4},{6,7},{7,6},{8,9},{9,8},{10,11... | collective-permute-start | bytes 258056 | tf_op jit(solution)/shard_map/ppermute | solution.py:414
  312.8 5.2 collective-permute-start.8
  313.0 3.4 collective-permute-start.10
  316.1 14.9 %collective-permute-start.13 = (bf16[28,768]{1,0:T(8,128)(2,1)S(1)}, bf16[28,768]{1,0:T(8,128)(2,1)S(1)}, u32[]{:S(2)}, u32[]{:S(2)}) collective-permute-start(bf16[28,768]{1,0:T(8,128)(2,1)S(1)} %get-tuple-element.143), channel_id=1, source_target_pairs={{0,1},{1,0},{2,3},{3,2},{4,5},{5,4},{6,7},{7,6},{8,9},{9,8},{10,11... | collective-permute-start | bytes 129032 | tf_op jit(solution)/shard_map/ppermute | solution.py:414
  321.2 1.4 collective-permute-start.9
  321.7 5.1 collective-permute-start.11
  333.0 276.9 %all-gather.7.cloned.1.call-start = ((), (), s32[]{:S(2)}) async-start(), calls=%async_computation.1 | async-start | bytes 33288192 | tf_op jit(solution)/shard_map/all_gather | solution.py:410
  366.9 119.0 %copy-start.7 = (f32[2,28,1536]{2,0,1:T(2,128)S(1)}, f32[2,28,1536]{2,0,1:T(2,128)}, u32[]{:S(2)}) copy-start(f32[2,28,1536]{2,0,1:T(2,128)} %param.18) | copy-start | bytes 1032196
  366.9 119.0 %copy-start.8 = (f32[2,28,1536]{2,0,1:T(2,128)S(1)}, f32[2,28,1536]{2,0,1:T(2,128)}, u32[]{:S(2)}) copy-start(f32[2,28,1536]{2,0,1:T(2,128)} %param.21) | copy-start | bytes 1032196
  366.9 119.1 %copy-start.9 = (f32[2,12,3584]{2,0,1:T(2,128)S(1)}, f32[2,12,3584]{2,0,1:T(2,128)}, u32[]{:S(2)}) copy-start(f32[2,12,3584]{2,0,1:T(2,128)} %param.16) | copy-start | bytes 1032196
  366.9 119.2 %copy-start.10 = (f32[2,12,3584]{2,0,1:T(2,128)S(1)}, f32[2,12,3584]{2,0,1:T(2,128)}, u32[]{:S(2)}) copy-start(f32[2,12,3584]{2,0,1:T(2,128)} %param.19) | copy-start | bytes 1032196
  366.9 119.3 %copy-start.11 = (f32[2,12,3584]{2,0,1:T(2,128)S(1)}, f32[2,12,3584]{2,0,1:T(2,128)}, u32[]{:S(2)}) copy-start(f32[2,12,3584]{2,0,1:T(2,128)} %param.17) | copy-start | bytes 1032196
  482.3 11.1 %copy-start.16 = (bf16[24,1792]{1,0:T(8,128)(2,1)S(1)}, bf16[24,1792]{1,0:T(8,128)(2,1)}, u32[]{:S(2)}) copy-start(bf16[24,1792]{1,0:T(8,128)(2,1)} %get-tuple-element.79) | copy-start | bytes 258052
  482.3 23.5 %copy-start.6 = (f32[1,28,1536]{2,0,1:T(1,128)S(1)}, f32[1,28,1536]{2,0,1:T(1,128)}, u32[]{:S(2)}) copy-start(f32[1,28,1536]{2,0,1:T(1,128)} %slice.252) | copy-start | bytes 516100
  482.4 24.5 %copy-start.4 = (f32[1,12,3584]{2,0,1:T(1,128)S(1)}, f32[1,12,3584]{2,0,1:T(1,128)}, u32[]{:S(2)}) copy-start(f32[1,12,3584]{2,0,1:T(1,128)} %slice.239) | copy-start | bytes 516100
  482.4 24.5 %copy-start.5 = (f32[1,12,3584]{2,0,1:T(1,128)S(1)}, f32[1,12,3584]{2,0,1:T(1,128)}, u32[]{:S(2)}) copy-start(f32[1,12,3584]{2,0,1:T(1,128)} %slice.242) | copy-start | bytes 516100
  482.4 4.9 collective-permute-start.18
  485.3 4.9 collective-permute-start.14
  485.4 8.0 %collective-permute-start.16 = (bf16[24,1792]{1,0:T(8,128)(2,1)}, bf16[24,1792]{1,0:T(8,128)(2,1)S(1)}, u32[]{:S(2)}, u32[]{:S(2)}) collective-permute-start(bf16[24,1792]{1,0:T(8,128)(2,1)} %get-tuple-element.79), channel_id=1, source_target_pairs={{0,1},{1,0},{2,3},{3,2},{4,5},{5,4},{6,7},{7,6},{8,9},{9,8},{10,11... | collective-permute-start | bytes 258056 | tf_op jit(solution)/shard_map/ppermute | solution.py:414
  489.9 9.7 %collective-permute-start.19 = (bf16[28,768]{1,0:T(8,128)(2,1)S(1)}, bf16[28,768]{1,0:T(8,128)(2,1)S(1)}, u32[]{:S(2)}, u32[]{:S(2)}) collective-permute-start(bf16[28,768]{1,0:T(8,128)(2,1)S(1)} %get-tuple-element.141), channel_id=1, source_target_pairs={{0,1},{1,0},{2,3},{3,2},{4,5},{5,4},{6,7},{7,6},{8,9},{9,8},{10,11... | collective-permute-start | bytes 129032 | tf_op jit(solution)/shard_map/ppermute | solution.py:414
  492.9 2.5 collective-permute-start.15
  495.2 4.4 collective-permute-start.17
  505.8 5.9 copy-start.12
  505.8 5.9 copy-start.13
  505.8 8.1 %copy-start.14 = (bf16[1,12,1792]{2,1,0:T(8,128)(2,1)S(1)}, bf16[1,12,1792]{2,1,0:T(8,128)(2,1)}, u32[]{:S(2)}) copy-start(bf16[1,12,1792]{2,1,0:T(8,128)(2,1)} %get-tuple-element.104) | copy-start | bytes 129028
  505.8 8.1 %copy-start.15 = (bf16[1,12,1792]{2,1,0:T(8,128)(2,1)S(1)}, bf16[1,12,1792]{2,1,0:T(8,128)(2,1)}, u32[]{:S(2)}) copy-start(bf16[1,12,1792]{2,1,0:T(8,128)(2,1)} %get-tuple-element.107) | copy-start | bytes 129028
Sparse Core Ops, SparseCore 0:
  333.1 146.7 all-gather.4
  505.9 103.8 all-gather.6

commit v4 on v3

--- a/solution.py
+++ b/solution.py
@@ -38,11 +38,11 @@
         out[...] = total.astype(out.dtype)
 
 
-def scatter_kernel(work, *refs):
+def scatter_kernel(layer, work, *refs):
     ins, made = (work.inputs, work.outputs) if work else (0, 0)
-    grads, given, refs = refs[:3], refs[3 : 3 + ins], refs[3 + ins :]
-    outs, making, scratch = refs[:3], refs[3 : 3 + made], refs[3 + made :]
-    per = 8
+    grads, weights, moments, given, refs = refs[:3], refs[3:6], refs[6:12], refs[12 : 12 + ins], refs[12 + ins :]
+    new_moments, block, making, scratch = refs[:6], refs[6], refs[7 : 7 + made], refs[7 + made :]
+    per = 17
     me = [lax.axis_index(a) for a in RING]
     right = [lax.rem(i + 1, N) for i in me]
     left = [lax.rem(i + N - 1, N) for i in me]
@@ -52,14 +52,15 @@
     for axis in range(3):
         for to in (right[axis], left[axis]):
             pl.semaphore_signal(barrier, inc=1, device_id={RING[axis]: to}, device_id_type=MESH)
-    if work:
-        pl.semaphore_signal(barrier, inc=1, device_id={"core": 1 - lax.axis_index("core")}, device_id_type=MESH)
-
-    colours = []
+    core = lax.axis_index("core")
+    pl.semaphore_signal(barrier, inc=1, device_id={"core": 1 - core}, device_id_type=MESH)
+
+    colours, tails = [], []
     for m in range(3):
-        own, rx1, rx2, relay2, sum2, rx3, relay3, sum3 = scratch[m * per : (m + 1) * per]
+        own, rx1, rx2, relay2, sum2, rx3, relay3, sum3, *tail = scratch[m * per : (m + 1) * per]
+        tails.append(tail)
         colours.append((own, (rx1, rx2, rx3), (None, relay2, relay3), (None, sum2, sum3)))
-    local_sem, send_sem, recv_sem, *work_sem = scratch[3 * per :]
+    local_sem, send_sem, recv_sem, tail_sem, pair_send, pair_recv, *work_sem = scratch[3 * per :]
 
     def source(m, phase, index, half):
         own, _, _, sums = colours[m]
@@ -82,7 +83,17 @@
             copy.start()
             loads.append(copy)
 
-    pl.semaphore_wait(barrier, 7 if work else 6)
+    chip = (me[0] * N + me[1]) * N + me[2]
+    for m in range(3):
+        w, mom, vel = tails[m][:3]
+        rows = w.shape[0]
+        reads = (weights[m].at[layer, pl.ds(pl.multiple_of(chip * rows, 8), rows)], moments[m].at[layer], moments[3 + m].at[layer])
+        for k, (src, dst) in enumerate(zip(reads, (w, mom, vel))):
+            copy = pltpu.make_async_copy(src, dst, tail_sem.at[m, k])
+            copy.start()
+            loads.append(copy)
+
+    pl.semaphore_wait(barrier, 7)
 
     pending = []
     for phase in range(3):
@@ -147,45 +158,102 @@
                 mine = own.at[2 + half] if phase == 0 else source(m, phase, me[axis], half)
                 target = mine if phase == 0 else sums[phase].at[half]
                 add_blocks(lead, target, mine, rx[phase].at[direct], rx[phase].at[relayed])
+    def swapped(m, k, src, dst):
+        copy = pltpu.make_async_remote_copy(
+            src_ref=src,
+            dst_ref=dst,
+            send_sem=pair_send.at[m, k],
+            recv_sem=pair_recv.at[m, k],
+            device_id={"core": 1 - core},
+            device_id_type=MESH,
+        )
+        copy.start()
+        return copy
+
+    first = core == 0
+    swaps = []
+    for m in range(3):
+        w, _, _, held, other, *_ = tails[m]
+        width = held.shape[1] // 2
+        for half in range(2):
+            held[:, half * width : (half + 1) * width] = colours[m][3][2][half]
+        swaps.append(swapped(m, 0, held, other))
+    later = []
+    for m in range(3):
+        w, mom, vel, held, other, full, give, take, both = tails[m]
+        rows, width = held.shape
+        h = rows // 2
+        full[...] = w[...].astype(F32)
+        w_rows = jnp.where(first, full[:h, :], full[h:, :])
+        swaps[m].wait()
+        a, b = held[...].astype(F32), other[...].astype(F32)
+        full[:, :width] = jnp.where(first, a, b)
+        full[:, width:] = jnp.where(first, b, a)
+        g = jnp.where(first, full[:h, :], full[h:, :])
+        w_new, m_new, v_new = adamw(w_rows, mom[...], vel[...], g)
+        new_moments[m][...] = m_new
+        new_moments[3 + m][...] = v_new
+        w_new = w_new.astype(F32)
+        give[...] = jnp.where(first, w_new[:, width:], w_new[:, :width]).astype(BF16)
+        both[:h, :] = jnp.where(first, w_new[:, :width], w_new[:, width:])
+        later.append(swapped(m, 1, give, take))
+    for m in range(3):
+        take, both = tails[m][-2:]
+        rows, width = both.shape
+        h = rows // 2
+        later[m].wait()
+        kept, taken = both[:h, :], take[...].astype(F32)
+        both[:h, :] = jnp.where(first, kept, taken)
+        both[h:, :] = jnp.where(first, taken, kept)
+        base = m * block.shape[0] // 3
+        for part in range(width // LANES):
+            at = base + part * rows
+            block[at : at + rows, :] = both[:, part * LANES : (part + 1) * LANES].astype(BF16)
     for copy in pending:
         copy.wait_send()
     if work:
         for copy in handed:
             copy.wait()
-    for m in range(3):
-        width = outs[m].shape[-1] // 2
-        for half in range(2):
-            outs[m][:, half * width : (half + 1) * width] = colours[m][3][2][half].astype(outs[m].dtype)
-
-
-def sum_over_chips(grads, work=None, given=()):
+
+
+def summed_and_updated(layer, grads, weights, moments, work=None, given=()):
     scratch = []
-    for g in grads:
-        rows, half = g.shape[-2], g.shape[-1] // 2
+    for g, mom in zip(grads, moments):
+        rows, width = g.shape[-2:]
+        half, h = width // 2, rows // 2
         for lead in ((4, N, N), (6, N, N), (6, N), (2, N), (2, N), (6,), (2,), (2,)):
             scratch.append(pltpu.VMEM((*lead, rows, half), BF16))
-    scratch += [
-        pltpu.SemaphoreType.DMA((3, 4)),
-        pltpu.SemaphoreType.DMA((3, 3, 6)),
-        pltpu.SemaphoreType.DMA((3, 3, 6)),
-    ]
-    anywhere = pl.BlockSpec(memory_space=pl.ANY)
-    out_shape = [jax.ShapeDtypeStruct(g.shape[-2:], BF16) for g in grads]
-    out_specs = [pl.BlockSpec(memory_space=pltpu.VMEM)] * 3
+        scratch += [
+            pltpu.VMEM((rows, 2 * width), BF16),
+            pltpu.VMEM((h, 2 * width), F32),
+            pltpu.VMEM((h, 2 * width), F32),
+            pltpu.VMEM((rows, width), BF16),
+            pltpu.VMEM((rows, width), BF16),
+            pltpu.VMEM((rows, 2 * width), F32),
+            pltpu.VMEM((h, width), BF16),
+            pltpu.VMEM((h, width), BF16),
+            pltpu.VMEM((rows, width), F32),
+        ]
+    for shape in ((3, 4), (3, 3, 6), (3, 3, 6), (3, 3), (3, 2), (3, 2)):
+        scratch.append(pltpu.SemaphoreType.DMA(shape))
+    anywhere, vmem = pl.BlockSpec(memory_space=pl.ANY), pl.BlockSpec(memory_space=pltpu.VMEM)
+    blocks = 3 * grads[0].shape[-2] * grads[0].shape[-1] // LANES
+    out_shape = [jax.ShapeDtypeStruct(t.shape[1:], F32) for t in moments] + [jax.ShapeDtypeStruct((blocks, LANES), BF16)]
+    out_specs = [vmem] * 7
     if work:
         scratch += [pltpu.SemaphoreType.DMA((2,)), pltpu.SemaphoreType.DMA((2,))]
         out_shape += work.shapes
         out_specs += [anywhere] * work.outputs
     return pl.pallas_call(
-        functools.partial(scatter_kernel, work),
-        name="sum_over_chips",
+        functools.partial(scatter_kernel, layer, work),
+        name="summed_and_updated",
         out_shape=out_shape,
-        in_specs=[anywhere] * (3 + len(given)),
+        in_specs=[anywhere] * (12 + len(given)),
         out_specs=out_specs,
         scratch_shapes=scratch,
-        compiler_params=pltpu.CompilerParams(collective_id=1 if work else 0, has_side_effects=True, vmem_limit_bytes=60 * 2**20),
+        compiler_params=pltpu.CompilerParams(collective_id=1 if work else 0, has_side_effects=True, vmem_limit_bytes=62 * 2**20),
         cost_estimate=pl.CostEstimate(flops=40_000_000_000, bytes_accessed=60_000_000, transcendentals=0),
-    )(*grads, *given)
+    )(*grads, *weights, *moments, *given)
 
 
 class LayerBelow:
@@ -272,7 +340,7 @@
             in_specs=[left, left, side, side],
             out_specs=pl.BlockSpec((bm, n), lambda i, core: (i, 0)),
         ),
-        compiler_params=pltpu.CompilerParams(vmem_limit_bytes=48 * 2**20),
+        compiler_params=pltpu.CompilerParams(vmem_limit_bytes=60 * 2**20),
         cost_estimate=pl.CostEstimate(flops=4 * tokens * m * n, bytes_accessed=4 * tokens * (m + n) + 2 * m * n, transcendentals=0),
     )(core, a, a_other, d, d_other)
 
@@ -379,7 +447,7 @@
     lax.fori_loop(0, out.shape[1] // rows, one, 0)
 
 
-def place(gathered, which, layer, shape, so_far, steps=8):
+def place(gathered, which, layer, shape, so_far, steps=16):
     _, total, width = shape
     rows = total // 64
     chips = 64 // steps
@@ -427,10 +495,8 @@
 
 
 def local_step(x, dy, wg, wu, wd, *moments):
-    ms, vs = moments[:3], moments[3:]
     weights = (wg, wu, wd)
     core = lax.axis_index("core")
-    chip = (lax.axis_index("x") * N + lax.axis_index("y")) * N + lax.axis_index("z")
     which = core.astype(jnp.int32)[None]
     layers = wg.shape[0]
 
@@ -465,38 +531,19 @@
             by_down = pair_gradient(which, act, act_other, back, back_other, 896)
             _, _, _, gate0, up0, act0, act0_other = kept[0]
             work = LayerBelow(*back.shape, gate0.shape[1])
-            *sums, by_down0, d_gate, d_up, _, _, d_gate_other, d_up_other = sum_over_chips(
-                cut((by_gate, by_up, by_down)), work, (act0, act0_other, below, below_other, wd, gate0, up0)
+            *made, pending, by_down0, d_gate, d_up, _, _, d_gate_other, d_up_other = summed_and_updated(
+                n, cut((by_gate, by_up, by_down)), weights, moments, work, (act0, act0_other, below, below_other, wd, gate0, up0)
             )
         else:
             by_gate = pair_gradient(which, a, a_other, d_gate, d_gate_other, 512, True)
             d_up, pending = tied(d_up, pending)
             gathered[n + 1] = gather(pending)
             by_up = pair_gradient(which, a, a_other, d_up, d_up_other, 512, True)
-            sums = sum_over_chips(cut((by_gate, by_up, by_down0)))
-            tied_all = tied(*sums, *ms, *vs)
-            sums, ms, vs = tied_all[:3], tied_all[3:6], tied_all[6:]
-
-        blocks = []
-        for k, total in enumerate(sums):
-            other = swap(total)
-            rows, half = total.shape[0] // 2, total.shape[1]
-            halves = jnp.where(core == 0, jnp.stack([total, other]), jnp.stack([other, total]))
-            mine = lax.dynamic_slice_in_dim(halves, core * rows, rows, 1)
-            g = jnp.concatenate([mine[0], mine[1]], 1).astype(F32)
-            at = (chip * 2 + core) * rows
-            w = lax.dynamic_slice(weights[k], (n, at, 0), (1, rows, 2 * half))[0].astype(F32)
-            w, m, v = adamw(w, ms[k][n], vs[k][n], g)
-            new[3 + k][n], new[6 + k][n] = m, v
-            keep = jnp.where(core == 0, w[:, :half], w[:, half:])
-            give = jnp.where(core == 0, w[:, half:], w[:, :half])
-            take = swap(give)
-            both = jnp.where(core == 0, jnp.concatenate([keep, take], 0), jnp.concatenate([take, keep], 0))
-            blocks += [both[:, i : i + LANES] for i in range(0, half, LANES)]
-        pending = jnp.concatenate(blocks, 0)
-        if n == 0:
+            *made, pending = summed_and_updated(n, cut((by_gate, by_up, by_down0)), weights, moments)
             pending, *gathered[1:] = tied(pending, *gathered[1:])
             gathered[0] = gather(pending)
+        for k in range(6):
+            new[3 + k][n] = made[k]
 
     for n in reversed(range(layers)):
         for k in range(3):

time: 655 us -> 639 us (0.976)
  Pallas kernels: 475 us -> 511 us
  local copies, waits for them, and re-layouts: 43.3 us -> 17.7 us
  waiting for transfers between devices: 63.7 us -> 50.9 us
  other arithmetic: 22.6 us -> 13.1 us
  starting transfers between devices: 12.8 us -> 3.5 us
    pallas_call x6, Pallas kernels: 63.4 us -> 86.2 us  [place(): local_call(functools.partial(place_kernel, rows), 'place', 100000000, 4 *...]
    slice x12 -> x0, local copies, waits for them, and re-layouts: 13.5 us -> none  [the longest x6 9.62 us: local_step(): w, m, v = adamw(w, ms[k][n], vs[k][n], g)]
    pallas_call x2, Pallas kernels: 207 us -> 220 us  [summed_and_updated(): pl.pallas_call(functools.partial(scatter_kernel, layer, work), name='summ...]
    all_gather x2, waiting for transfers between devices: 62.1 us -> 50.9 us  [gather(): return lax.all_gather(blocks, ALL, axis=0, tiled=False)]
    unnamed x72 -> x36, local copies, waits for them, and re-layouts: 27.1 us -> 17.7 us
    ppermute x20 -> x8, starting transfers between devices: 12.8 us -> 3.42 us  [swap(): return lax.ppermute(t, 'core', [(0, 1), (1, 0)])]
  transfers between devices with their start and end apart: 22 -> 10, of which waited for: 3 -> 1; matrix products, arithmetic and copies ran while one was open for 11% -> 6% of each run, Pallas kernels for 54% -> 59%
where the time goes in v4:
time: 639 us; the launch traced here: 627 us
  Pallas kernels  511 us (80%)
  waiting for transfers between devices  50.9 us (8%)
  local copies, waits for them, and re-layouts  17.7 us (3%)
  matrix products  16.4 us (3%)
  between operations  14.4 us (2%)
  other arithmetic  13.1 us (2%)
    pallas_call x2, Pallas kernels, summed_and_updated(): pl.pallas_call(functools.partial(scatter_kernel, layer, work), name='summ...  220 us
    pallas_call x6, Pallas kernels, place(): local_call(functools.partial(place_kernel, rows), 'place', 100000000, 4 *...  86.2 us
    pallas_call x5, Pallas kernels, pair_gradient(): pl.pallas_call(grad_kernel, name='pair_gradient', out_shape=jax.ShapeDtyp...  84.8 us
    pallas_call x2, Pallas kernels, gated(): local_call(gated_kernel, 'gated', 4 * tokens * d * ff, 4 * d * ff + 10 *...  59.2 us
    all_gather x2, waiting for transfers between devices, gather(): return lax.all_gather(blocks, ALL, axis=0, tiled=False)  50.9 us
    pallas_call x1, Pallas kernels, normed_back(): local_call(normed_back_kernel, 'normed_back', 4 * tokens * d * ff, 4 * d...  35 us
    pallas_call x1, Pallas kernels, gated_back(): local_call(gated_back_kernel, 'gated_back', 2 * tokens * d * ff, 2 * d *...  26.1 us
    unnamed x36, local copies, waits for them, and re-layouts  17.7 us
  transfers between devices with their start and end apart: 10, of which 1 were waited for; matrix products, arithmetic and copies ran while one was open for 6% of the time, Pallas kernels for 59%

profile of v4, /device:TPU:1, one launch (start us, length us, event | category | flops | bytes accessed | tf_op | source)
XLA Modules:
  0.0 627.0 jit_solution(6208648138995482937)
XLA Ops:
  7.2 0.0 all-gather.5.cloned.1.call-start
  7.2 2.6 fusion.3
  9.8 4.1 fusion.4.a
  13.9 1.4 collective-permute-start.1
  15.3 29.7 %gated.2 = (f32[1024,3584]{1,0:T(8,128)}, f32[1024,3584]{1,0:T(8,128)}, bf16[1024,3584]{1,0:T(8,128)(2,1)}) custom-call(bf16[1024,1536]{1,0:T(8,128)(2,1)} %fusion.4.a, bf16[2,1536,3584]{2,1,0:T(8,128)(2,1)} %refs_3_.3, bf16[2,1536,3584]{2,1,0:T(8,128)(2,1)} %refs_4_.3), custom_call_target="tpu_custom_call" | custom-call | flops 22548578304 | bytes 58720256 | tf_op jit(solution)/shard_map/gated/pallas_call | solution.py:374
  45.0 0.6 collective-permute-start.2
  45.6 16.4 %fusion.5 = (f32[1024]{0:T(1024)S(1)}, bf16[1024,1536]{1,0:T(8,128)(2,1)S(1)}) fusion(bf16[1024,3584]{1,0:T(8,128)(2,1)} %get-tuple-element.47.refs_12_, bf16[2,3584,1536]{2,1,0:T(8,128)(2,1)} %refs_5_.3, bf16[1,1024,1536]{2,1,0:T(8,128)(2,1)S(1)} %copy-done), kind=kOutput, calls=%fused_computation.9 | convolution fusion | flops 11282152448 | bytes 24645632 | tf_op jit(solution)/shard_map/dot_general | solution.py:349
  62.1 1.6 copy-done.2
  63.7 2.3 fusion.6.a
  66.0 29.5 %gated.3 = (f32[1024,3584]{1,0:T(8,128)}, f32[1024,3584]{1,0:T(8,128)}, bf16[1024,3584]{1,0:T(8,128)(2,1)}) custom-call(bf16[1024,1536]{1,0:T(8,128)(2,1)} %fusion.6.a, bf16[2,1536,3584]{2,1,0:T(8,128)(2,1)} %refs_3_.3, bf16[2,1536,3584]{2,1,0:T(8,128)(2,1)} %refs_4_.3), custom_call_target="tpu_custom_call" | custom-call | flops 22548578304 | bytes 58720256 | tf_op jit(solution)/shard_map/gated/pallas_call | solution.py:374
  95.6 26.1 %gated_back.1 = (bf16[1024,3584]{1,0:T(8,128)(2,1)}, bf16[1024,3584]{1,0:T(8,128)(2,1)}) custom-call(bf16[1024,1536]{1,0:T(8,128)(2,1)} %bitcast.3.back.d, bf16[2,3584,1536]{2,1,0:T(8,128)(2,1)} %refs_5_.3, f32[1024,3584]{1,0:T(8,128)} %get-tuple-element.50.gate, f32[1024,3584]{1,0:T(8,128)} %get-tuple-element.51.up), custom_call_target="tpu_custom_call" | custom-call | flops 11274289152 | bytes 55050240 | tf_op jit(solution)/shard_map/gated_back/pallas_call | solution.py:398
  121.6 0.0 collective-permute-start.4
  121.6 0.5 collective-permute-start.5
  122.1 0.2 collective-permute-start.6
  122.3 0.7 collective-permute-start.3
  123.0 35.0 %normed_back.1.refs_14_ = bf16[1024,1536]{1,0:T(8,128)(2,1)} custom-call(bf16[1024,3584]{1,0:T(8,128)(2,1)} %get-tuple-element.54.d_gate.d, bf16[1024,3584]{1,0:T(8,128)(2,1)} %get-tuple-element.55.d_up.d, bf16[2,1536,3584]{2,1,0:T(8,128)(2,1)} %refs_3_.3, bf16[2,1536,3584]{2,1,0:T(8,128)(2,1)} %refs_4_.3, bf16[1024,1536]{1,0:T(8,128)(2,1)} %copy-done.2, ...), custom_call_target="tpu_custom_call" | custom-call | flops 22548578304 | bytes 36700160 | tf_op jit(solution)/shard_map/normed_back/pallas_call | solution.py:424
  158.0 0.1 collective-permute-start.7
  158.1 0.8 copy.25.refs_8_
  159.0 1.8 copy.28.refs_11_
  160.7 1.9 copy.23.refs_6_
  162.6 1.8 copy.24.refs_7_
  164.4 1.9 copy.26.refs_9_
  166.3 1.8 copy.27.refs_10_
  168.1 17.1 %pair_gradient.5 = bf16[1536,1792]{1,0:T(8,128)(2,1)} custom-call(s32[1]{0:T(128)} %bitcast.core, bf16[1024,1536]{1,0:T(8,128)(2,1)} %fusion.6.a, bf16[1024,1536]{1,0:T(8,128)(2,1)} %collective-permute-done.3.a_other, bf16[1024,3584]{1,0:T(8,128)(2,1)} %get-tuple-element.54.d_gate.d, bf16[1024,3584]{1,0:T(8,128)(2,1)} %collective-permute-done.4.d_other), custom_call_target="tpu_custom_call" | custom-call | flops 11274289152 | bytes 19136512 | tf_op jit(solution)/shard_map/pair_gradient/pallas_call | solution.py:333
  185.2 17.1 %pair_gradient.6 = bf16[1536,1792]{1,0:T(8,128)(2,1)} custom-call(s32[1]{0:T(128)} %bitcast.core, bf16[1024,1536]{1,0:T(8,128)(2,1)} %fusion.6.a, bf16[1024,1536]{1,0:T(8,128)(2,1)} %collective-permute-done.3.a_other, bf16[1024,3584]{1,0:T(8,128)(2,1)} %get-tuple-element.55.d_up.d, bf16[1024,3584]{1,0:T(8,128)(2,1)} %collective-permute-done.5.d_other), custom_call_target="tpu_custom_call" | custom-call | flops 11274289152 | bytes 19136512 | tf_op jit(solution)/shard_map/pair_gradient/pallas_call | solution.py:333
  202.3 16.5 %pair_gradient.7 = bf16[3584,768]{1,0:T(8,128)(2,1)} custom-call(s32[1]{0:T(128)} %bitcast.core, bf16[1024,3584]{1,0:T(8,128)(2,1)} %get-tuple-element.56.a, bf16[1024,3584]{1,0:T(8,128)(2,1)} %collective-permute-done.6.a_other, bf16[1024,1536]{1,0:T(8,128)(2,1)} %bitcast.3.back.d, bf16[1024,1536]{1,0:T(8,128)(2,1)} %collective-permute-done.d_other), custom_call_target="tpu_custom_call" | custom-call | flops 11274289152 | bytes 23330816 | tf_op jit(solution)/shard_map/pair_gradient/pallas_call | solution.py:333
  218.8 98.5 %summed_and_updated.2 = (f32[12,3584]{1,0:T(8,128)}, f32[12,3584]{1,0:T(8,128)}, f32[28,1536]{1,0:T(8,128)}, f32[12,3584]{1,0:T(8,128)}, f32[12,3584]{1,0:T(8,12...) custom-call(bf16[4,4,4,24,1792]{4,3,2,1,0:T(8,128)(2,1)} %bitcast.42, ...), custom_call_target="tpu_custom_call" | custom-call | flops 40000000000 | bytes 60000000 | tf_op jit(solution)/shard_map/summed_and_updated/pallas_call | solution.py:247
  317.3 0.0 all-gather.7.cloned.1.call-start
  317.3 17.1 %pair_gradient.8 = bf16[1536,1792]{1,0:T(8,128)(2,1)} custom-call(s32[1]{0:T(128)} %bitcast.core, bf16[1024,1536]{1,0:T(8,128)(2,1)} %fusion.4.a, bf16[1024,1536]{1,0:T(8,128)(2,1)} %collective-permute-done.1.a_other, bf16[1024,1792]{1,0:T(8,128)(2,1)} %get-tuple-element.62.d, bf16[1024,1792]{1,0:T(8,128)(2,1)} %get-tuple-element.63.d_other), custom_call_target="tpu_custom_call" | custom-call | flops 11274289152 | bytes 19136512 | tf_op jit(solution)/shard_map/pair_gradient/pallas_call | solution.py:333
  334.4 17.1 %pair_gradient.9 = bf16[1536,1792]{1,0:T(8,128)(2,1)} custom-call(s32[1]{0:T(128)} %bitcast.core, bf16[1024,1536]{1,0:T(8,128)(2,1)} %fusion.4.a, bf16[1024,1536]{1,0:T(8,128)(2,1)} %collective-permute-done.1.a_other, bf16[1024,1792]{1,0:T(8,128)(2,1)} %get-tuple-element.66.d, bf16[1024,1792]{1,0:T(8,128)(2,1)} %get-tuple-element.67.d_other), custom_call_target="tpu_custom_call" | custom-call | flops 11274289152 | bytes 19136512 | tf_op jit(solution)/shard_map/pair_gradient/pallas_call | solution.py:333
  351.6 121.2 %summed_and_updated.3 = (f32[12,3584]{1,0:T(8,128)}, f32[12,3584]{1,0:T(8,128)}, f32[28,1536]{1,0:T(8,128)}, f32[12,3584]{1,0:T(8,128)}, f32[12,3584]{1,0:T(8,12...) custom-call(bf16[4,4,4,24,1792]{4,3,2,1,0:T(8,128)(2,1)} %bitcast.58, bf16[4,4,4,24,1792]{4,3,2,1,0:T(8,128)(2,1)} %bitcast.59, ...), custom_call_target="tpu_custom_call" | custom-call | flops 40000000000 | bytes 60000000 | tf_op jit(solution)/shard_map/summed_and_updated/pallas_call | solution.py:247
  472.9 1.1 pad_maximum_fusion
  474.0 1.0 copy.35
  475.0 1.0 pad_maximum_fusion.4
  476.0 1.0 copy.37
  477.0 1.0 pad_maximum_fusion.5
  477.9 1.0 copy.40
  478.9 1.0 pad_maximum_fusion.1
  479.9 1.0 copy.36
  480.9 1.0 copy.38
  482.0 1.0 copy.39
  483.0 14.4 %place.10.refs_1_ = bf16[2,3584,1536]{2,1,0:T(8,128)(2,1)} custom-call(bf16[128,504,256]{2,1,0:T(8,128)(2,1)} %bitcast.39), custom_call_target="tpu_custom_call" | custom-call | flops 100000000 | bytes 22020096 | tf_op jit(solution)/shard_map/place/pallas_call | solution.py:460
  497.3 14.4 %place.8.refs_1_ = bf16[2,1536,3584]{2,1,0:T(8,128)(2,1)} custom-call(bf16[128,504,256]{2,1,0:T(8,128)(2,1)} %bitcast.40), custom_call_target="tpu_custom_call" | custom-call | flops 100000000 | bytes 22020096 | tf_op jit(solution)/shard_map/place/pallas_call | solution.py:460
  511.7 14.4 %place.6.refs_1_ = bf16[2,1536,3584]{2,1,0:T(8,128)(2,1)} custom-call(bf16[128,504,256]{2,1,0:T(8,128)(2,1)} %bitcast.41), custom_call_target="tpu_custom_call" | custom-call | flops 100000000 | bytes 22020096 | tf_op jit(solution)/shard_map/place/pallas_call | solution.py:460
  526.1 50.8 %all-gather.7.cloned.1.call-done = bf16[64512,256]{1,0:T(8,128)(2,1)} async-done(((bf16[504,256]{1,0:T(8,128)(2,1)}), bf16[64512,256]{1,0:T(8,128)(2,1)}) %all-gather.7.cloned.1.call-update) | async-done | bytes 33030160 | tf_op jit(solution)/shard_map/all_gather | solution.py:478
  576.9 14.4 %place.11 = bf16[2,3584,1536]{2,1,0:T(8,128)(2,1)} custom-call(bf16[128,504,256]{2,1,0:T(8,128)(2,1)} %bitcast.36, bf16[2,3584,1536]{2,1,0:T(8,128)(2,1)} %place.10.refs_1_), custom_call_target="tpu_custom_call", output_to_operand_aliasing={{}: (1, {})} | custom-call | flops 100000000 | bytes 22020096 | tf_op jit(solution)/shard_map/place/pallas_call | solution.py:460
  591.3 14.4 %place.7 = bf16[2,1536,3584]{2,1,0:T(8,128)(2,1)} custom-call(bf16[128,504,256]{2,1,0:T(8,128)(2,1)} %bitcast.37, bf16[2,1536,3584]{2,1,0:T(8,128)(2,1)} %place.6.refs_1_), custom_call_target="tpu_custom_call", output_to_operand_aliasing={{}: (1, {})} | custom-call | flops 100000000 | bytes 22020096 | tf_op jit(solution)/shard_map/place/pallas_call | solution.py:460
  605.7 14.4 %place.9 = bf16[2,1536,3584]{2,1,0:T(8,128)(2,1)} custom-call(bf16[128,504,256]{2,1,0:T(8,128)(2,1)} %bitcast.38, bf16[2,1536,3584]{2,1,0:T(8,128)(2,1)} %place.8.refs_1_), custom_call_target="tpu_custom_call", output_to_operand_aliasing={{}: (1, {})} | custom-call | flops 100000000 | bytes 22020096 | tf_op jit(solution)/shard_map/place/pallas_call | solution.py:460
  (39 shorter events, 0.2 us)
Async XLA Ops:
  7.2 465.7 %all-gather.5.cloned.1.call-start = ((), (), s32[]{:S(2)}) async-start(), calls=%async_computation | async-start | bytes 33288192 | tf_op jit(solution)/shard_map/all_gather | solution.py:478
  13.9 108.2 %collective-permute-start.1 = (bf16[1024,1536]{1,0:T(8,128)(2,1)}, bf16[1024,1536]{1,0:T(8,128)(2,1)}, u32[]{:S(2)}, u32[]{:S(2)}) collective-permute-start(bf16[1024,1536]{1,0:T(8,128)(2,1)} %fusion.4.a), channel_id=1, source_target_pairs={{0,1},{1,0},{2,3},{3,2},{4,5},{5,4},{6,7},{7,6},{8,9},{9,8},{10,11... | collective-permute-start | bytes 9437192 | tf_op jit(solution)/shard_map/ppermute | solution.py:482
  15.3 30.3 %copy-start = (bf16[1,1024,1536]{2,1,0:T(8,128)(2,1)S(1)}, bf16[1,1024,1536]{2,1,0:T(8,128)(2,1)}, u32[]{:S(2)}) copy-start(bf16[1,1024,1536]{2,1,0:T(8,128)(2,1)} %param.11) | copy-start | bytes 9437188
  15.3 106.8 %collective-permute-start = (bf16[1024,1536]{1,0:T(8,128)(2,1)}, bf16[1024,1536]{1,0:T(8,128)(2,1)}, u32[]{:S(2)}, u32[]{:S(2)}) collective-permute-start(bf16[1024,1536]{1,0:T(8,128)(2,1)} %bitcast.3.back.d), channel_id=1, source_target_pairs={{0,1},{1,0},{2,3},{3,2},{4,5},{5,4},{6,7},{7,6},{8,9},{9,8},{10,11... | collective-permute-start | bytes 9437192 | tf_op jit(solution)/shard_map/ppermute | solution.py:482
  45.0 77.1 %collective-permute-start.2 = (bf16[1024,3584]{1,0:T(8,128)(2,1)}, bf16[1024,3584]{1,0:T(8,128)(2,1)}, u32[]{:S(2)}, u32[]{:S(2)}) collective-permute-start(bf16[1024,3584]{1,0:T(8,128)(2,1)} %get-tuple-element.47.refs_12_), channel_id=1, source_target_pairs={{0,1},{1,0},{2,3},{3,2},{4,5},{5,4},{6,7},{7,6},{8,9},{9,8},{10,11... | collective-permute-start | bytes 22020104 | tf_op jit(solution)/shard_map/ppermute | solution.py:482
  62.0 1.7 copy-start.2
  95.5 26.8 %copy-start.1 = (bf16[1024,1536]{1,0:T(8,128)(2,1)S(1)}, bf16[1024,1536]{1,0:T(8,128)(2,1)}, u32[]{:S(2)}) copy-start(bf16[1024,1536]{1,0:T(8,128)(2,1)} %fusion.6.a) | copy-start | bytes 9437188
  121.6 46.5 %collective-permute-start.4 = (bf16[1024,3584]{1,0:T(8,128)(2,1)}, bf16[1024,3584]{1,0:T(8,128)(2,1)}, u32[]{:S(2)}, u32[]{:S(2)}) collective-permute-start(bf16[1024,3584]{1,0:T(8,128)(2,1)} %get-tuple-element.54.d_gate.d), channel_id=1, source_target_pairs={{0,1},{1,0},{2,3},{3,2},{4,5},{5,4},{6,7},{7,6},{8,9},{9,8},{10,11... | collective-permute-start | bytes 22020104 | tf_op jit(solution)/shard_map/ppermute | solution.py:482
  121.6 63.6 %collective-permute-start.5 = (bf16[1024,3584]{1,0:T(8,128)(2,1)}, bf16[1024,3584]{1,0:T(8,128)(2,1)}, u32[]{:S(2)}, u32[]{:S(2)}) collective-permute-start(bf16[1024,3584]{1,0:T(8,128)(2,1)} %get-tuple-element.55.d_up.d), channel_id=1, source_target_pairs={{0,1},{1,0},{2,3},{3,2},{4,5},{5,4},{6,7},{7,6},{8,9},{9,8},{10,11... | collective-permute-start | bytes 22020104 | tf_op jit(solution)/shard_map/ppermute | solution.py:482
  122.1 36.0 %copy-start.3 = (f32[2,28,1536]{2,0,1:T(2,128)S(1)}, f32[2,28,1536]{2,0,1:T(2,128)}, u32[]{:S(2)}) copy-start(f32[2,28,1536]{2,0,1:T(2,128)} %param.18) | copy-start | bytes 1032196
  122.1 80.2 %collective-permute-start.6 = (bf16[1024,3584]{1,0:T(8,128)(2,1)}, bf16[1024,3584]{1,0:T(8,128)(2,1)}, u32[]{:S(2)}, u32[]{:S(2)}) collective-permute-start(bf16[1024,3584]{1,0:T(8,128)(2,1)} %get-tuple-element.56.a), channel_id=1, source_target_pairs={{0,1},{1,0},{2,3},{3,2},{4,5},{5,4},{6,7},{7,6},{8,9},{9,8},{10,11... | collective-permute-start | bytes 22020104 | tf_op jit(solution)/shard_map/ppermute | solution.py:482
  122.3 45.8 %collective-permute-start.3 = (bf16[1024,1536]{1,0:T(8,128)(2,1)S(1)}, bf16[1024,1536]{1,0:T(8,128)(2,1)}, u32[]{:S(2)}, u32[]{:S(2)}) collective-permute-start(bf16[1024,1536]{1,0:T(8,128)(2,1)S(1)} %copy-done.1), channel_id=1, source_target_pairs={{0,1},{1,0},{2,3},{3,2},{4,5},{5,4},{6,7},{7,6},{8,9},{9,8},{10,11... | collective-permute-start | bytes 9437192 | tf_op jit(solution)/shard_map/ppermute | solution.py:482
  158.0 60.8 %collective-permute-start.7 = (bf16[1024,1536]{1,0:T(8,128)(2,1)}, bf16[1024,1536]{1,0:T(8,128)(2,1)}, u32[]{:S(2)}, u32[]{:S(2)}) collective-permute-start(bf16[1024,1536]{1,0:T(8,128)(2,1)} %normed_back.1.refs_14_), channel_id=1, source_target_pairs={{0,1},{1,0},{2,3},{3,2},{4,5},{5,4},{6,7},{7,6},{8,9},{9,8},{10,11... | collective-permute-start | bytes 9437192 | tf_op jit(solution)/shard_map/ppermute | solution.py:482
  317.3 259.6 %all-gather.7.cloned.1.call-start = ((), (), s32[]{:S(2)}) async-start(), calls=%async_computation.1 | async-start | bytes 33288192 | tf_op jit(solution)/shard_map/all_gather | solution.py:478
  351.5 121.4 %copy-start.7 = (f32[12,3584]{1,0:T(8,128)S(1)}, f32[12,3584]{1,0:T(8,128)}, u32[]{:S(2)}) copy-start(f32[12,3584]{1,0:T(8,128)} %get-tuple-element.74) | copy-start | bytes 516100
  351.5 123.5 %copy-start.11 = (f32[28,1536]{1,0:T(8,128)S(1)}, f32[28,1536]{1,0:T(8,128)}, u32[]{:S(2)}) copy-start(f32[28,1536]{1,0:T(8,128)} %get-tuple-element.78) | copy-start | bytes 516100
  351.5 125.4 %copy-start.10 = (f32[28,1536]{1,0:T(8,128)S(1)}, f32[28,1536]{1,0:T(8,128)}, u32[]{:S(2)}) copy-start(f32[28,1536]{1,0:T(8,128)} %get-tuple-element.84) | copy-start | bytes 516100
  351.5 127.4 %copy-start.6 = (f32[12,3584]{1,0:T(8,128)S(1)}, f32[12,3584]{1,0:T(8,128)}, u32[]{:S(2)}) copy-start(f32[12,3584]{1,0:T(8,128)} %get-tuple-element.76) | copy-start | bytes 516100
  472.8 8.1 %copy-start.5 = (f32[12,3584]{1,0:T(8,128)S(1)}, f32[12,3584]{1,0:T(8,128)}, u32[]{:S(2)}) copy-start(f32[12,3584]{1,0:T(8,128)} %get-tuple-element.80) | copy-start | bytes 516100
  472.8 8.1 %copy-start.9 = (f32[12,3584]{1,0:T(8,128)S(1)}, f32[12,3584]{1,0:T(8,128)}, u32[]{:S(2)}) copy-start(f32[12,3584]{1,0:T(8,128)} %get-tuple-element.79) | copy-start | bytes 516100
  472.8 9.1 %copy-start.4 = (f32[12,3584]{1,0:T(8,128)S(1)}, f32[12,3584]{1,0:T(8,128)}, u32[]{:S(2)}) copy-start(f32[12,3584]{1,0:T(8,128)} %get-tuple-element.82) | copy-start | bytes 516100
  472.8 9.1 %copy-start.8 = (f32[12,3584]{1,0:T(8,128)S(1)}, f32[12,3584]{1,0:T(8,128)}, u32[]{:S(2)}) copy-start(f32[12,3584]{1,0:T(8,128)} %get-tuple-element.81) | copy-start | bytes 516100
Sparse Core Ops, SparseCore 0:
  317.4 146.6 all-gather.4
  473.0 103.8 all-gather.6

commit v5 on v4

--- a/solution.py
+++ b/solution.py
@@ -391,20 +391,32 @@
     d_gate[...] = (d_act * u * (s * (1 + g * (1 - s)))).astype(d_gate.dtype)
 
 
-def gated_back(back, w_down, gate, up, layer, bn=512):
-    tokens, d = back.shape
-    ff = gate.shape[1]
-    wide = pl.BlockSpec((tokens, bn), lambda j: (0, j))
+def turned_kernel(a, back, w_gate, w_up, w_down, act, d_gate, d_up):
+    g, u = dot(a[...], w_gate[...]), dot(a[...], w_up[...])
+    d_act = dot(back[...], w_down[...], (1, 1)).astype(BF16).astype(F32)
+    s = jax.nn.sigmoid(g)
+    gs = g * s
+    act[...] = (gs * u).astype(act.dtype)
+    d_up[...] = (d_act * gs).astype(d_up.dtype)
+    d_gate[...] = (d_act * u * (s * (1 + g * (1 - s)))).astype(d_gate.dtype)
+
+
+def turned(a, back, w_gate, w_up, w_down, layer, bn=512):
+    tokens, d = a.shape
+    ff = w_gate.shape[2]
+    rows = pl.BlockSpec((tokens, d), lambda j: (0, 0))
+    weight = pl.BlockSpec((None, d, bn), lambda j: (layer, 0, j))
+    out = pl.BlockSpec((tokens, bn), lambda j: (0, j))
     return local_call(
-        gated_back_kernel,
-        "gated_back",
-        2 * tokens * d * ff,
-        2 * d * ff + 12 * tokens * ff,
-        out_shape=[jax.ShapeDtypeStruct((tokens, ff), BF16)] * 2,
+        turned_kernel,
+        "turned",
+        6 * tokens * d * ff,
+        6 * d * ff + 6 * tokens * ff,
+        out_shape=[jax.ShapeDtypeStruct((tokens, ff), BF16)] * 3,
         grid=(ff // bn,),
-        in_specs=[pl.BlockSpec((tokens, d), lambda j: (0, 0)), pl.BlockSpec((None, bn, d), lambda j: (layer, j, 0)), wide, wide],
-        out_specs=[wide] * 2,
-    )(back, w_down, gate, up)
+        in_specs=[rows, rows, weight, weight, pl.BlockSpec((None, bn, d), lambda j: (layer, j, 0))],
+        out_specs=[out] * 3,
+    )(a, back, w_gate, w_up, w_down)
 
 
 def normed_back_kernel(d_gate, d_up, w_gate, w_up, h, back, out):
@@ -433,40 +445,39 @@
     )(d_gate, d_up, w_gate, w_up, h, back)
 
 
-def place_kernel(rows, *refs):
-    blocks, out = refs[0], refs[-1]
-    parts = out.shape[2] // 2 // LANES
-
-    def one(chip, _):
-        for core in range(2):
-            for part in range(parts):
-                at = (core * parts + part) * LANES
-                out[0, pl.ds(chip * rows, rows), at : at + LANES] = blocks[chip * 2 + core, part * rows : (part + 1) * rows, :]
-        return 0
-
-    lax.fori_loop(0, out.shape[1] // rows, one, 0)
-
-
-def place(gathered, which, layer, shape, so_far, steps=16):
-    _, total, width = shape
-    rows = total // 64
-    chips = 64 // steps
-    size = gathered.shape[1] // 3
-    in_specs = [pl.BlockSpec((2 * chips, size, LANES), lambda p: (p, which, 0))]
-    args = [gathered]
+def place_kernel(*refs):
+    blocks, outs = refs[:3], refs[-3:]
+    for block, out in zip(blocks, outs):
+        rows = block.shape[1] * LANES * 2 // out.shape[2]
+        parts = out.shape[2] // 2 // LANES
+
+        def one(chip, _):
+            for core in range(2):
+                for part in range(parts):
+                    at = (core * parts + part) * LANES
+                    out[0, pl.ds(chip * rows, rows), at : at + LANES] = block[chip * 2 + core, part * rows : (part + 1) * rows, :]
+            return 0
+
+        lax.fori_loop(0, out.shape[1] // rows, one, 0)
+
+
+def place(gathered, layer, shapes, so_far, steps=4):
+    devices, rows, _ = gathered.shape
+    in_specs = [pl.BlockSpec((devices // steps, rows // 3, LANES), lambda p, k=k: (p, k, 0)) for k in range(3)]
+    args = [gathered] * 3
     if so_far is not None:
-        in_specs.append(pl.BlockSpec(memory_space=pl.ANY))
-        args.append(so_far)
+        in_specs += [pl.BlockSpec(memory_space=pl.ANY)] * 3
+        args += so_far
     return local_call(
-        functools.partial(place_kernel, rows),
+        place_kernel,
         "place",
-        100_000_000,
-        4 * total * width,
-        out_shape=jax.ShapeDtypeStruct(shape, BF16),
+        300_000_000,
+        4 * gathered.size,
+        out_shape=[jax.ShapeDtypeStruct(shape, BF16) for shape in shapes],
         grid=(steps,),
         in_specs=in_specs,
-        out_specs=pl.BlockSpec((1, rows * chips, width), lambda p: (layer, p, 0)),
-        input_output_aliases={} if so_far is None else {1: 0},
+        out_specs=[pl.BlockSpec((1, shape[1] // steps, shape[2]), lambda p: (layer, p, 0)) for shape in shapes],
+        input_output_aliases={} if so_far is None else {3: 0, 4: 1, 5: 2},
     )(*args)
 
 
@@ -507,47 +518,45 @@
     for n in range(layers):
         a = (h.astype(F32) * scale_of(h)).astype(BF16)
         a_other = swap(a)
+        if n == last:
+            break
         gate, up, act = gated(a, wg, wu, n)
-        if n > 0:
-            act, back_other, kept[n - 1][2], kept[n - 1][6] = tied(act, back_other, kept[n - 1][2], kept[n - 1][6])
-        kept.append([h, a, a_other, gate, up, act, swap(act)])
-        if n < last:
-            h = h + dot(act, wd[n]).astype(BF16)
+        kept.append((a, a_other, gate, up, act, swap(act)))
+        h = h + dot(act, wd[n]).astype(BF16)
 
     new = [[None] * layers for _ in range(9)]
-    placed = [None] * 3
     gathered = [None] * layers
     cut = lambda gs: [g.reshape(N, N, N, -1, g.shape[1]) for g in gs]
     for n in reversed(range(layers)):
-        h, a, a_other, gate, up, act, act_other = kept[n]
         if n == last:
-            d_gate, d_up = gated_back(back, wd, gate, up, n)
-            d_up_other, d_gate_other = swap(d_up), swap(d_gate)
+            act, d_gate, d_up = turned(a, back, wg, wu, wd, n)
+            a0, a0_other, gate0, up0, act0, act0_other = kept[0]
+            d_gate, d_up, act, a_other, back_other, a0_other, act0_other = tied(d_gate, d_up, act, a_other, back_other, a0_other, act0_other)
+            d_gate_other, d_up_other, act_other = swap(d_gate), swap(d_up), swap(act)
             below = normed_back(d_gate, d_up, wg, wu, h, back, n)
             d_gate, d_up, below = tied(d_gate, d_up, below)
             below_other = swap(below)
             by_gate = pair_gradient(which, a, a_other, d_gate, d_gate_other, 512)
             by_up = pair_gradient(which, a, a_other, d_up, d_up_other, 512)
             by_down = pair_gradient(which, act, act_other, back, back_other, 896)
-            _, _, _, gate0, up0, act0, act0_other = kept[0]
             work = LayerBelow(*back.shape, gate0.shape[1])
             *made, pending, by_down0, d_gate, d_up, _, _, d_gate_other, d_up_other = summed_and_updated(
                 n, cut((by_gate, by_up, by_down)), weights, moments, work, (act0, act0_other, below, below_other, wd, gate0, up0)
             )
         else:
-            by_gate = pair_gradient(which, a, a_other, d_gate, d_gate_other, 512, True)
+            by_gate = pair_gradient(which, a0, a0_other, d_gate, d_gate_other, 512, True)
             d_up, pending = tied(d_up, pending)
             gathered[n + 1] = gather(pending)
-            by_up = pair_gradient(which, a, a_other, d_up, d_up_other, 512, True)
+            by_up = pair_gradient(which, a0, a0_other, d_up, d_up_other, 512, True)
             *made, pending = summed_and_updated(n, cut((by_gate, by_up, by_down0)), weights, moments)
             pending, *gathered[1:] = tied(pending, *gathered[1:])
             gathered[0] = gather(pending)
         for k in range(6):
             new[3 + k][n] = made[k]
 
+    placed = None
     for n in reversed(range(layers)):
-        for k in range(3):
-            placed[k] = place(gathered[n], k, n, weights[k].shape, placed[k])
+        placed = place(gathered[n], n, [w.shape for w in weights], placed)
     return (*placed, *(jnp.stack(new[i]) for i in range(3, 9)))
 
 

time: 639 us -> 601 us (0.941)
  Pallas kernels: 511 us -> 454 us
  waiting for transfers between devices: 50.9 us -> 72.8 us
    pallas_call x2 -> x1, Pallas kernels: 59.2 us -> 29.7 us  [gated(): local_call(gated_kernel, 'gated', 4 * tokens * d * ff, 4 * d * ff + 10 *...]
    pallas_call x7 -> x3, Pallas kernels: 112 us -> 85.4 us  [the longest x1 42.9 us: turned(): local_call(turned_kernel, 'turned', 6 * tokens * d * ff, 6 * d * ff + 6 *...]
    all_gather x2, waiting for transfers between devices: 50.9 us -> 72.7 us  [gather(): return lax.all_gather(blocks, ALL, axis=0, tiled=False)]
    unnamed x36 -> x38, local copies, waits for them, and re-layouts: 17.7 us -> 18.2 us
  transfers between devices with their start and end apart: 10 -> 10, of which waited for: 1 -> 1; matrix products, arithmetic and copies ran while one was open for 6% -> 6% of each run, Pallas kernels for 59% -> 52%
where the time goes in v5:
time: 601 us; the launch traced here: 591 us
  Pallas kernels  454 us (76%)
  waiting for transfers between devices  72.8 us (12%)
  local copies, waits for them, and re-layouts  18.2 us (3%)
  matrix products  16.4 us (3%)
  between operations  14.4 us (2%)
  other arithmetic  11.3 us (2%)
    pallas_call x2, Pallas kernels, summed_and_updated(): pl.pallas_call(functools.partial(scatter_kernel, layer, work), name='summ...  220 us
    pallas_call x5, Pallas kernels, pair_gradient(): pl.pallas_call(grad_kernel, name='pair_gradient', out_shape=jax.ShapeDtyp...  84.9 us
    all_gather x2, waiting for transfers between devices, gather(): return lax.all_gather(blocks, ALL, axis=0, tiled=False)  72.7 us
    pallas_call x1, Pallas kernels, turned(): local_call(turned_kernel, 'turned', 6 * tokens * d * ff, 6 * d * ff + 6 *...  42.9 us
    pallas_call x2, Pallas kernels, place(): local_call(place_kernel, 'place', 300000000, 4 * gathered.size, out_shape...  42.5 us
    pallas_call x1, Pallas kernels, normed_back(): local_call(normed_back_kernel, 'normed_back', 4 * tokens * d * ff, 4 * d...  34.8 us
    pallas_call x1, Pallas kernels, gated(): local_call(gated_kernel, 'gated', 4 * tokens * d * ff, 4 * d * ff + 10 *...  29.7 us
    unnamed x38, local copies, waits for them, and re-layouts  18.2 us
  transfers between devices with their start and end apart: 10, of which 1 were waited for; matrix products, arithmetic and copies ran while one was open for 6% of the time, Pallas kernels for 52%

profile of v5, /device:TPU:1, one launch (start us, length us, event | category | flops | bytes accessed | tf_op | source)
XLA Modules:
  0.0 590.9 jit_solution(13757997104244854112)
XLA Ops:
  7.2 0.0 all-gather.5.cloned.1.call-start
  7.2 2.6 fusion.3
  9.8 4.1 fusion.4.a
  13.9 29.7 %gated.1 = (f32[1024,3584]{1,0:T(8,128)}, f32[1024,3584]{1,0:T(8,128)}, bf16[1024,3584]{1,0:T(8,128)(2,1)}) custom-call(bf16[1024,1536]{1,0:T(8,128)(2,1)} %fusion.4.a, bf16[2,1536,3584]{2,1,0:T(8,128)(2,1)} %refs_3_.3, bf16[2,1536,3584]{2,1,0:T(8,128)(2,1)} %refs_4_.3), custom_call_target="tpu_custom_call" | custom-call | flops 22548578304 | bytes 58720256 | tf_op jit(solution)/shard_map/gated/pallas_call | solution.py:374
  43.6 1.3 collective-permute-start.3
  44.9 0.5 collective-permute-start.1
  45.4 16.4 %fusion.5 = (f32[1024]{0:T(1024)S(1)}, bf16[1024,1536]{1,0:T(8,128)(2,1)S(1)}) fusion(bf16[1024,3584]{1,0:T(8,128)(2,1)} %get-tuple-element.54.refs_12_, bf16[2,3584,1536]{2,1,0:T(8,128)(2,1)} %refs_5_.3, bf16[1,1024,1536]{2,1,0:T(8,128)(2,1)S(1)} %copy-done), kind=kOutput, calls=%fused_computation.9 | convolution fusion | flops 11282152448 | bytes 24645632 | tf_op jit(solution)/shard_map/dot_general | solution.py:349
  61.9 1.7 copy-done.2
  63.6 0.6 fusion.6.a
  64.2 0.0 copy-start.4
  64.2 0.1 collective-permute-start
  64.3 1.5 copy-done.1
  65.8 42.9 %turned.1 = (bf16[1024,3584]{1,0:T(8,128)(2,1)}, bf16[1024,3584]{1,0:T(8,128)(2,1)}, bf16[1024,3584]{1,0:T(8,128)(2,1)}) custom-call(bf16[1024,1536]{1,0:T(8,128)(2,1)} %copy-done.1, bf16[1024,1536]{1,0:T(8,128)(2,1)} %bitcast.59, bf16[2,1536,3584]{2,1,0:T(8,128)(2,1)} %refs_3_.3, bf16[2,1536,3584]{2,1,0:T(8,128)(2,1)} %refs_4_.3, bf16[2,3584,1536]{2,1,0:T(8,128)(2,1)} %refs_5_.3), custom_call_target="tpu_custom_call" | custom-call | flops 33822867456 | bytes 55050240 | tf_op jit(solution)/shard_map/turned/pallas_call | solution.py:410
  108.7 0.1 collective-permute-start.6
  108.8 0.5 collective-permute-start.4
  109.3 0.3 collective-permute-start.5
  109.7 0.8 copy.25.refs_8_
  110.5 0.8 copy.28.refs_11_
  111.3 1.8 copy.23.refs_6_
  113.1 1.8 copy.24.refs_7_
  114.9 1.8 copy.26.refs_9_
  116.8 1.8 copy.27.refs_10_
  118.6 34.8 %normed_back.1.refs_14_ = bf16[1024,1536]{1,0:T(8,128)(2,1)} custom-call(bf16[1024,3584]{1,0:T(8,128)(2,1)} %get-tuple-element.62.d_gate.d, bf16[1024,3584]{1,0:T(8,128)(2,1)} %get-tuple-element.63.d_up.d, bf16[2,1536,3584]{2,1,0:T(8,128)(2,1)} %refs_3_.3, bf16[2,1536,3584]{2,1,0:T(8,128)(2,1)} %refs_4_.3, bf16[1024,1536]{1,0:T(8,128)(2,1)} %copy-done.2, ...), custom_call_target="tpu_custom_call" | custom-call | flops 22548578304 | bytes 36700160 | tf_op jit(solution)/shard_map/normed_back/pallas_call | solution.py:436
  153.5 0.4 collective-permute-start.7
  153.9 16.4 %pair_gradient.7 = bf16[3584,768]{1,0:T(8,128)(2,1)} custom-call(s32[1]{0:T(128)} %bitcast.core, bf16[1024,3584]{1,0:T(8,128)(2,1)} %get-tuple-element.64.a, bf16[1024,3584]{1,0:T(8,128)(2,1)} %collective-permute-done.6.a_other, bf16[1024,1536]{1,0:T(8,128)(2,1)} %bitcast.61, bf16[1024,1536]{1,0:T(8,128)(2,1)} %collective-permute-done.1.d_other), custom_call_target="tpu_custom_call" | custom-call | flops 11274289152 | bytes 23330816 | tf_op jit(solution)/shard_map/pair_gradient/pallas_call | solution.py:333
  170.3 17.1 %pair_gradient.5 = bf16[1536,1792]{1,0:T(8,128)(2,1)} custom-call(s32[1]{0:T(128)} %bitcast.core, bf16[1024,1536]{1,0:T(8,128)(2,1)} %copy-done.1, bf16[1024,1536]{1,0:T(8,128)(2,1)} %collective-permute-done.a_other, bf16[1024,3584]{1,0:T(8,128)(2,1)} %get-tuple-element.62.d_gate.d, bf16[1024,3584]{1,0:T(8,128)(2,1)} %collective-permute-done.4.d_other), custom_call_target="tpu_custom_call" | custom-call | flops 11274289152 | bytes 19136512 | tf_op jit(solution)/shard_map/pair_gradient/pallas_call | solution.py:333
  187.4 17.2 %pair_gradient.6 = bf16[1536,1792]{1,0:T(8,128)(2,1)} custom-call(s32[1]{0:T(128)} %bitcast.core, bf16[1024,1536]{1,0:T(8,128)(2,1)} %copy-done.1, bf16[1024,1536]{1,0:T(8,128)(2,1)} %collective-permute-done.a_other, bf16[1024,3584]{1,0:T(8,128)(2,1)} %get-tuple-element.63.d_up.d, bf16[1024,3584]{1,0:T(8,128)(2,1)} %collective-permute-done.5.d_other), custom_call_target="tpu_custom_call" | custom-call | flops 11274289152 | bytes 19136512 | tf_op jit(solution)/shard_map/pair_gradient/pallas_call | solution.py:333
  204.6 98.5 %summed_and_updated.2 = (f32[12,3584]{1,0:T(8,128)}, f32[12,3584]{1,0:T(8,128)}, f32[28,1536]{1,0:T(8,128)}, f32[12,3584]{1,0:T(8,128)}, f32[12,3584]{1,0:T(8,12...) custom-call(bf16[4,4,4,24,1792]{4,3,2,1,0:T(8,128)(2,1)} %bitcast.43, ...), custom_call_target="tpu_custom_call" | custom-call | flops 40000000000 | bytes 60000000 | tf_op jit(solution)/shard_map/summed_and_updated/pallas_call | solution.py:247
  303.1 0.0 all-gather.5.cloned.1.call-update
  303.1 0.0 all-gather.7.cloned.1.call-start
  303.1 17.1 %pair_gradient.8 = bf16[1536,1792]{1,0:T(8,128)(2,1)} custom-call(s32[1]{0:T(128)} %bitcast.core, bf16[1024,1536]{1,0:T(8,128)(2,1)} %fusion.4.a, bf16[1024,1536]{1,0:T(8,128)(2,1)} %collective-permute-done.2.a_other, bf16[1024,1792]{1,0:T(8,128)(2,1)} %get-tuple-element.70.d, bf16[1024,1792]{1,0:T(8,128)(2,1)} %get-tuple-element.71.d_other), custom_call_target="tpu_custom_call" | custom-call | flops 11274289152 | bytes 19136512 | tf_op jit(solution)/shard_map/pair_gradient/pallas_call | solution.py:333
  320.2 17.1 %pair_gradient.9 = bf16[1536,1792]{1,0:T(8,128)(2,1)} custom-call(s32[1]{0:T(128)} %bitcast.core, bf16[1024,1536]{1,0:T(8,128)(2,1)} %fusion.4.a, bf16[1024,1536]{1,0:T(8,128)(2,1)} %collective-permute-done.2.a_other, bf16[1024,1792]{1,0:T(8,128)(2,1)} %get-tuple-element.74.d, bf16[1024,1792]{1,0:T(8,128)(2,1)} %get-tuple-element.75.d_other), custom_call_target="tpu_custom_call" | custom-call | flops 11274289152 | bytes 19136512 | tf_op jit(solution)/shard_map/pair_gradient/pallas_call | solution.py:333
  337.4 121.1 %summed_and_updated.3 = (f32[12,3584]{1,0:T(8,128)}, f32[12,3584]{1,0:T(8,128)}, f32[28,1536]{1,0:T(8,128)}, f32[12,3584]{1,0:T(8,128)}, f32[12,3584]{1,0:T(8,12...) custom-call(bf16[4,4,4,24,1792]{4,3,2,1,0:T(8,128)(2,1)} %bitcast.62, bf16[4,4,4,24,1792]{4,3,2,1,0:T(8,128)(2,1)} %bitcast.63, ...), custom_call_target="tpu_custom_call" | custom-call | flops 40000000000 | bytes 60000000 | tf_op jit(solution)/shard_map/summed_and_updated/pallas_call | solution.py:247
  458.5 0.0 all-gather.5.cloned.1.call-done
  458.5 0.0 all-gather.7.cloned.1.call-update
  458.6 1.1 pad_maximum_fusion
  459.7 1.0 copy.35
  460.7 1.0 pad_maximum_fusion.4
  461.6 1.0 copy.37
  462.6 1.0 pad_maximum_fusion.5
  463.6 1.0 copy.40
  464.6 1.0 pad_maximum_fusion.1
  465.6 1.0 copy.36
  466.6 1.0 copy.38
  467.6 1.0 copy.39
  468.6 21.3 %place.2 = (bf16[2,1536,3584]{2,1,0:T(8,128)(2,1)}, bf16[2,1536,3584]{2,1,0:T(8,128)(2,1)}, bf16[2,3584,1536]{2,1,0:T(8,128)(2,1)}) custom-call(bf16[128,504,256]{2,1,0:T(8,128)(2,1)} %bitcast.36, bf16[128,504,256]{2,1,0:T(8,128)(2,1)} %bitcast.37, bf16[128,504,256]{2,1,0:T(8,128)(2,1)} %bitcast.38), custom_call_target="tpu_custom_call" | custom-call | flops 300000000 | bytes 66060288 | tf_op jit(solution)/shard_map/place/pallas_call | solution.py:471
  489.9 72.7 %all-gather.7.cloned.1.call-done = bf16[64512,256]{1,0:T(8,128)(2,1)} async-done(((bf16[504,256]{1,0:T(8,128)(2,1)}), bf16[64512,256]{1,0:T(8,128)(2,1)}) %all-gather.7.cloned.1.call-update) | async-done | bytes 33030160 | tf_op jit(solution)/shard_map/all_gather | solution.py:489
  562.6 21.3 %place.3 = (bf16[2,1536,3584]{2,1,0:T(8,128)(2,1)}, bf16[2,1536,3584]{2,1,0:T(8,128)(2,1)}, bf16[2,3584,1536]{2,1,0:T(8,128)(2,1)}) custom-call(bf16[128,504,256]{2,1,0:T(8,128)(2,1)} %bitcast.39, bf16[128,504,256]{2,1,0:T(8,128)(2,1)} %bitcast.40, bf16[128,504,256]{2,1,0:T(8,128)(2,1)} %bitcast.41, ...), custom_call_target="tpu_custom_call", output_to_operand_aliasing={{0}: (3, {}), {1}: (4, {}), {2}: (5, {})} | custom-call | flops 300000000 | bytes 66060288 | tf_op jit(solution)/shard_map/place/pallas_call | solution.py:471
  (36 shorter events, 0.2 us)
Async XLA Ops:
  7.2 451.3 %all-gather.5.cloned.1.call-start = ((), (), s32[]{:S(2)}) async-start(), calls=%async_computation | async-start | bytes 33288192 | tf_op jit(solution)/shard_map/all_gather | solution.py:489
  13.9 31.5 %copy-start = (bf16[1,1024,1536]{2,1,0:T(8,128)(2,1)S(1)}, bf16[1,1024,1536]{2,1,0:T(8,128)(2,1)}, u32[]{:S(2)}) copy-start(bf16[1,1024,1536]{2,1,0:T(8,128)(2,1)} %param.11) | copy-start | bytes 9437188
  43.6 65.2 %collective-permute-start.3 = (bf16[1024,3584]{1,0:T(8,128)(2,1)}, bf16[1024,3584]{1,0:T(8,128)(2,1)}, u32[]{:S(2)}, u32[]{:S(2)}) collective-permute-start(bf16[1024,3584]{1,0:T(8,128)(2,1)} %get-tuple-element.54.refs_12_), channel_id=1, source_target_pairs={{0,1},{1,0},{2,3},{3,2},{4,5},{5,4},{6,7},{7,6},{8,9},{9,8},{10,11... | collective-permute-start | bytes 22020104 | tf_op jit(solution)/shard_map/ppermute | solution.py:493
  44.9 63.8 %collective-permute-start.2 = (bf16[1024,1536]{1,0:T(8,128)(2,1)}, bf16[1024,1536]{1,0:T(8,128)(2,1)}, u32[]{:S(2)}, u32[]{:S(2)}) collective-permute-start(bf16[1024,1536]{1,0:T(8,128)(2,1)} %fusion.4.a), channel_id=1, source_target_pairs={{0,1},{1,0},{2,3},{3,2},{4,5},{5,4},{6,7},{7,6},{8,9},{9,8},{10,11... | collective-permute-start | bytes 9437192 | tf_op jit(solution)/shard_map/ppermute | solution.py:493
  44.9 63.8 %collective-permute-start.1 = (bf16[1024,1536]{1,0:T(8,128)(2,1)}, bf16[1024,1536]{1,0:T(8,128)(2,1)}, u32[]{:S(2)}, u32[]{:S(2)}) collective-permute-start(bf16[1024,1536]{1,0:T(8,128)(2,1)} %bitcast.58), channel_id=1, source_target_pairs={{0,1},{1,0},{2,3},{3,2},{4,5},{5,4},{6,7},{7,6},{8,9},{9,8},{10,11... | collective-permute-start | bytes 9437192 | tf_op jit(solution)/shard_map/ppermute | solution.py:493
  61.9 1.7 copy-start.2
  64.1 1.7 copy-start.1
  64.2 45.5 %copy-start.3 = (f32[2,28,1536]{2,0,1:T(2,128)S(1)}, f32[2,28,1536]{2,0,1:T(2,128)}, u32[]{:S(2)}) copy-start(f32[2,28,1536]{2,0,1:T(2,128)} %param.18) | copy-start | bytes 1032196
  64.2 46.3 %copy-start.4 = (f32[2,28,1536]{2,0,1:T(2,128)S(1)}, f32[2,28,1536]{2,0,1:T(2,128)}, u32[]{:S(2)}) copy-start(f32[2,28,1536]{2,0,1:T(2,128)} %param.21) | copy-start | bytes 1032196
  64.2 44.5 %collective-permute-start = (bf16[1024,1536]{1,0:T(8,128)(2,1)S(1)}, bf16[1024,1536]{1,0:T(8,128)(2,1)}, u32[]{:S(2)}, u32[]{:S(2)}) collective-permute-start(bf16[1024,1536]{1,0:T(8,128)(2,1)S(1)} %fusion.6.a), channel_id=1, source_target_pairs={{0,1},{1,0},{2,3},{3,2},{4,5},{5,4},{6,7},{7,6},{8,9},{9,8},{10,11... | collective-permute-start | bytes 9437192 | tf_op jit(solution)/shard_map/ppermute | solution.py:493
  108.7 45.2 %collective-permute-start.6 = (bf16[1024,3584]{1,0:T(8,128)(2,1)}, bf16[1024,3584]{1,0:T(8,128)(2,1)}, u32[]{:S(2)}, u32[]{:S(2)}) collective-permute-start(bf16[1024,3584]{1,0:T(8,128)(2,1)} %get-tuple-element.64.a), channel_id=1, source_target_pairs={{0,1},{1,0},{2,3},{3,2},{4,5},{5,4},{6,7},{7,6},{8,9},{9,8},{10,11... | collective-permute-start | bytes 22020104 | tf_op jit(solution)/shard_map/ppermute | solution.py:493
  108.8 61.5 %collective-permute-start.4 = (bf16[1024,3584]{1,0:T(8,128)(2,1)}, bf16[1024,3584]{1,0:T(8,128)(2,1)}, u32[]{:S(2)}, u32[]{:S(2)}) collective-permute-start(bf16[1024,3584]{1,0:T(8,128)(2,1)} %get-tuple-element.62.d_gate.d), channel_id=1, source_target_pairs={{0,1},{1,0},{2,3},{3,2},{4,5},{5,4},{6,7},{7,6},{8,9},{9,8},{10,11... | collective-permute-start | bytes 22020104 | tf_op jit(solution)/shard_map/ppermute | solution.py:493
  109.3 78.1 %collective-permute-start.5 = (bf16[1024,3584]{1,0:T(8,128)(2,1)}, bf16[1024,3584]{1,0:T(8,128)(2,1)}, u32[]{:S(2)}, u32[]{:S(2)}) collective-permute-start(bf16[1024,3584]{1,0:T(8,128)(2,1)} %get-tuple-element.63.d_up.d), channel_id=1, source_target_pairs={{0,1},{1,0},{2,3},{3,2},{4,5},{5,4},{6,7},{7,6},{8,9},{9,8},{10,11... | collective-permute-start | bytes 22020104 | tf_op jit(solution)/shard_map/ppermute | solution.py:493
  153.5 51.1 %collective-permute-start.7 = (bf16[1024,1536]{1,0:T(8,128)(2,1)}, bf16[1024,1536]{1,0:T(8,128)(2,1)}, u32[]{:S(2)}, u32[]{:S(2)}) collective-permute-start(bf16[1024,1536]{1,0:T(8,128)(2,1)} %normed_back.1.refs_14_), channel_id=1, source_target_pairs={{0,1},{1,0},{2,3},{3,2},{4,5},{5,4},{6,7},{7,6},{8,9},{9,8},{10,11... | collective-permute-start | bytes 9437192 | tf_op jit(solution)/shard_map/ppermute | solution.py:493
  303.1 259.5 %all-gather.7.cloned.1.call-start = ((), (), s32[]{:S(2)}) async-start(), calls=%async_computation.1 | async-start | bytes 33288192 | tf_op jit(solution)/shard_map/all_gather | solution.py:489
  337.3 121.2 %copy-start.8 = (f32[12,3584]{1,0:T(8,128)S(1)}, f32[12,3584]{1,0:T(8,128)}, u32[]{:S(2)}) copy-start(f32[12,3584]{1,0:T(8,128)} %get-tuple-element.88) | copy-start | bytes 516100
  337.3 123.3 %copy-start.12 = (f32[28,1536]{1,0:T(8,128)S(1)}, f32[28,1536]{1,0:T(8,128)}, u32[]{:S(2)}) copy-start(f32[28,1536]{1,0:T(8,128)} %get-tuple-element.92) | copy-start | bytes 516100
  337.3 125.3 %copy-start.11 = (f32[28,1536]{1,0:T(8,128)S(1)}, f32[28,1536]{1,0:T(8,128)}, u32[]{:S(2)}) copy-start(f32[28,1536]{1,0:T(8,128)} %get-tuple-element.98) | copy-start | bytes 516100
  337.3 127.2 %copy-start.7 = (f32[12,3584]{1,0:T(8,128)S(1)}, f32[12,3584]{1,0:T(8,128)}, u32[]{:S(2)}) copy-start(f32[12,3584]{1,0:T(8,128)} %get-tuple-element.90) | copy-start | bytes 516100
  458.5 8.1 %copy-start.6 = (f32[12,3584]{1,0:T(8,128)S(1)}, f32[12,3584]{1,0:T(8,128)}, u32[]{:S(2)}) copy-start(f32[12,3584]{1,0:T(8,128)} %get-tuple-element.94) | copy-start | bytes 516100
  458.5 8.1 %copy-start.10 = (f32[12,3584]{1,0:T(8,128)S(1)}, f32[12,3584]{1,0:T(8,128)}, u32[]{:S(2)}) copy-start(f32[12,3584]{1,0:T(8,128)} %get-tuple-element.93) | copy-start | bytes 516100
  458.5 9.1 %copy-start.5 = (f32[12,3584]{1,0:T(8,128)S(1)}, f32[12,3584]{1,0:T(8,128)}, u32[]{:S(2)}) copy-start(f32[12,3584]{1,0:T(8,128)} %get-tuple-element.96) | copy-start | bytes 516100
  458.5 9.1 %copy-start.9 = (f32[12,3584]{1,0:T(8,128)S(1)}, f32[12,3584]{1,0:T(8,128)}, u32[]{:S(2)}) copy-start(f32[12,3584]{1,0:T(8,128)} %get-tuple-element.95) | copy-start | bytes 516100
Sparse Core Ops, SparseCore 0:
  303.2 146.5 all-gather.4
  458.7 103.8 all-gather.6

commit v6 on v5

--- a/solution.py
+++ b/solution.py
@@ -532,10 +532,10 @@
             act, d_gate, d_up = turned(a, back, wg, wu, wd, n)
             a0, a0_other, gate0, up0, act0, act0_other = kept[0]
             d_gate, d_up, act, a_other, back_other, a0_other, act0_other = tied(d_gate, d_up, act, a_other, back_other, a0_other, act0_other)
-            d_gate_other, d_up_other, act_other = swap(d_gate), swap(d_up), swap(act)
+            d_gate_other, d_up_other = swap(d_gate), swap(d_up)
             below = normed_back(d_gate, d_up, wg, wu, h, back, n)
-            d_gate, d_up, below = tied(d_gate, d_up, below)
-            below_other = swap(below)
+            d_gate, d_up, act, below, d_gate_other, d_up_other = tied(d_gate, d_up, act, below, d_gate_other, d_up_other)
+            below_other, act_other = swap(below), swap(act)
             by_gate = pair_gradient(which, a, a_other, d_gate, d_gate_other, 512)
             by_up = pair_gradient(which, a, a_other, d_up, d_up_other, 512)
             by_down = pair_gradient(which, act, act_other, back, back_other, 896)

time: 601 us -> 597 us (level)
    unnamed x38 -> x46, local copies, waits for them, and re-layouts: 18.2 us -> 14.3 us
  transfers between devices with their start and end apart: 10 -> 10, of which waited for: 1 -> 1; matrix products, arithmetic and copies ran while one was open for 6% -> 5% of each run, Pallas kernels for 52% -> 52%
where the time goes in v6:
time: 597 us; the launch traced here: 587 us
  Pallas kernels  454 us (76%)
  waiting for transfers between devices  72.7 us (12%)
  matrix products  16.4 us (3%)
  between operations  14.5 us (2%)
  local copies, waits for them, and re-layouts  14.3 us (2%)
  other arithmetic  11.3 us (2%)
    pallas_call x2, Pallas kernels, summed_and_updated(): pl.pallas_call(functools.partial(scatter_kernel, layer, work), name='summ...  220 us
    pallas_call x5, Pallas kernels, pair_gradient(): pl.pallas_call(grad_kernel, name='pair_gradient', out_shape=jax.ShapeDtyp...  84.9 us
    all_gather x2, waiting for transfers between devices, gather(): return lax.all_gather(blocks, ALL, axis=0, tiled=False)  72.7 us
    pallas_call x1, Pallas kernels, turned(): local_call(turned_kernel, 'turned', 6 * tokens * d * ff, 6 * d * ff + 6 *...  42.8 us
    pallas_call x2, Pallas kernels, place(): local_call(place_kernel, 'place', 300000000, 4 * gathered.size, out_shape...  42.5 us
    pallas_call x1, Pallas kernels, normed_back(): local_call(normed_back_kernel, 'normed_back', 4 * tokens * d * ff, 4 * d...  34.8 us
    pallas_call x1, Pallas kernels, gated(): local_call(gated_kernel, 'gated', 4 * tokens * d * ff, 4 * d * ff + 10 *...  29.6 us
    dot_general x1, matrix products, dot(): lax.dot_general(a, b, (((over[0],), (over[1],)), ((), ())), preferred_ele...  16.4 us
  transfers between devices with their start and end apart: 10, of which 1 were waited for; matrix products, arithmetic and copies ran while one was open for 5% of the time, Pallas kernels for 52%

profile of v6, /device:TPU:1, one launch (start us, length us, event | category | flops | bytes accessed | tf_op | source)
XLA Modules:
  0.0 587.1 jit_solution(11653982880885903810)
XLA Ops:
  7.2 0.0 all-gather.5.cloned.1.call-start
  7.2 2.6 fusion.3
  9.8 4.1 fusion.4.a
  13.9 29.6 %gated.1 = (f32[1024,3584]{1,0:T(8,128)}, f32[1024,3584]{1,0:T(8,128)}, bf16[1024,3584]{1,0:T(8,128)(2,1)}) custom-call(bf16[1024,1536]{1,0:T(8,128)(2,1)} %fusion.4.a, bf16[2,1536,3584]{2,1,0:T(8,128)(2,1)} %refs_3_.3, bf16[2,1536,3584]{2,1,0:T(8,128)(2,1)} %refs_4_.3), custom_call_target="tpu_custom_call" | custom-call | flops 22548578304 | bytes 58720256 | tf_op jit(solution)/shard_map/gated/pallas_call | solution.py:374
  43.6 1.4 collective-permute-start.3
  44.9 0.5 collective-permute-start.1
  45.4 16.4 %fusion.5 = (f32[1024]{0:T(1024)S(1)}, bf16[1024,1536]{1,0:T(8,128)(2,1)S(1)}) fusion(bf16[1024,3584]{1,0:T(8,128)(2,1)} %get-tuple-element.57.refs_12_, bf16[2,3584,1536]{2,1,0:T(8,128)(2,1)} %refs_5_.3, bf16[1,1024,1536]{2,1,0:T(8,128)(2,1)S(1)} %copy-done), kind=kOutput, calls=%fused_computation.9 | convolution fusion | flops 11282152448 | bytes 24645632 | tf_op jit(solution)/shard_map/dot_general | solution.py:349
  61.9 1.7 copy-done.2
  63.5 0.6 fusion.6.a
  64.1 0.1 collective-permute-start
  64.2 1.6 copy-done.1
  65.8 42.8 %turned.1 = (bf16[1024,3584]{1,0:T(8,128)(2,1)}, bf16[1024,3584]{1,0:T(8,128)(2,1)}, bf16[1024,3584]{1,0:T(8,128)(2,1)}) custom-call(bf16[1024,1536]{1,0:T(8,128)(2,1)} %copy-done.1, bf16[1024,1536]{1,0:T(8,128)(2,1)} %bitcast.59, bf16[2,1536,3584]{2,1,0:T(8,128)(2,1)} %refs_3_.3, bf16[2,1536,3584]{2,1,0:T(8,128)(2,1)} %refs_4_.3, bf16[2,3584,1536]{2,1,0:T(8,128)(2,1)} %refs_5_.3), custom_call_target="tpu_custom_call" | custom-call | flops 33822867456 | bytes 55050240 | tf_op jit(solution)/shard_map/turned/pallas_call | solution.py:410
  108.7 0.0 copy-start.5
  108.7 0.1 collective-permute-start.4
  108.8 0.7 collective-permute-start.5
  109.6 34.8 %normed_back.1.refs_14_ = bf16[1024,1536]{1,0:T(8,128)(2,1)} custom-call(bf16[1024,3584]{1,0:T(8,128)(2,1)} %get-tuple-element.66.d_gate.d, bf16[1024,3584]{1,0:T(8,128)(2,1)} %get-tuple-element.68.d_up.d, bf16[2,1536,3584]{2,1,0:T(8,128)(2,1)} %refs_3_.3, bf16[2,1536,3584]{2,1,0:T(8,128)(2,1)} %refs_4_.3, bf16[1024,1536]{1,0:T(8,128)(2,1)} %copy-done.2, ...), custom_call_target="tpu_custom_call" | custom-call | flops 22548578304 | bytes 36700160 | tf_op jit(solution)/shard_map/normed_back/pallas_call | solution.py:436
  144.4 0.2 collective-permute-start.6
  144.6 0.8 copy.25.refs_8_
  145.4 0.8 copy.28.refs_11_
  146.2 0.9 copy.23.refs_6_
  147.1 0.8 copy.24.refs_7_
  148.0 0.8 copy.26.refs_9_
  148.8 0.9 copy.27.refs_10_
  149.7 0.4 collective-permute-start.7
  150.0 17.1 %pair_gradient.5 = bf16[1536,1792]{1,0:T(8,128)(2,1)} custom-call(s32[1]{0:T(128)} %bitcast.core, bf16[1024,1536]{1,0:T(8,128)(2,1)} %copy-done.1, bf16[1024,1536]{1,0:T(8,128)(2,1)} %collective-permute-done.a_other, bf16[1024,3584]{1,0:T(8,128)(2,1)} %get-tuple-element.66.d_gate.d, bf16[1024,3584]{1,0:T(8,128)(2,1)} %collective-permute-done.4.d_other), custom_call_target="tpu_custom_call" | custom-call | flops 11274289152 | bytes 19136512 | tf_op jit(solution)/shard_map/pair_gradient/pallas_call | solution.py:333
  167.2 17.2 %pair_gradient.6 = bf16[1536,1792]{1,0:T(8,128)(2,1)} custom-call(s32[1]{0:T(128)} %bitcast.core, bf16[1024,1536]{1,0:T(8,128)(2,1)} %copy-done.1, bf16[1024,1536]{1,0:T(8,128)(2,1)} %collective-permute-done.a_other, bf16[1024,3584]{1,0:T(8,128)(2,1)} %get-tuple-element.68.d_up.d, bf16[1024,3584]{1,0:T(8,128)(2,1)} %collective-permute-done.5.d_other), custom_call_target="tpu_custom_call" | custom-call | flops 11274289152 | bytes 19136512 | tf_op jit(solution)/shard_map/pair_gradient/pallas_call | solution.py:333
  184.3 16.4 %pair_gradient.7 = bf16[3584,768]{1,0:T(8,128)(2,1)} custom-call(s32[1]{0:T(128)} %bitcast.core, bf16[1024,3584]{1,0:T(8,128)(2,1)} %get-tuple-element.70.a, bf16[1024,3584]{1,0:T(8,128)(2,1)} %collective-permute-done.6.a_other, bf16[1024,1536]{1,0:T(8,128)(2,1)} %bitcast.61, bf16[1024,1536]{1,0:T(8,128)(2,1)} %collective-permute-done.1.d_other), custom_call_target="tpu_custom_call" | custom-call | flops 11274289152 | bytes 23330816 | tf_op jit(solution)/shard_map/pair_gradient/pallas_call | solution.py:333
  200.7 98.3 %summed_and_updated.2 = (f32[12,3584]{1,0:T(8,128)}, f32[12,3584]{1,0:T(8,128)}, f32[28,1536]{1,0:T(8,128)}, f32[12,3584]{1,0:T(8,128)}, f32[12,3584]{1,0:T(8,12...) custom-call(bf16[4,4,4,24,1792]{4,3,2,1,0:T(8,128)(2,1)} %bitcast.42, ...), custom_call_target="tpu_custom_call" | custom-call | flops 40000000000 | bytes 60000000 | tf_op jit(solution)/shard_map/summed_and_updated/pallas_call | solution.py:247
  299.1 0.0 all-gather.5.cloned.1.call-update
  299.1 0.0 all-gather.7.cloned.1.call-start
  299.1 17.1 %pair_gradient.8 = bf16[1536,1792]{1,0:T(8,128)(2,1)} custom-call(s32[1]{0:T(128)} %bitcast.core, bf16[1024,1536]{1,0:T(8,128)(2,1)} %fusion.4.a, bf16[1024,1536]{1,0:T(8,128)(2,1)} %collective-permute-done.2.a_other, bf16[1024,1792]{1,0:T(8,128)(2,1)} %get-tuple-element.76.d, bf16[1024,1792]{1,0:T(8,128)(2,1)} %get-tuple-element.77.d_other), custom_call_target="tpu_custom_call" | custom-call | flops 11274289152 | bytes 19136512 | tf_op jit(solution)/shard_map/pair_gradient/pallas_call | solution.py:333
  316.2 17.1 %pair_gradient.9 = bf16[1536,1792]{1,0:T(8,128)(2,1)} custom-call(s32[1]{0:T(128)} %bitcast.core, bf16[1024,1536]{1,0:T(8,128)(2,1)} %fusion.4.a, bf16[1024,1536]{1,0:T(8,128)(2,1)} %collective-permute-done.2.a_other, bf16[1024,1792]{1,0:T(8,128)(2,1)} %get-tuple-element.80.d, bf16[1024,1792]{1,0:T(8,128)(2,1)} %get-tuple-element.81.d_other), custom_call_target="tpu_custom_call" | custom-call | flops 11274289152 | bytes 19136512 | tf_op jit(solution)/shard_map/pair_gradient/pallas_call | solution.py:333
  333.3 121.3 %summed_and_updated.3 = (f32[12,3584]{1,0:T(8,128)}, f32[12,3584]{1,0:T(8,128)}, f32[28,1536]{1,0:T(8,128)}, f32[12,3584]{1,0:T(8,128)}, f32[12,3584]{1,0:T(8,12...) custom-call(bf16[4,4,4,24,1792]{4,3,2,1,0:T(8,128)(2,1)} %bitcast.62, bf16[4,4,4,24,1792]{4,3,2,1,0:T(8,128)(2,1)} %bitcast.63, ...), custom_call_target="tpu_custom_call" | custom-call | flops 40000000000 | bytes 60000000 | tf_op jit(solution)/shard_map/summed_and_updated/pallas_call | solution.py:247
  454.7 0.0 all-gather.5.cloned.1.call-done
  454.8 0.0 all-gather.7.cloned.1.call-update
  454.8 1.1 pad_maximum_fusion
  455.9 1.0 copy.35
  456.9 1.0 pad_maximum_fusion.4
  457.9 1.0 copy.37
  458.9 1.0 pad_maximum_fusion.5
  459.8 1.0 copy.40
  460.8 1.0 pad_maximum_fusion.1
  461.8 1.0 copy.36
  462.8 1.0 copy.38
  463.9 1.0 copy.39
  464.9 21.3 %place.2 = (bf16[2,1536,3584]{2,1,0:T(8,128)(2,1)}, bf16[2,1536,3584]{2,1,0:T(8,128)(2,1)}, bf16[2,3584,1536]{2,1,0:T(8,128)(2,1)}) custom-call(bf16[128,504,256]{2,1,0:T(8,128)(2,1)} %bitcast.36, bf16[128,504,256]{2,1,0:T(8,128)(2,1)} %bitcast.37, bf16[128,504,256]{2,1,0:T(8,128)(2,1)} %bitcast.38), custom_call_target="tpu_custom_call" | custom-call | flops 300000000 | bytes 66060288 | tf_op jit(solution)/shard_map/place/pallas_call | solution.py:471
  486.1 72.7 %all-gather.7.cloned.1.call-done = bf16[64512,256]{1,0:T(8,128)(2,1)} async-done(((bf16[504,256]{1,0:T(8,128)(2,1)}), bf16[64512,256]{1,0:T(8,128)(2,1)}) %all-gather.7.cloned.1.call-update) | async-done | bytes 33030160 | tf_op jit(solution)/shard_map/all_gather | solution.py:489
  558.8 21.3 %place.3 = (bf16[2,1536,3584]{2,1,0:T(8,128)(2,1)}, bf16[2,1536,3584]{2,1,0:T(8,128)(2,1)}, bf16[2,3584,1536]{2,1,0:T(8,128)(2,1)}) custom-call(bf16[128,504,256]{2,1,0:T(8,128)(2,1)} %bitcast.39, bf16[128,504,256]{2,1,0:T(8,128)(2,1)} %bitcast.40, bf16[128,504,256]{2,1,0:T(8,128)(2,1)} %bitcast.41, ...), custom_call_target="tpu_custom_call", output_to_operand_aliasing={{0}: (3, {}), {1}: (4, {}), {2}: (5, {})} | custom-call | flops 300000000 | bytes 66060288 | tf_op jit(solution)/shard_map/place/pallas_call | solution.py:471
  (44 shorter events, 0.2 us)
Async XLA Ops:
  7.2 447.6 %all-gather.5.cloned.1.call-start = ((), (), s32[]{:S(2)}) async-start(), calls=%async_computation | async-start | bytes 33288192 | tf_op jit(solution)/shard_map/all_gather | solution.py:489
  13.9 31.5 %copy-start = (bf16[1,1024,1536]{2,1,0:T(8,128)(2,1)S(1)}, bf16[1,1024,1536]{2,1,0:T(8,128)(2,1)}, u32[]{:S(2)}) copy-start(bf16[1,1024,1536]{2,1,0:T(8,128)(2,1)} %param.11) | copy-start | bytes 9437188
  43.6 65.1 %collective-permute-start.3 = (bf16[1024,3584]{1,0:T(8,128)(2,1)}, bf16[1024,3584]{1,0:T(8,128)(2,1)}, u32[]{:S(2)}, u32[]{:S(2)}) collective-permute-start(bf16[1024,3584]{1,0:T(8,128)(2,1)} %get-tuple-element.57.refs_12_), channel_id=1, source_target_pairs={{0,1},{1,0},{2,3},{3,2},{4,5},{5,4},{6,7},{7,6},{8,9},{9,8},{10,11... | collective-permute-start | bytes 22020104 | tf_op jit(solution)/shard_map/ppermute | solution.py:493
  44.9 63.7 %collective-permute-start.2 = (bf16[1024,1536]{1,0:T(8,128)(2,1)}, bf16[1024,1536]{1,0:T(8,128)(2,1)}, u32[]{:S(2)}, u32[]{:S(2)}) collective-permute-start(bf16[1024,1536]{1,0:T(8,128)(2,1)} %fusion.4.a), channel_id=1, source_target_pairs={{0,1},{1,0},{2,3},{3,2},{4,5},{5,4},{6,7},{7,6},{8,9},{9,8},{10,11... | collective-permute-start | bytes 9437192 | tf_op jit(solution)/shard_map/ppermute | solution.py:493
  44.9 63.7 %collective-permute-start.1 = (bf16[1024,1536]{1,0:T(8,128)(2,1)}, bf16[1024,1536]{1,0:T(8,128)(2,1)}, u32[]{:S(2)}, u32[]{:S(2)}) collective-permute-start(bf16[1024,1536]{1,0:T(8,128)(2,1)} %bitcast.58), channel_id=1, source_target_pairs={{0,1},{1,0},{2,3},{3,2},{4,5},{5,4},{6,7},{7,6},{8,9},{9,8},{10,11... | collective-permute-start | bytes 9437192 | tf_op jit(solution)/shard_map/ppermute | solution.py:493
  61.9 1.7 copy-start.2
  64.1 1.7 copy-start.1
  64.1 44.5 %collective-permute-start = (bf16[1024,1536]{1,0:T(8,128)(2,1)S(1)}, bf16[1024,1536]{1,0:T(8,128)(2,1)}, u32[]{:S(2)}, u32[]{:S(2)}) collective-permute-start(bf16[1024,1536]{1,0:T(8,128)(2,1)S(1)} %fusion.6.a), channel_id=1, source_target_pairs={{0,1},{1,0},{2,3},{3,2},{4,5},{5,4},{6,7},{7,6},{8,9},{9,8},{10,11... | collective-permute-start | bytes 9437192 | tf_op jit(solution)/shard_map/ppermute | solution.py:493
  108.7 35.9 %copy-start.3 = (f32[2,28,1536]{2,0,1:T(2,128)S(1)}, f32[2,28,1536]{2,0,1:T(2,128)}, u32[]{:S(2)}) copy-start(f32[2,28,1536]{2,0,1:T(2,128)} %param.18) | copy-start | bytes 1032196
  108.7 36.8 %copy-start.4 = (f32[2,28,1536]{2,0,1:T(2,128)S(1)}, f32[2,28,1536]{2,0,1:T(2,128)}, u32[]{:S(2)}) copy-start(f32[2,28,1536]{2,0,1:T(2,128)} %param.21) | copy-start | bytes 1032196
  108.7 37.6 %copy-start.5 = (f32[2,12,3584]{2,0,1:T(2,128)S(1)}, f32[2,12,3584]{2,0,1:T(2,128)}, u32[]{:S(2)}) copy-start(f32[2,12,3584]{2,0,1:T(2,128)} %param.16) | copy-start | bytes 1032196
  108.7 38.4 %copy-start.6 = (f32[2,12,3584]{2,0,1:T(2,128)S(1)}, f32[2,12,3584]{2,0,1:T(2,128)}, u32[]{:S(2)}) copy-start(f32[2,12,3584]{2,0,1:T(2,128)} %param.17) | copy-start | bytes 1032196
  108.7 39.3 %copy-start.7 = (f32[2,12,3584]{2,0,1:T(2,128)S(1)}, f32[2,12,3584]{2,0,1:T(2,128)}, u32[]{:S(2)}) copy-start(f32[2,12,3584]{2,0,1:T(2,128)} %param.19) | copy-start | bytes 1032196
  108.7 40.1 %copy-start.8 = (f32[2,12,3584]{2,0,1:T(2,128)S(1)}, f32[2,12,3584]{2,0,1:T(2,128)}, u32[]{:S(2)}) copy-start(f32[2,12,3584]{2,0,1:T(2,128)} %param.20) | copy-start | bytes 1032196
  108.7 35.7 %collective-permute-start.4 = (bf16[1024,3584]{1,0:T(8,128)(2,1)}, bf16[1024,3584]{1,0:T(8,128)(2,1)}, u32[]{:S(2)}, u32[]{:S(2)}) collective-permute-start(bf16[1024,3584]{1,0:T(8,128)(2,1)} %get-tuple-element.66.d_gate.d), channel_id=1, source_target_pairs={{0,1},{1,0},{2,3},{3,2},{4,5},{5,4},{6,7},{7,6},{8,9},{9,8},{10,11... | collective-permute-start | bytes 22020104 | tf_op jit(solution)/shard_map/ppermute | solution.py:493
  108.8 35.6 %collective-permute-start.5 = (bf16[1024,3584]{1,0:T(8,128)(2,1)}, bf16[1024,3584]{1,0:T(8,128)(2,1)}, u32[]{:S(2)}, u32[]{:S(2)}) collective-permute-start(bf16[1024,3584]{1,0:T(8,128)(2,1)} %get-tuple-element.68.d_up.d), channel_id=1, source_target_pairs={{0,1},{1,0},{2,3},{3,2},{4,5},{5,4},{6,7},{7,6},{8,9},{9,8},{10,11... | collective-permute-start | bytes 22020104 | tf_op jit(solution)/shard_map/ppermute | solution.py:493
  144.4 39.9 %collective-permute-start.6 = (bf16[1024,3584]{1,0:T(8,128)(2,1)}, bf16[1024,3584]{1,0:T(8,128)(2,1)}, u32[]{:S(2)}, u32[]{:S(2)}) collective-permute-start(bf16[1024,3584]{1,0:T(8,128)(2,1)} %get-tuple-element.70.a), channel_id=1, source_target_pairs={{0,1},{1,0},{2,3},{3,2},{4,5},{5,4},{6,7},{7,6},{8,9},{9,8},{10,11... | collective-permute-start | bytes 22020104 | tf_op jit(solution)/shard_map/ppermute | solution.py:493
  149.7 51.1 %collective-permute-start.7 = (bf16[1024,1536]{1,0:T(8,128)(2,1)}, bf16[1024,1536]{1,0:T(8,128)(2,1)}, u32[]{:S(2)}, u32[]{:S(2)}) collective-permute-start(bf16[1024,1536]{1,0:T(8,128)(2,1)} %normed_back.1.refs_14_), channel_id=1, source_target_pairs={{0,1},{1,0},{2,3},{3,2},{4,5},{5,4},{6,7},{7,6},{8,9},{9,8},{10,11... | collective-permute-start | bytes 9437192 | tf_op jit(solution)/shard_map/ppermute | solution.py:493
  299.1 259.7 %all-gather.7.cloned.1.call-start = ((), (), s32[]{:S(2)}) async-start(), calls=%async_computation.1 | async-start | bytes 33288192 | tf_op jit(solution)/shard_map/all_gather | solution.py:489
  333.3 121.5 %copy-start.12 = (f32[12,3584]{1,0:T(8,128)S(1)}, f32[12,3584]{1,0:T(8,128)}, u32[]{:S(2)}) copy-start(f32[12,3584]{1,0:T(8,128)} %get-tuple-element.94) | copy-start | bytes 516100
  333.3 123.6 %copy-start.16 = (f32[28,1536]{1,0:T(8,128)S(1)}, f32[28,1536]{1,0:T(8,128)}, u32[]{:S(2)}) copy-start(f32[28,1536]{1,0:T(8,128)} %get-tuple-element.98) | copy-start | bytes 516100
  333.3 125.5 %copy-start.15 = (f32[28,1536]{1,0:T(8,128)S(1)}, f32[28,1536]{1,0:T(8,128)}, u32[]{:S(2)}) copy-start(f32[28,1536]{1,0:T(8,128)} %get-tuple-element.104) | copy-start | bytes 516100
  333.3 127.5 %copy-start.11 = (f32[12,3584]{1,0:T(8,128)S(1)}, f32[12,3584]{1,0:T(8,128)}, u32[]{:S(2)}) copy-start(f32[12,3584]{1,0:T(8,128)} %get-tuple-element.96) | copy-start | bytes 516100
  454.7 8.1 %copy-start.10 = (f32[12,3584]{1,0:T(8,128)S(1)}, f32[12,3584]{1,0:T(8,128)}, u32[]{:S(2)}) copy-start(f32[12,3584]{1,0:T(8,128)} %get-tuple-element.100) | copy-start | bytes 516100
  454.7 8.1 %copy-start.14 = (f32[12,3584]{1,0:T(8,128)S(1)}, f32[12,3584]{1,0:T(8,128)}, u32[]{:S(2)}) copy-start(f32[12,3584]{1,0:T(8,128)} %get-tuple-element.99) | copy-start | bytes 516100
  454.7 9.1 %copy-start.9 = (f32[12,3584]{1,0:T(8,128)S(1)}, f32[12,3584]{1,0:T(8,128)}, u32[]{:S(2)}) copy-start(f32[12,3584]{1,0:T(8,128)} %get-tuple-element.102) | copy-start | bytes 516100
  454.7 9.1 %copy-start.13 = (f32[12,3584]{1,0:T(8,128)S(1)}, f32[12,3584]{1,0:T(8,128)}, u32[]{:S(2)}) copy-start(f32[12,3584]{1,0:T(8,128)} %get-tuple-element.101) | copy-start | bytes 516100
Sparse Core Ops, SparseCore 0:
  299.2 146.7 all-gather.4
  454.9 103.8 all-gather.6
